TPU v7x, 1024 devices: a whole 8x8x8 slice. The times are simulated.
1024 devices in a mesh: fsdp: 16 (over y_lo, x), tp: 8 (over y_hi, core), rep: 8 (over z).
Axes of the slice: x: 8, y: 8 (y_hi: 4, y_lo: 2; y = y_hi * 2 + y_lo), z: 8, core: 2. Of those that a mesh axis runs over, the one named last changes fastest.
Arguments:
- tokens: bfloat16 [16384, 5120], P('fsdp', 'rep'), may hold values from -6 to 6
- ref_qkv: bfloat16 [5120, 7168], P(('rep', 'fsdp'), 'tp'), may hold values from -0.078125 to 0.078125
- ref_bias: float32 [7168], P('tp'), may hold values from -9 to 9
- segment_ids: int32 [16, 1024], P('fsdp'), may hold values from 0 to 7, never falling along the last dimension, each value on 1 to 512 neighbouring positions
- policy_key: bfloat16 [5120, 1024], P(('rep', 'fsdp'), 'tp'), may hold values from -0.078125 to 0.078125
Outputs:
- context: bfloat16 [16384, 5120], P(('fsdp', 'rep'), 'tp')
- policy_key_tp: bfloat16 [5120, 1024], P(None, 'tp')
All inputs are finite; a program needn't handle non-finite values.
Results may differ from a plain program's by a relative error of at most 0.0093.
Values may be sent and summed in bfloat16 or wider, within the bound.
No kernel may reach another device: no remote copies, remote signals or barrier semaphores. Data moves between devices by JAX's collectives and lax.ppermute only.
A program may use at most 32 MiB of HBM per device.

v0:
```python
import jax
import jax.numpy as jnp
from jax import lax
from jax.sharding import PartitionSpec as P

QH = 40
KVH = 8
HD = 128


def laid_out(parts, dim):
    lengths = list(parts.shape[1:])
    lengths[dim] *= parts.shape[0]
    return jnp.moveaxis(parts, 0, dim).reshape(lengths)


def copy_for_each(array, axis):
    copies = jnp.broadcast_to(array, (lax.axis_size(axis), *array.shape))
    return lax.all_to_all(copies, axis, split_axis=0, concat_axis=0, tiled=True)


def collect(array, axis, dim):
    return laid_out(copy_for_each(array, axis), dim)


def sent_together(arrays, axis, dim, along):
    ends, at = ([], 0)
    for a in arrays[:-1]:
        at += a.shape[along]
        ends.append(at)
    both = jnp.concatenate(arrays, axis=along)
    return tuple(jnp.split(lax.all_gather(both, axis, axis=dim, tiled=True), ends, axis=along))


def positions_of(seg):
    count = seg.shape[0]
    index = jnp.arange(count, dtype=jnp.int32)
    starts = jnp.concatenate([jnp.ones((1,), bool), seg[1:] != seg[:-1]])
    first = lax.cummax(jnp.where(starts, index, 0), axis=0)
    return index - first


def rotary(values, pos):
    half = values.shape[-1] // 2
    freq = 1000000.0 ** (-2.0 * jnp.arange(half, dtype=jnp.float32) / values.shape[-1])
    angle = pos.astype(jnp.float32)[:, None] * freq[None, :]
    shape = (values.shape[0],) + (1,) * (values.ndim - 2) + (half,)
    cosine = jnp.cos(angle).reshape(shape)
    sine = jnp.sin(angle).reshape(shape)
    first = values[..., :half]
    second = values[..., half:]
    return jnp.concatenate(
        [first * cosine - second * sine, second * cosine + first * sine], axis=-1
    )


def per_device(tokens, ref_qkv, ref_bias, segment_ids, policy_key):
    share = QH // KVH
    rows = tokens.shape[0]
    columns = ref_qkv.shape[1]
    groups = columns // ((share + 2) * HD)
    replicas = lax.axis_size("rep")
    mine = rows // replicas
    rank = lax.axis_index("rep")
    partial_value = jnp.dot(tokens, collect(ref_qkv, "fsdp", 0), preferred_element_type=jnp.float32)
    partial_value = partial_value.reshape(rows, groups, share + 2, HD)
    bias = ref_bias.reshape(groups, share + 2, HD)
    seg = segment_ids[0]
    pos = positions_of(seg)
    start = rank * mine
    my_pos = lax.dynamic_slice_in_dim(pos, start, mine, 0)
    summed = lax.psum_scatter(partial_value, "rep", scatter_dimension=0, tiled=True) + bias[None]
    query = rotary(summed[:, :, :share], my_pos).astype(jnp.bfloat16)
    my_keys = rotary(summed[:, :, share], my_pos).astype(jnp.bfloat16)
    my_vals = summed[:, :, share + 1].astype(jnp.bfloat16)
    keys, vals = sent_together((my_keys, my_vals), "rep", 0, 1)
    scores = jnp.einsum(
        "qhgd,khd->hgqk", query, keys, preferred_element_type=jnp.float32
    ) / jnp.sqrt(jnp.float32(HD))
    query_index = start + jnp.arange(mine, dtype=jnp.int32)
    key_index = jnp.arange(rows, dtype=jnp.int32)
    my_seg = lax.dynamic_slice_in_dim(seg, start, mine, 0)
    allowed = (my_seg[:, None] == seg[None, :]) & (key_index[None, :] <= query_index[:, None])
    scores = jnp.where(allowed[None, None], scores, -1e30)
    top = jnp.max(scores, axis=-1, keepdims=True)
    expo = jnp.exp(scores - top)
    weights = (expo / jnp.sum(expo, axis=-1, keepdims=True)).astype(jnp.bfloat16)
    context = jnp.einsum("hgqk,khd->qhgd", weights, vals, preferred_element_type=jnp.float32)
    context = context.astype(jnp.bfloat16).reshape(mine, groups * share * HD)
    inner = collect(policy_key, "rep", 0)
    outer = lax.all_gather(inner, "fsdp", axis=0, tiled=True)
    blocks = policy_key.shape[0]
    shards = outer.shape[0] // (blocks * replicas)
    whole = (
        outer.reshape(shards, replicas, blocks, outer.shape[1])
        .transpose(1, 0, 2, 3)
        .reshape(outer.shape)
    )
    return (context, whole)


def solution(mesh):
    in_specs = (
        P("fsdp", "rep"),
        P(("rep", "fsdp"), "tp"),
        P("tp"),
        P("fsdp", None),
        P(("rep", "fsdp"), "tp"),
    )
    out_specs = (P(("fsdp", "rep"), "tp"), P(None, "tp"))
    return jax.shard_map(
        per_device, mesh=mesh, in_specs=in_specs, out_specs=out_specs, check_vma=False
    )
```

profile of v0, /device:TPU:4, one launch (start us, length us, event | category | flops | bytes accessed | tf_op | source)
XLA Modules:
  0.0 166.1 jit_solution(12220243201968932724)
XLA Ops:
  8.0 0.0 copy-start
  8.0 0.8 broadcast_in_dim.36
  8.8 25.1 %all_to_all.10 = bf16[8,40,128]{2,1,0:T(8,128)(2,1)} all-to-all(bf16[8,40,128]{2,1,0:T(8,128)(2,1)S(1)} %broadcast_in_dim.36), channel_id=1, replica_groups=mesh['fsdp'=16,'tp'=8,'rep'=8] {'rep'}, dimensions={0} | all-to-all | bytes 163840 | tf_op jit(solution)/shard_map/all_to_all | solution.py:19
  34.0 2.0 %broadcast_in_dim.20 = bf16[16,40,896]{2,1,0:T(8,128)(2,1)} broadcast(bf16[40,896]{1,0:T(8,128)(2,1)} %param.6), dimensions={1,2} | broadcast | bytes 1218560 | tf_op jit(solution)/shard_map/broadcast_in_dim | solution.py:18
  35.9 8.4 %all-to-all-start = ((bf16[16,40,896]{2,1,0:T(8,128)(2,1)}), bf16[16,40,896]{2,1,0:T(8,128)(2,1)S(1)}, u32[]{:S(2)}, u32[]{:S(2)}) async-start(bf16[16,40,896]{2,1,0:T(8,128)(2,1)} %broadcast_in_dim.20), calls=%async_computation | async-start | bytes 2293760 | tf_op jit(solution)/shard_map/all_to_all | solution.py:19
  44.3 0.0 all-gather.2.cloned.1.call-start
  44.4 0.7 all-gather.2.cloned.1.call-update
  45.1 0.0 reduce-scatter.2.cloned.1.call-start
  45.1 27.0 %all-to-all-done = bf16[16,40,896]{2,1,0:T(8,128)(2,1)S(1)} async-done(((bf16[16,40,896]{2,1,0:T(8,128)(2,1)}), bf16[16,40,896]{2,1,0:T(8,128)(2,1)S(1)}, u32[]{:S(2)}, u32[]{:S(2)}) %all-to-all-start) | async-done | bytes 1146912 | tf_op jit(solution)/shard_map/all_to_all | solution.py:19
  72.1 1.4 copy.20
  73.6 0.0 copy-done
  73.6 4.7 %convolution_bitcast_fusion = f32[1024,1,7,128]{0,3,2,1:T(8,128)} fusion(bf16[7,128,640]{2,1,0:T(8,128)(2,1)} %bitcast.72, bf16[1024,640]{1,0:T(8,128)(2,1)S(1)} %copy-done), kind=kOutput, calls=%fused_computation.4 | convolution fusion | flops 1174405120 | bytes 6127616 | tf_op jit(solution)/shard_map/dot_general | solution.py:65
  78.3 0.0 copy-start.1
  78.3 0.0 copy-start.2
  78.3 0.0 reduce-scatter.2.cloned.1.call-update
  78.3 0.7 copy-done.1
  78.9 0.1 compare_reduce_fusion
  79.0 0.1 add_select_fusion
  79.1 0.3 reduce-window.9
  79.4 0.1 slice.41
  79.5 0.1 slice_reduce_fusion
  79.7 0.1 bitcast_subtract_fusion
  79.7 0.1 dynamic-slice_convert_fusion
  79.8 0.2 multiply_cosine_fusion
  80.0 0.2 fusion.8
  80.2 37.1 %all-gather.2.cloned.1.call-done = bf16[5120,128]{1,0:T(8,128)(2,1)} async-done(((bf16[320,128]{1,0:T(8,128)(2,1)}), bf16[5120,128]{1,0:T(8,128)(2,1)}) %all-gather.2.cloned.1.call-update) | async-done | bytes 1310736 | tf_op jit(solution)/shard_map/all_gather | solution.py:91
  117.3 2.5 %copy.25 = bf16[8,16,40,128]{3,2,1,0:T(8,128)(2,1)} copy(bf16[8,16,40,128]{3,2,0,1:T(8,128)(2,1)} %bitcast.70) | data formatting | bytes 2621440 | tf_op jit(solution)/shard_map/transpose | solution.py:96
  119.9 11.1 %reduce-scatter.2.cloned.1.call-done = f32[128,1,7,128]{0,3,2,1:T(8,128)} async-done(((f32[1024,1,7,128]{0,3,2,1:T(8,128)}), f32[128,1,7,128]{0,3,2,1:T(8,128)}) %reduce-scatter.2.cloned.1.call-update) | async-done | bytes 458768 | tf_op jit(solution)/shard_map/reduce_scatter | solution.py:72
  130.9 0.0 copy-done.2
  130.9 1.2 broadcast_add_fusion
  132.2 0.2 fusion.20
  132.4 23.3 %all_gather.6 = bf16[1024,2,128]{0,2,1:T(8,128)(2,1)S(1)} all-gather(bf16[128,2,128]{0,2,1:T(8,128)(2,1)S(1)} %pad_maximum_fusion), channel_id=1, replica_groups=mesh['fsdp'=16,'tp'=8,'rep'=8] {'rep'}, dimensions={0}, use_global_device_ids=true | all-gather | bytes 589824 | tf_op jit(solution)/shard_map/all_gather | solution.py:32
  155.8 0.6 fusion.1
  156.4 0.6 fusion
  156.9 0.9 fusion.5
  157.8 0.8 copy.26
  (8 shorter events, 0.1 us)
Async XLA Ops:
  8.0 65.6 %copy-start = (bf16[1024,640]{1,0:T(8,128)(2,1)S(1)}, bf16[1024,640]{1,0:T(8,128)(2,1)}, u32[]{:S(2)}) copy-start(bf16[1024,640]{1,0:T(8,128)(2,1)} %param.5) | copy-start | bytes 3932164
  35.9 36.2 %all-to-all-start = ((bf16[16,40,896]{2,1,0:T(8,128)(2,1)}), bf16[16,40,896]{2,1,0:T(8,128)(2,1)S(1)}, u32[]{:S(2)}, u32[]{:S(2)}) async-start(bf16[16,40,896]{2,1,0:T(8,128)(2,1)} %broadcast_in_dim.20), calls=%async_computation | async-start | bytes 2293760 | tf_op jit(solution)/shard_map/all_to_all | solution.py:19
  44.3 73.0 %all-gather.2.cloned.1.call-start = ((), (), s32[]{:S(2)}) async-start(), calls=%async_computation.4 | async-start | bytes 1392640 | tf_op jit(solution)/shard_map/all_gather | solution.py:91
  45.1 85.8 %reduce-scatter.2.cloned.1.call-start = ((), (), s32[]{:S(2)}) async-start(), calls=%async_computation.3 | async-start | bytes 4128768 | tf_op jit(solution)/shard_map/reduce_scatter | solution.py:72
  78.3 0.7 copy-start.1
  78.3 52.7 %copy-start.2 = (f32[896]{0:T(1024)S(1)}, f32[896]{0:T(1024)}, u32[]{:S(2)}) copy-start(f32[896]{0:T(1024)} %param.7) | copy-start | bytes 10756
Sparse Core Ops, SparseCore 0:
  47.8 69.4 all-gather.1
Sparse Core Ops, SparseCore 1:
  78.4 52.5 reduce-scatter.1
where the time goes:
time: 167 us; the launch traced here: 166 us
  waiting for transfers between devices  75.9 us (45%)
  blocking collectives  48.5 us (29%)
  between operations  15.6 us (9%)
  starting transfers between devices  8.48 us (5%)
  local copies, waits for them, and re-layouts  8.43 us (5%)
  matrix products  6.14 us (4%)
  other arithmetic  3.07 us (2%)
    all_gather x1, waiting for transfers between devices, per_device(): outer = lax.all_gather(inner, 'fsdp', axis=0, tiled=True)  37.1 us
    all_to_all x1, waiting for transfers between devices, copy_for_each(): return lax.all_to_all(copies, axis, split_axis=0, concat_axis=0, tiled=True)  27 us
    all_to_all x1, blocking collectives, copy_for_each(): return lax.all_to_all(copies, axis, split_axis=0, concat_axis=0, tiled=True)  25.1 us
    all_gather x1, blocking collectives, sent_together(): lax.all_gather(both, axis, axis=dim, tiled=True)  23.3 us
    reduce_scatter x1, waiting for transfers between devices, per_device(): lax.psum_scatter(partial_value, 'rep', scatter_dimension=0, tiled=True)  11.1 us
    all_to_all x1, starting transfers between devices, copy_for_each(): return lax.all_to_all(copies, axis, split_axis=0, concat_axis=0, tiled=True)  8.4 us
    dot_general x1, matrix products, per_device(): jnp.dot(tokens, collect(ref_qkv, 'fsdp', 0), preferred_element_type=jnp.f...  4.68 us
  transfers between devices with their start and end apart: 3, of which 3 were waited for; matrix products, arithmetic and copies ran while one was open for 6% of the time, Pallas kernels for 0%

commit v1 on v0

v1 whole, which is shorter than its diff:
```python
import jax
import jax.numpy as jnp
from jax import lax
from jax.experimental import pallas as pl
from jax.experimental.pallas import tpu as pltpu
from jax.sharding import PartitionSpec as P

QH = 40
KVH = 8
HD = 128
HALF = HD // 2
SHARE = QH // KVH
WINDOW = 5


def copies_of(array, count):
    return jnp.broadcast_to(array, (count, *array.shape))


def exchanged(blocks, axis):
    return lax.all_to_all(blocks, axis, split_axis=0, concat_axis=0, tiled=True)


def cost(flops, moved):
    return pl.CostEstimate(flops=flops, bytes_accessed=moved, transcendentals=0)


def call(kernel, outs, flops, *args, scalars=0):
    vmem = pl.BlockSpec(memory_space=pltpu.VMEM)
    smem = pl.BlockSpec(memory_space=pltpu.SMEM)
    moved = sum(a.size * a.dtype.itemsize for a in (*args, *outs))
    return pl.pallas_call(
        kernel,
        out_shape=outs if len(outs) > 1 else outs[0],
        in_specs=[smem] * scalars + [vmem] * (len(args) - scalars),
        out_specs=tuple(vmem for _ in outs) if len(outs) > 1 else vmem,
        compiler_params=pltpu.CompilerParams(vmem_limit_bytes=24 * 1024 * 1024),
        cost_estimate=cost(flops, moved),
    )(*args)


def lanes_below_half(shape):
    return lax.broadcasted_iota(jnp.int32, shape, len(shape) - 1) < HALF


def project(own_ref, other_ref, w_ref, kv_ref, q_ref):
    blocks = kv_ref.shape[0]
    rows = own_ref.shape[0]
    step = rows // 2
    shared = w_ref[:, 3 * HD : 4 * HD]
    w_own = w_ref[:, : 4 * HD]
    swapped = pltpu.roll(shared.astype(jnp.float32), HALF, 1).astype(jnp.bfloat16)
    w_other = jnp.concatenate([w_ref[:, 4 * HD :], swapped], axis=1)
    size = rows // blocks
    low = lanes_below_half((size // 2, HD))
    for part in range(2):
        at = part * step
        own = own_ref[at : at + step, :]
        other = other_ref[at : at + step, :]
        value = jnp.dot(own, w_own, preferred_element_type=jnp.float32)
        value = value + jnp.dot(other, w_other, preferred_element_type=jnp.float32)
        for b in range(step // size):
            j = at // size + b
            piece = value[b * size : (b + 1) * size]
            kv_ref[j] = piece[:, :HD].astype(jnp.bfloat16)
            q_ref[j, :size] = piece[:, HD : 2 * HD].astype(jnp.bfloat16)
            q_ref[j, size : 2 * size] = piece[:, 2 * HD : 3 * HD].astype(jnp.bfloat16)
            last = piece[:, 3 * HD :]
            packed = jnp.where(low, last[: size // 2], pltpu.roll(last[size // 2 :], HALF, 1))
            q_ref[j, 2 * size :] = packed.astype(jnp.bfloat16)


def turned(value, cosine, sine):
    return value * cosine + pltpu.roll(value, HALF, 1) * sine


def added(ref, parity, rows):
    value = ref[parity, rows].astype(jnp.float32)
    for j in range(parity + 2, ref.shape[0], 2):
        value = value + ref[j, rows].astype(jnp.float32)
    return value


def keys_and_values(part_ref, bias_ref, cos_ref, sin_ref, out_ref):
    size = part_ref.shape[1]
    every = slice(0, size)
    key = added(part_ref, 0, every) + bias_ref[SHARE : SHARE + 1]
    key = turned(key, cos_ref[...], sin_ref[...]).astype(jnp.bfloat16)
    val = (added(part_ref, 1, every) + bias_ref[SHARE + 1 : SHARE + 2]).astype(jnp.bfloat16)
    for j in range(out_ref.shape[0]):
        out_ref[j, :size] = key
        out_ref[j, size:] = val


def attend(rank_ref, part_ref, kv_ref, bias_ref, cos_ref, sin_ref, seg_ref, mine_ref, out_ref):
    size = out_ref.shape[0]
    blocks = kv_ref.shape[0]
    window = min(WINDOW, blocks)
    rank = rank_ref[0]
    first = jnp.clip(rank - (window - 1), 0, blocks - window)
    low = lanes_below_half((size // 2, HD))
    left = added(part_ref, 0, slice(2 * size, 5 * size // 2))
    right = added(part_ref, 1, slice(2 * size, 5 * size // 2))
    middle = jnp.concatenate(
        [
            jnp.where(low, left, pltpu.roll(right, HALF, 1)),
            jnp.where(low, pltpu.roll(left, HALF, 1), right),
        ],
        axis=0,
    )
    heads = [
        added(part_ref, 0, slice(0, size)),
        added(part_ref, 0, slice(size, 2 * size)),
        middle,
        added(part_ref, 1, slice(0, size)),
        added(part_ref, 1, slice(size, 2 * size)),
    ]
    span = kv_ref[pl.ds(first, window)]
    keys = span[:, :size].reshape(window * size, HD)
    vals = span[:, size:].reshape(window * size, HD)
    row = rank * size + lax.broadcasted_iota(jnp.int32, (size, size), 0)
    lane = lax.broadcasted_iota(jnp.int32, (size, size), 1)
    masks = []
    for b in range(window):
        seg = seg_ref[pl.ds(first + b, 1), :]
        column = (first + b) * size + lane
        masks.append((mine_ref[...] == seg) & (column <= row))
    allowed = jnp.concatenate(masks, axis=1)
    cosine, sine = cos_ref[...], sin_ref[...]
    for h in range(SHARE):
        query = turned(heads[h] + bias_ref[h : h + 1], cosine, sine).astype(jnp.bfloat16)
        scores = lax.dot_general(
            query, keys, (((1,), (1,)), ((), ())), preferred_element_type=jnp.float32
        )
        scores = jnp.where(allowed, scores / jnp.sqrt(jnp.float32(HD)), -1e30)
        top = jnp.max(scores, axis=-1, keepdims=True)
        expo = jnp.exp(scores - top)
        weights = (expo / jnp.sum(expo, axis=-1, keepdims=True)).astype(jnp.bfloat16)
        context = jnp.dot(weights, vals, preferred_element_type=jnp.float32)
        out_ref[:, h * HD : (h + 1) * HD] = context.astype(jnp.bfloat16)


def per_device(tokens, ref_qkv, ref_bias, segment_ids, policy_key):
    replicas = lax.axis_size("rep")
    shards = lax.axis_size("fsdp")
    rows, features = tokens.shape
    mine = rows // replicas
    rank = lax.axis_index("rep")
    odd = (rank & 1) == 1
    swap = [(i, i ^ 1) for i in range(replicas)]
    bf16, f32 = jnp.bfloat16, jnp.float32

    w = ref_qkv
    kv = (w[:, 5 * HD : 6 * HD], w[:, 6 * HD :])
    wide = (w[:, : 2 * HD], w[:, 3 * HD : 5 * HD])
    thin = (w[:, 2 * HD : 2 * HD + HALF], w[:, 2 * HD + HALF : 3 * HD])
    keep = jnp.where(
        odd,
        jnp.concatenate([kv[1], wide[1], thin[1]], axis=1),
        jnp.concatenate([kv[0], wide[0], thin[0]], axis=1),
    )
    give = jnp.where(
        odd,
        jnp.concatenate([thin[0], kv[0], wide[0]], axis=1),
        jnp.concatenate([thin[1], kv[1], wide[1]], axis=1),
    )
    with jax.named_scope("w_swap"):
        got = lax.ppermute(give, "rep", swap)
    with jax.named_scope("t_swap"):
        other = lax.ppermute(tokens, "rep", swap)
    mixed = jnp.concatenate([keep, got], axis=1)
    with jax.named_scope("w_gather"):
        weights = exchanged(copies_of(mixed, shards), "fsdp").reshape(features, -1)

    with jax.named_scope("pol_rep"):
        inner = exchanged(copies_of(policy_key, replicas), "rep")
    blocks, width = policy_key.shape
    with jax.named_scope("pol_fsdp"):
        outer = exchanged(copies_of(inner.reshape(replicas * blocks, width), shards), "fsdp")
    whole = (
        outer.reshape(shards, replicas, blocks, width)
        .transpose(1, 0, 2, 3)
        .reshape(shards * replicas * blocks, width)
    )

    seg = segment_ids[0]
    start = rank * mine
    my_seg = lax.dynamic_slice_in_dim(seg, start, mine, 0)
    before = jnp.sum((seg[None, :] < my_seg[:, None]).astype(jnp.int32), axis=1)
    pos = start + jnp.arange(mine, dtype=jnp.int32) - before
    freq = 1000000.0 ** (-2.0 * jnp.arange(HALF, dtype=f32) / HD)
    angle = pos.astype(f32)[:, None] * freq[None, :]
    cosine, sine = jnp.cos(angle), jnp.sin(angle)
    cosine = jnp.concatenate([cosine, cosine], axis=1)
    sine = jnp.concatenate([-sine, sine], axis=1)
    bias = ref_bias.reshape(SHARE + 2, HD)

    part_kv, part_q = call(
        project,
        (
            jax.ShapeDtypeStruct((replicas, mine, HD), bf16),
            jax.ShapeDtypeStruct((replicas, 5 * mine // 2, HD), bf16),
        ),
        4 * rows * features * 4 * HD,
        tokens,
        other,
        weights,
    )
    with jax.named_scope("kv_sum"):
        part_kv = exchanged(part_kv, "rep")
    with jax.named_scope("q_sum"):
        part_q = exchanged(part_q, "rep")
    my_kv = call(
        keys_and_values,
        (jax.ShapeDtypeStruct((replicas, 2 * mine, HD), bf16),),
        16 * mine * HD,
        part_kv,
        bias,
        cosine,
        sine,
    )
    with jax.named_scope("kv_gather"):
        all_kv = exchanged(my_kv, "rep")
    context = call(
        attend,
        (jax.ShapeDtypeStruct((mine, SHARE * HD), bf16),),
        4 * SHARE * mine * WINDOW * mine * HD,
        rank.reshape(1),
        part_q,
        all_kv,
        bias,
        cosine,
        sine,
        seg.reshape(replicas, mine),
        my_seg[:, None],
        scalars=1,
    )
    return (context, whole)


def solution(mesh):
    in_specs = (
        P("fsdp", "rep"),
        P(("rep", "fsdp"), "tp"),
        P("tp"),
        P("fsdp", None),
        P(("rep", "fsdp"), "tp"),
    )
    out_specs = (P(("fsdp", "rep"), "tp"), P(None, "tp"))
    return jax.shard_map(
        per_device, mesh=mesh, in_specs=in_specs, out_specs=out_specs, check_vma=False
    )
```

time: 167 us -> 162 us (0.970)
  the two profiles are of different devices: /device:TPU:4 before, /device:TPU:34 now
where the time goes in v1:
time: 162 us; the launch traced here: 161 us
  waiting for transfers between devices  60.8 us (38%)
  blocking collectives  49.5 us (31%)
  starting transfers between devices  34.5 us (21%)
  local copies, waits for them, and re-layouts  8.46 us (5%)
  Pallas kernels  6.61 us (4%)
    all_to_all x2, blocking collectives, exchanged(): return lax.all_to_all(blocks, axis, split_axis=0, concat_axis=0, tiled=True)  49.5 us
    all_to_all x4, waiting for transfers between devices, exchanged(): return lax.all_to_all(blocks, axis, split_axis=0, concat_axis=0, tiled=True)  33.5 us
    ppermute x1, waiting for transfers between devices, per_device(): other = lax.ppermute(tokens, 'rep', swap)  27.3 us
    all_to_all x4, starting transfers between devices, exchanged(): return lax.all_to_all(blocks, axis, split_axis=0, concat_axis=0, tiled=True)  26.9 us
    pallas_call x3, Pallas kernels, call(): pl.pallas_call(kernel, out_shape=outs if len(outs) > 1 else outs[0], in_s...  6.61 us
    ppermute x1, starting transfers between devices, per_device(): got = lax.ppermute(give, 'rep', swap)  5.19 us
  transfers between devices with their start and end apart: 6, of which 4 were waited for; matrix products, arithmetic and copies ran while one was open for 3% of the time, Pallas kernels for 2%

profile of v1, /device:TPU:34, one launch (start us, length us, event | category | flops | bytes accessed | tf_op | source)
XLA Modules:
  0.0 161.4 jit_solution(5444845083216985890)
XLA Ops:
  0.6 0.8 fusion.5
  1.4 0.9 fusion.3
  2.2 0.7 fusion.4
  3.0 0.8 slice.25
  3.7 0.1 maximum_select_fusion
  3.8 5.2 %collective-permute-start.1 = (bf16[40,448]{1,0:T(8,128)(2,1)S(1)}, bf16[40,448]{1,0:T(8,128)(2,1)S(1)}, u32[]{:S(2)}, u32[]{:S(2)}) collective-permute-start(bf16[40,448]{1,0:T(8,128)(2,1)S(1)} %get-tuple-element.13), channel_id=1, source_target_pairs={{0,1},{1,0},{2,3},{3,2},{4,5},{5,4},{6,7},{7,6},{8,9},{9,8},{10,11... | collective-permute-start | bytes 107528 | tf_op jit(solution)/shard_map/w_swap/ppermute | solution.py:168
  9.0 1.4 broadcast_in_dim.17
  10.4 14.9 %all-to-all-start.4 = ((bf16[8,40,128]{2,1,0:T(8,128)(2,1)}), bf16[8,40,128]{2,1,0:T(8,128)(2,1)S(1)}, u32[]{:S(2)}, u32[]{:S(2)}) async-start(bf16[8,40,128]{2,1,0:T(8,128)(2,1)} %broadcast_in_dim.17), calls=%async_computation.4 | async-start | bytes 163840 | tf_op jit(solution)/shard_map/pol_rep/all_to_all | solution.py:21
  25.2 0.0 collective-permute-done.1
  25.2 0.1 pad_maximum_fusion
  25.3 8.5 %all-to-all-done.4 = bf16[8,40,128]{2,1,0:T(8,128)(2,1)S(1)} async-done(((bf16[8,40,128]{2,1,0:T(8,128)(2,1)}), bf16[8,40,128]{2,1,0:T(8,128)(2,1)S(1)}, u32[]{:S(2)}, u32[]{:S(2)}) %all-to-all-start.4) | async-done | bytes 81952 | tf_op jit(solution)/shard_map/pol_rep/all_to_all | solution.py:21
  33.8 0.1 broadcast_in_dim.15
  33.9 36.5 %all_to_all.30 = bf16[16,40,896]{2,1,0:T(8,128)(2,1)S(1)} all-to-all(bf16[16,40,896]{2,1,0:T(8,128)(2,1)S(1)} %broadcast_in_dim.15), channel_id=1, replica_groups=mesh['fsdp'=16,'tp'=8,'rep'=8] {'fsdp'}, dimensions={0} | all-to-all | bytes 2293760 | tf_op jit(solution)/shard_map/w_gather/all_to_all | solution.py:21
  70.4 1.3 broadcast_in_dim.18
  71.7 0.0 copy-start.2
  71.7 5.0 %all-to-all-start.5 = ((bf16[16,320,128]{2,1,0:T(8,128)(2,1)}), bf16[16,320,128]{2,1,0:T(8,128)(2,1)}, u32[]{:S(2)}, u32[]{:S(2)}) async-start(bf16[16,320,128]{2,1,0:T(8,128)(2,1)} %broadcast_in_dim.18), calls=%async_computation.5 | async-start | bytes 2621440 | tf_op jit(solution)/shard_map/pol_fsdp/all_to_all | solution.py:21
  76.6 0.0 copy-done.2
  76.6 2.5 %collective-permute-start = (bf16[1024,640]{1,0:T(8,128)(2,1)S(1)}, bf16[1024,640]{1,0:T(8,128)(2,1)S(1)}, u32[]{:S(2)}, u32[]{:S(2)}) collective-permute-start(bf16[1024,640]{1,0:T(8,128)(2,1)S(1)} %copy-done.2), channel_id=1, source_target_pairs={{0,1},{1,0},{2,3},{3,2},{4,5},{5,4},{6,7},{7,6},{8,9},{9,8},{10,11... | collective-permute-start | bytes 3932168 | tf_op jit(solution)/shard_map/t_swap/ppermute | solution.py:170
  79.1 27.3 %collective-permute-done.other_ref = bf16[1024,640]{1,0:T(8,128)(2,1)S(1)} collective-permute-done((bf16[1024,640]{1,0:T(8,128)(2,1)S(1)}, bf16[1024,640]{1,0:T(8,128)(2,1)S(1)}, u32[]{:S(2)}, u32[]{:S(2)}) %collective-permute-start) | collective-permute-done | bytes 1310752 | tf_op jit(solution)/shard_map/t_swap/ppermute | solution.py:170
  106.4 2.8 %shard_map.68 = (bf16[8,128,128]{2,1,0:T(8,128)(2,1)S(1)}, bf16[8,320,128]{2,1,0:T(8,128)(2,1)}) custom-call(bf16[1024,640]{1,0:T(8,128)(2,1)S(1)} %copy-done.2, bf16[1024,640]{1,0:T(8,128)(2,1)S(1)} %collective-permute-done.other_ref, bf16[640,896]{1,0:T(8,128)(2,1)S(1)} %bitcast.14), custom_call_target="tpu_custom_call" | custom-call | flops 1342177280 | bytes 4685824 | tf_op jit(solution)/shard_map/pallas_call | solution.py:32
  109.2 0.0 copy-start
  109.2 0.0 copy-start.1
  109.2 0.0 all-to-all-done.5
  109.2 13.0 %all_to_all.31.part_ref = bf16[8,128,128]{2,1,0:T(8,128)(2,1)S(1)} all-to-all(bf16[8,128,128]{2,1,0:T(8,128)(2,1)S(1)} %get-tuple-element.5), channel_id=1, replica_groups=mesh['fsdp'=16,'tp'=8,'rep'=8] {'rep'}, dimensions={0} | all-to-all | bytes 524288 | tf_op jit(solution)/shard_map/kv_sum/all_to_all | solution.py:21
  122.2 3.5 %all-to-all-start.1 = ((bf16[8,320,128]{2,1,0:T(8,128)(2,1)}), bf16[8,320,128]{2,1,0:T(8,128)(2,1)S(1)}, u32[]{:S(2)}, u32[]{:S(2)}) async-start(bf16[8,320,128]{2,1,0:T(8,128)(2,1)} %get-tuple-element.4), calls=%async_computation.1 | async-start | bytes 1310720 | tf_op jit(solution)/shard_map/q_sum/all_to_all | solution.py:21
  125.8 0.0 copy-done
  125.8 0.2 convert_reduce_fusion
  126.0 0.3 fusion
  126.3 0.1 pad_maximum_fusion.1
  126.4 0.0 copy-done.1
  126.4 0.9 shard_map.69
  127.3 14.4 %all-to-all-done.1.part_ref = bf16[8,320,128]{2,1,0:T(8,128)(2,1)S(1)} async-done(((bf16[8,320,128]{2,1,0:T(8,128)(2,1)}), bf16[8,320,128]{2,1,0:T(8,128)(2,1)S(1)}, u32[]{:S(2)}, u32[]{:S(2)}) %all-to-all-start.1) | async-done | bytes 655392 | tf_op jit(solution)/shard_map/q_sum/all_to_all | solution.py:21
  141.8 3.5 %all-to-all-start.3 = ((bf16[8,256,128]{2,1,0:T(8,128)(2,1)}), bf16[8,256,128]{2,1,0:T(8,128)(2,1)S(1)}, u32[]{:S(2)}, u32[]{:S(2)}) async-start(bf16[8,256,128]{2,1,0:T(8,128)(2,1)} %shard_map.69), calls=%async_computation.3 | async-start | bytes 1048576 | tf_op jit(solution)/shard_map/kv_gather/all_to_all | solution.py:21
  145.3 0.1 copy.11.mine_ref
  145.4 2.5 %copy.12 = bf16[8,16,40,128]{3,2,1,0:T(8,128)(2,1)} copy(bf16[8,16,40,128]{3,2,0,1:T(8,128)(2,1)} %bitcast.9) | data formatting | bytes 2621440 | tf_op jit(solution)/shard_map/transpose | solution.py:182
  147.9 10.6 %all-to-all-done.3.kv_ref = bf16[8,256,128]{2,1,0:T(8,128)(2,1)S(1)} async-done(((bf16[8,256,128]{2,1,0:T(8,128)(2,1)}), bf16[8,256,128]{2,1,0:T(8,128)(2,1)S(1)}, u32[]{:S(2)}, u32[]{:S(2)}) %all-to-all-start.3) | async-done | bytes 524320 | tf_op jit(solution)/shard_map/kv_gather/all_to_all | solution.py:21
  158.5 2.9 %shard_map.70 = bf16[128,640]{1,0:T(8,128)(2,1)} custom-call(s32[1]{0:T(128)} %bitcast.rank_ref, bf16[8,320,128]{2,1,0:T(8,128)(2,1)S(1)} %all-to-all-done.1.part_ref, bf16[8,256,128]{2,1,0:T(8,128)(2,1)S(1)} %all-to-all-done.3.kv_ref, f32[7,128]{1,0:T(8,128)S(1)} %bitcast.18, f32[128,128]{1,0:T(8,128)S(1)} %get-tuple-element.19.cos_ref, ...), custom_call_target="tpu_custom_call" | custom-call | flops 209715200 | bytes 1482756 | tf_op jit(solution)/shard_map/pallas_call | solution.py:32
  (3 shorter events, 0.0 us)
Async XLA Ops:
  3.8 21.4 %collective-permute-start.1 = (bf16[40,448]{1,0:T(8,128)(2,1)S(1)}, bf16[40,448]{1,0:T(8,128)(2,1)S(1)}, u32[]{:S(2)}, u32[]{:S(2)}) collective-permute-start(bf16[40,448]{1,0:T(8,128)(2,1)S(1)} %get-tuple-element.13), channel_id=1, source_target_pairs={{0,1},{1,0},{2,3},{3,2},{4,5},{5,4},{6,7},{7,6},{8,9},{9,8},{10,11... | collective-permute-start | bytes 107528 | tf_op jit(solution)/shard_map/w_swap/ppermute | solution.py:168
  10.4 23.4 %all-to-all-start.4 = ((bf16[8,40,128]{2,1,0:T(8,128)(2,1)}), bf16[8,40,128]{2,1,0:T(8,128)(2,1)S(1)}, u32[]{:S(2)}, u32[]{:S(2)}) async-start(bf16[8,40,128]{2,1,0:T(8,128)(2,1)} %broadcast_in_dim.17), calls=%async_computation.4 | async-start | bytes 163840 | tf_op jit(solution)/shard_map/pol_rep/all_to_all | solution.py:21
  71.7 5.0 %copy-start.2 = (bf16[1024,640]{1,0:T(8,128)(2,1)S(1)}, bf16[1024,640]{1,0:T(8,128)(2,1)}, u32[]{:S(2)}) copy-start(bf16[1024,640]{1,0:T(8,128)(2,1)} %own_ref.1) | copy-start | bytes 3932164
  71.7 37.5 %all-to-all-start.5 = ((bf16[16,320,128]{2,1,0:T(8,128)(2,1)}), bf16[16,320,128]{2,1,0:T(8,128)(2,1)}, u32[]{:S(2)}, u32[]{:S(2)}) async-start(bf16[16,320,128]{2,1,0:T(8,128)(2,1)} %broadcast_in_dim.18), calls=%async_computation.5 | async-start | bytes 2621440 | tf_op jit(solution)/shard_map/pol_fsdp/all_to_all | solution.py:21
  76.6 29.8 %collective-permute-start = (bf16[1024,640]{1,0:T(8,128)(2,1)S(1)}, bf16[1024,640]{1,0:T(8,128)(2,1)S(1)}, u32[]{:S(2)}, u32[]{:S(2)}) collective-permute-start(bf16[1024,640]{1,0:T(8,128)(2,1)S(1)} %copy-done.2), channel_id=1, source_target_pairs={{0,1},{1,0},{2,3},{3,2},{4,5},{5,4},{6,7},{7,6},{8,9},{9,8},{10,11... | collective-permute-start | bytes 3932168 | tf_op jit(solution)/shard_map/t_swap/ppermute | solution.py:170
  109.2 16.6 %copy-start = (s32[1,1024]{1,0:T(1,128)S(1)}, s32[1,1024]{1,0:T(1,128)}, u32[]{:S(2)}) copy-start(s32[1,1024]{1,0:T(1,128)} %param.8) | copy-start | bytes 12292
  109.2 17.2 %copy-start.1 = (f32[896]{0:T(1024)S(1)}, f32[896]{0:T(1024)}, u32[]{:S(2)}) copy-start(f32[896]{0:T(1024)} %param.7) | copy-start | bytes 10756
  122.2 19.6 %all-to-all-start.1 = ((bf16[8,320,128]{2,1,0:T(8,128)(2,1)}), bf16[8,320,128]{2,1,0:T(8,128)(2,1)S(1)}, u32[]{:S(2)}, u32[]{:S(2)}) async-start(bf16[8,320,128]{2,1,0:T(8,128)(2,1)} %get-tuple-element.4), calls=%async_computation.1 | async-start | bytes 1310720 | tf_op jit(solution)/shard_map/q_sum/all_to_all | solution.py:21
  141.8 16.7 %all-to-all-start.3 = ((bf16[8,256,128]{2,1,0:T(8,128)(2,1)}), bf16[8,256,128]{2,1,0:T(8,128)(2,1)S(1)}, u32[]{:S(2)}, u32[]{:S(2)}) async-start(bf16[8,256,128]{2,1,0:T(8,128)(2,1)} %shard_map.69), calls=%async_computation.3 | async-start | bytes 1048576 | tf_op jit(solution)/shard_map/kv_gather/all_to_all | solution.py:21

commit v2 on v1

v2 whole, which is shorter than its diff:
```python
import jax
import jax.numpy as jnp
from jax import lax
from jax.experimental import pallas as pl
from jax.experimental.pallas import tpu as pltpu
from jax.sharding import PartitionSpec as P

QH = 40
KVH = 8
HD = 128
HALF = HD // 2
SHARE = QH // KVH
WINDOW = 5


def copies_of(array, count):
    return jnp.broadcast_to(array, (count, *array.shape))


def exchanged(blocks, axis):
    return lax.all_to_all(blocks, axis, split_axis=0, concat_axis=0, tiled=True)


def cost(flops, moved):
    return pl.CostEstimate(flops=flops, bytes_accessed=moved, transcendentals=0)


def call(kernel, outs, flops, *args, scalars=0):
    vmem = pl.BlockSpec(memory_space=pltpu.VMEM)
    smem = pl.BlockSpec(memory_space=pltpu.SMEM)
    moved = sum(a.size * a.dtype.itemsize for a in (*args, *outs))
    return pl.pallas_call(
        kernel,
        out_shape=outs if len(outs) > 1 else outs[0],
        in_specs=[smem] * scalars + [vmem] * (len(args) - scalars),
        out_specs=tuple(vmem for _ in outs) if len(outs) > 1 else vmem,
        compiler_params=pltpu.CompilerParams(vmem_limit_bytes=24 * 1024 * 1024),
        cost_estimate=cost(flops, moved),
    )(*args)


def project(tokens_ref, w_hbm, kv_ref, q_ref, w_ref, sem):
    load = pltpu.make_async_copy(w_hbm, w_ref, sem)
    load.start()
    load.wait()
    blocks = kv_ref.shape[0]
    rows = tokens_ref.shape[0]
    size = rows // blocks
    step = rows // 2
    for part in range(2):
        at = part * step
        own = tokens_ref[at : at + step, :]
        value = jnp.dot(own, w_ref[:, SHARE * HD :], preferred_element_type=jnp.float32)
        value = value.astype(jnp.bfloat16)
        for b in range(step // size):
            j = at // size + b
            kv_ref[j, :size] = value[b * size : (b + 1) * size, :HD]
            kv_ref[j, size:] = value[b * size : (b + 1) * size, HD:]
        value = jnp.dot(own, w_ref[:, : SHARE * HD], preferred_element_type=jnp.float32)
        q_ref[at : at + step, :] = value.astype(jnp.bfloat16)


def projected(tokens, weights, blocks):
    rows, features = tokens.shape
    vmem = pl.BlockSpec(memory_space=pltpu.VMEM)
    return pl.pallas_call(
        project,
        out_shape=(
            jax.ShapeDtypeStruct((blocks, 2 * rows // blocks, HD), jnp.bfloat16),
            jax.ShapeDtypeStruct((rows, SHARE * HD), jnp.bfloat16),
        ),
        in_specs=[vmem, pl.BlockSpec(memory_space=pltpu.HBM)],
        out_specs=(vmem, vmem),
        scratch_shapes=[pltpu.VMEM(weights.shape, weights.dtype), pltpu.SemaphoreType.DMA],
        compiler_params=pltpu.CompilerParams(vmem_limit_bytes=60 * 1024 * 1024),
        cost_estimate=cost(2 * rows * weights.size, 2 * (tokens.size + weights.size)),
    )(tokens, weights)


def turned(value, cosine, sine):
    return value * cosine + pltpu.roll(value, HALF, 1) * sine


def added(ref, rows):
    value = ref[0, rows].astype(jnp.float32)
    for j in range(1, ref.shape[0]):
        value = value + ref[j, rows].astype(jnp.float32)
    return value


def keys_and_values(part_ref, bias_ref, cos_ref, sin_ref, out_ref):
    size = part_ref.shape[1] // 2
    key = added(part_ref, slice(0, size)) + bias_ref[SHARE : SHARE + 1]
    key = turned(key, cos_ref[...], sin_ref[...]).astype(jnp.bfloat16)
    val = added(part_ref, slice(size, 2 * size)) + bias_ref[SHARE + 1 : SHARE + 2]
    val = val.astype(jnp.bfloat16)
    for j in range(out_ref.shape[0]):
        out_ref[j, :size] = key
        out_ref[j, size:] = val


def attend(rank_ref, q_ref, kv_ref, bias_ref, cos_ref, sin_ref, seg_ref, mine_ref, out_ref):
    size = out_ref.shape[0]
    blocks = kv_ref.shape[0]
    window = min(WINDOW, blocks)
    rank = rank_ref[0]
    first = jnp.clip(rank - (window - 1), 0, blocks - window)
    span = kv_ref[pl.ds(first, window)]
    keys = span[:, :size].reshape(window * size, HD)
    vals = span[:, size:].reshape(window * size, HD)
    row = rank * size + lax.broadcasted_iota(jnp.int32, (size, size), 0)
    lane = lax.broadcasted_iota(jnp.int32, (size, size), 1)
    masks = []
    for b in range(window):
        seg = seg_ref[pl.ds(first + b, 1), :]
        column = (first + b) * size + lane
        masks.append((mine_ref[...] == seg) & (column <= row))
    allowed = jnp.concatenate(masks, axis=1)
    cosine, sine = cos_ref[...], sin_ref[...]
    for h in range(SHARE):
        query = q_ref[:, h * HD : (h + 1) * HD].astype(jnp.float32) + bias_ref[h : h + 1]
        query = turned(query, cosine, sine).astype(jnp.bfloat16)
        scores = lax.dot_general(
            query, keys, (((1,), (1,)), ((), ())), preferred_element_type=jnp.float32
        )
        scores = jnp.where(allowed, scores / jnp.sqrt(jnp.float32(HD)), -1e30)
        top = jnp.max(scores, axis=-1, keepdims=True)
        expo = jnp.exp(scores - top)
        weights = (expo / jnp.sum(expo, axis=-1, keepdims=True)).astype(jnp.bfloat16)
        context = jnp.dot(weights, vals, preferred_element_type=jnp.float32)
        out_ref[:, h * HD : (h + 1) * HD] = context.astype(jnp.bfloat16)


def per_device(tokens, ref_qkv, ref_bias, segment_ids, policy_key):
    replicas = lax.axis_size("rep")
    shards = lax.axis_size("fsdp")
    rows, features = tokens.shape
    mine = rows // replicas
    rank = lax.axis_index("rep")
    bf16, f32 = jnp.bfloat16, jnp.float32

    with jax.named_scope("w_gather"):
        weights = exchanged(copies_of(ref_qkv, shards), "fsdp").reshape(features, -1)
    blocks, width = policy_key.shape
    with jax.named_scope("pol_rep"):
        inner = exchanged(copies_of(policy_key, replicas), "rep").reshape(-1, width)
    with jax.named_scope("pol_fsdp"):
        outer = lax.all_gather(inner, "fsdp", axis=0, tiled=True)
    whole = (
        outer.reshape(shards, replicas, blocks, width)
        .transpose(1, 0, 2, 3)
        .reshape(shards * replicas * blocks, width)
    )

    seg = segment_ids[0]
    start = rank * mine
    my_seg = lax.dynamic_slice_in_dim(seg, start, mine, 0)
    before = jnp.sum((seg[None, :] < my_seg[:, None]).astype(jnp.int32), axis=1)
    pos = start + jnp.arange(mine, dtype=jnp.int32) - before
    freq = 1000000.0 ** (-2.0 * jnp.arange(HALF, dtype=f32) / HD)
    angle = pos.astype(f32)[:, None] * freq[None, :]
    cosine, sine = jnp.cos(angle), jnp.sin(angle)
    cosine = jnp.concatenate([cosine, cosine], axis=1)
    sine = jnp.concatenate([-sine, sine], axis=1)
    bias = ref_bias.reshape(SHARE + 2, HD)

    part_kv, part_q = projected(tokens, weights, replicas)
    with jax.named_scope("q_sum"):
        my_q = lax.psum_scatter(part_q, "rep", scatter_dimension=0, tiled=True)
    with jax.named_scope("kv_sum"):
        part_kv = exchanged(part_kv, "rep")
    my_kv = call(
        keys_and_values,
        (jax.ShapeDtypeStruct((replicas, 2 * mine, HD), bf16),),
        32 * mine * HD,
        part_kv,
        bias,
        cosine,
        sine,
    )
    with jax.named_scope("kv_gather"):
        all_kv = exchanged(my_kv, "rep")
    context = call(
        attend,
        (jax.ShapeDtypeStruct((mine, SHARE * HD), bf16),),
        4 * SHARE * mine * WINDOW * mine * HD,
        rank.reshape(1),
        my_q,
        all_kv,
        bias,
        cosine,
        sine,
        seg.reshape(replicas, mine),
        my_seg[:, None],
        scalars=1,
    )
    return (context, whole)


def solution(mesh):
    in_specs = (
        P("fsdp", "rep"),
        P(("rep", "fsdp"), "tp"),
        P("tp"),
        P("fsdp", None),
        P(("rep", "fsdp"), "tp"),
    )
    out_specs = (P(("fsdp", "rep"), "tp"), P(None, "tp"))
    return jax.shard_map(
        per_device, mesh=mesh, in_specs=in_specs, out_specs=out_specs, check_vma=False
    )
```

time: 162 us -> 140 us (0.86)
  the two profiles are of different devices: /device:TPU:34 before, /device:TPU:48 now
where the time goes in v2:
time: 140 us
  blocking collectives  67.5 us (48%)
  waiting for transfers between devices  34.3 us (24%)
  between operations  15.6 us (11%)
  Pallas kernels  9.2 us (7%)
  starting transfers between devices  7.08 us (5%)
  local copies, waits for them, and re-layouts  5.24 us (4%)
    all_to_all x2, blocking collectives, exchanged(): return lax.all_to_all(blocks, axis, split_axis=0, concat_axis=0, tiled=True)  67.5 us
    all_to_all x2, waiting for transfers between devices, exchanged(): return lax.all_to_all(blocks, axis, split_axis=0, concat_axis=0, tiled=True)  24 us
    reduce_scatter x1, waiting for transfers between devices, per_device(): my_q = lax.psum_scatter(part_q, 'rep', scatter_dimension=0, tiled=True)  7.72 us
    all_to_all x2, starting transfers between devices, exchanged(): return lax.all_to_all(blocks, axis, split_axis=0, concat_axis=0, tiled=True)  7 us
    pallas_call x1, Pallas kernels, projected(): pl.pallas_call(project, out_shape=(jax.ShapeDtypeStruct((blocks, 2 * rows...  5.38 us
    pallas_call x2, Pallas kernels, call(): pl.pallas_call(kernel, out_shape=outs if len(outs) > 1 else outs[0], in_s...  3.82 us
  transfers between devices with their start and end apart: 4, of which 4 were waited for; matrix products, arithmetic and copies ran while one was open for 3% of the time, Pallas kernels for 5%

profile of v2, /device:TPU:48, one launch (start us, length us, event | category | flops | bytes accessed | tf_op | source)
XLA Modules:
  0.0 139.6 jit_solution(14410768107049349149)
XLA Ops:
  8.0 0.0 all-gather.2.cloned.1.call-start
  8.0 0.7 broadcast_in_dim.14
  8.8 25.1 %all_to_all.20 = bf16[8,40,128]{2,1,0:T(8,128)(2,1)} all-to-all(bf16[8,40,128]{2,1,0:T(8,128)(2,1)S(1)} %broadcast_in_dim.14), channel_id=1, replica_groups=mesh['fsdp'=16,'tp'=8,'rep'=8] {'rep'}, dimensions={0} | all-to-all | bytes 163840 | tf_op jit(solution)/shard_map/pol_rep/all_to_all | solution.py:21
  33.9 0.0 all-gather.2.cloned.1.call-update
  33.9 0.0 reduce-scatter.2.cloned.1.call-start
  34.0 1.0 broadcast_in_dim.12
  34.9 42.4 %all_to_all.21 = bf16[16,40,896]{2,1,0:T(8,128)(2,1)} all-to-all(bf16[16,40,896]{2,1,0:T(8,128)(2,1)S(1)} %broadcast_in_dim.12), channel_id=1, replica_groups=mesh['fsdp'=16,'tp'=8,'rep'=8] {'fsdp'}, dimensions={0} | all-to-all | bytes 2293760 | tf_op jit(solution)/shard_map/w_gather/all_to_all | solution.py:21
  77.4 5.4 %shard_map.68 = (bf16[8,256,128]{2,1,0:T(8,128)(2,1)}, bf16[1024,640]{1,0:T(8,128)(2,1)}) custom-call(bf16[1024,640]{1,0:T(8,128)(2,1)} %tokens_ref.1, bf16[640,896]{1,0:T(8,128)(2,1)} %bitcast.20), custom_call_target="tpu_custom_call" | custom-call | flops 1174405120 | bytes 2457600 | tf_op jit(solution)/shard_map/pallas_call | solution.py:66
  82.7 0.0 copy-start.1
  82.8 0.0 copy-start.2
  82.8 0.0 reduce-scatter.2.cloned.1.call-update
  82.8 3.5 %all-to-all-start.1 = ((bf16[8,256,128]{2,1,0:T(8,128)(2,1)}), bf16[8,256,128]{2,1,0:T(8,128)(2,1)S(1)}, u32[]{:S(2)}, u32[]{:S(2)}) async-start(bf16[8,256,128]{2,1,0:T(8,128)(2,1)} %get-tuple-element.5), calls=%async_computation.2 | async-start | bytes 1048576 | tf_op jit(solution)/shard_map/kv_sum/all_to_all | solution.py:21
  86.3 0.0 copy-done.1
  86.4 0.2 convert_reduce_fusion
  86.6 0.3 fusion
  86.9 0.1 pad_maximum_fusion
  87.0 13.7 %all-to-all-done.1.part_ref = bf16[8,256,128]{2,1,0:T(8,128)(2,1)S(1)} async-done(((bf16[8,256,128]{2,1,0:T(8,128)(2,1)}), bf16[8,256,128]{2,1,0:T(8,128)(2,1)S(1)}, u32[]{:S(2)}, u32[]{:S(2)}) %all-to-all-start.1) | async-done | bytes 524320 | tf_op jit(solution)/shard_map/kv_sum/all_to_all | solution.py:21
  100.7 0.0 copy-done.2
  100.7 0.9 shard_map.69
  101.7 3.5 %all-to-all-start.2 = ((bf16[8,256,128]{2,1,0:T(8,128)(2,1)}), bf16[8,256,128]{2,1,0:T(8,128)(2,1)S(1)}, u32[]{:S(2)}, u32[]{:S(2)}) async-start(bf16[8,256,128]{2,1,0:T(8,128)(2,1)} %shard_map.69), calls=%async_computation.3 | async-start | bytes 1048576 | tf_op jit(solution)/shard_map/kv_gather/all_to_all | solution.py:21
  105.2 0.1 copy.11.mine_ref
  105.3 2.6 %all-gather.2.cloned.1.call-done = bf16[5120,128]{1,0:T(8,128)(2,1)} async-done(((bf16[320,128]{1,0:T(8,128)(2,1)}), bf16[5120,128]{1,0:T(8,128)(2,1)}) %all-gather.2.cloned.1.call-update) | async-done | bytes 1310736 | tf_op jit(solution)/shard_map/pol_fsdp/all_gather | solution.py:148
  107.8 2.5 %copy.12 = bf16[8,16,40,128]{3,2,1,0:T(8,128)(2,1)} copy(bf16[8,16,40,128]{3,2,0,1:T(8,128)(2,1)} %bitcast.18) | data formatting | bytes 2621440 | tf_op jit(solution)/shard_map/transpose | solution.py:151
  110.3 10.3 %all-to-all-done.2.kv_ref = bf16[8,256,128]{2,1,0:T(8,128)(2,1)S(1)} async-done(((bf16[8,256,128]{2,1,0:T(8,128)(2,1)}), bf16[8,256,128]{2,1,0:T(8,128)(2,1)S(1)}, u32[]{:S(2)}, u32[]{:S(2)}) %all-to-all-start.2) | async-done | bytes 524320 | tf_op jit(solution)/shard_map/kv_gather/all_to_all | solution.py:21
  120.6 7.7 %reduce-scatter.2.cloned.1.call-done.q_ref = bf16[128,640]{1,0:T(8,128)(2,1)} async-done(((bf16[1024,640]{1,0:T(8,128)(2,1)}), bf16[128,640]{1,0:T(8,128)(2,1)}) %reduce-scatter.2.cloned.1.call-update) | async-done | bytes 163856 | tf_op jit(solution)/shard_map/q_sum/reduce_scatter | solution.py:169
  128.3 0.0 copy-start
  128.3 0.9 copy-done
  129.2 2.9 %shard_map.70 = bf16[128,640]{1,0:T(8,128)(2,1)} custom-call(s32[1]{0:T(128)} %bitcast.rank_ref, bf16[128,640]{1,0:T(8,128)(2,1)S(1)} %copy-done, bf16[8,256,128]{2,1,0:T(8,128)(2,1)S(1)} %all-to-all-done.2.kv_ref, f32[7,128]{1,0:T(8,128)S(1)} %bitcast.17, f32[128,128]{1,0:T(8,128)S(1)} %get-tuple-element.11.cos_ref, ...), custom_call_target="tpu_custom_call" | custom-call | flops 209715200 | bytes 991236 | tf_op jit(solution)/shard_map/pallas_call | solution.py:32
  (3 shorter events, 0.0 us)
Async XLA Ops:
  8.0 99.8 %all-gather.2.cloned.1.call-start = ((), (), s32[]{:S(2)}) async-start(), calls=%async_computation.6 | async-start | bytes 1392640 | tf_op jit(solution)/shard_map/pol_fsdp/all_gather | solution.py:148
  33.9 94.4 %reduce-scatter.2.cloned.1.call-start = ((), (), s32[]{:S(2)}) async-start(), calls=%async_computation.5 | async-start | bytes 1474560 | tf_op jit(solution)/shard_map/q_sum/reduce_scatter | solution.py:169
  82.7 3.6 %copy-start.1 = (s32[1,1024]{1,0:T(1,128)S(1)}, s32[1,1024]{1,0:T(1,128)}, u32[]{:S(2)}) copy-start(s32[1,1024]{1,0:T(1,128)} %param.8) | copy-start | bytes 12292
  82.8 18.0 %copy-start.2 = (f32[896]{0:T(1024)S(1)}, f32[896]{0:T(1024)}, u32[]{:S(2)}) copy-start(f32[896]{0:T(1024)} %param.7) | copy-start | bytes 10756
  82.8 18.0 %all-to-all-start.1 = ((bf16[8,256,128]{2,1,0:T(8,128)(2,1)}), bf16[8,256,128]{2,1,0:T(8,128)(2,1)S(1)}, u32[]{:S(2)}, u32[]{:S(2)}) async-start(bf16[8,256,128]{2,1,0:T(8,128)(2,1)} %get-tuple-element.5), calls=%async_computation.2 | async-start | bytes 1048576 | tf_op jit(solution)/shard_map/kv_sum/all_to_all | solution.py:21
  101.7 18.9 %all-to-all-start.2 = ((bf16[8,256,128]{2,1,0:T(8,128)(2,1)}), bf16[8,256,128]{2,1,0:T(8,128)(2,1)S(1)}, u32[]{:S(2)}, u32[]{:S(2)}) async-start(bf16[8,256,128]{2,1,0:T(8,128)(2,1)} %shard_map.69), calls=%async_computation.3 | async-start | bytes 1048576 | tf_op jit(solution)/shard_map/kv_gather/all_to_all | solution.py:21
  128.3 0.9 copy-start
Sparse Core Ops, SparseCore 0:
  34.0 73.7 all-gather.1
Sparse Core Ops, SparseCore 1:
  82.9 45.4 reduce-scatter.1

commit v3 on v1

v3 whole, which is shorter than its diff:
```python
import jax
import jax.numpy as jnp
from jax import lax
from jax.experimental import pallas as pl
from jax.experimental.pallas import tpu as pltpu
from jax.sharding import PartitionSpec as P


QH = 40
KVH = 8
HD = 128
HALF = HD // 2
SHARE = QH // KVH
WINDOW = 5


def copies_of(array, count):
    return jnp.broadcast_to(array, (count, *array.shape))


def exchanged(blocks, axis):
    return lax.all_to_all(blocks, axis, split_axis=0, concat_axis=0, tiled=True)


def cost(flops, moved):
    return pl.CostEstimate(flops=flops, bytes_accessed=moved, transcendentals=0)


def call(kernel, outs, flops, *args, scalars=0):
    vmem = pl.BlockSpec(memory_space=pltpu.VMEM)
    smem = pl.BlockSpec(memory_space=pltpu.SMEM)
    moved = sum(a.size * a.dtype.itemsize for a in (*args, *outs))
    return pl.pallas_call(
        kernel,
        out_shape=outs if len(outs) > 1 else outs[0],
        in_specs=[smem] * scalars + [vmem] * (len(args) - scalars),
        out_specs=tuple(vmem for _ in outs) if len(outs) > 1 else vmem,
        compiler_params=pltpu.CompilerParams(vmem_limit_bytes=24 * 1024 * 1024),
        cost_estimate=cost(flops, moved),
    )(*args)


def lanes_below_half(shape):
    return lax.broadcasted_iota(jnp.int32, shape, len(shape) - 1) < HALF


def split(rank_ref, w_ref, keep_ref, give_ref):
    key, val = w_ref[:, 5 * HD : 6 * HD], w_ref[:, 6 * HD :]
    low, high = w_ref[:, : 2 * HD], w_ref[:, 3 * HD : 5 * HD]
    left, right = w_ref[:, 2 * HD : 2 * HD + HALF], w_ref[:, 2 * HD + HALF : 3 * HD]
    odd = jnp.bitwise_and(rank_ref[0], 1)

    @pl.when(odd == 0)
    def _():
        keep_ref[...] = jnp.concatenate([key, low, left], axis=1)
        give_ref[...] = jnp.concatenate([right, val, high], axis=1)

    @pl.when(odd == 1)
    def _():
        keep_ref[...] = jnp.concatenate([val, high, right], axis=1)
        give_ref[...] = jnp.concatenate([left, key, low], axis=1)


def pack(keep_ref, got_ref, inner_ref, out_ref):
    parts = [keep_ref[...], got_ref[...]] + [inner_ref[j] for j in range(inner_ref.shape[0])]
    row = jnp.concatenate(parts, axis=1)
    for j in range(out_ref.shape[0]):
        out_ref[j] = row


def arrange(in_ref, out_ref):
    out_ref[0] = in_ref[...]


def arranged(gathered, replicas, width):
    rows = gathered.shape[0]
    first = 7 * HD // width
    return pl.pallas_call(
        arrange,
        grid=(replicas,),
        out_shape=jax.ShapeDtypeStruct((replicas, rows, width), gathered.dtype),
        in_specs=[pl.BlockSpec((rows, width), lambda j: (0, first + j))],
        out_specs=pl.BlockSpec((1, rows, width), lambda j: (j, 0, 0)),
        compiler_params=pltpu.CompilerParams(vmem_limit_bytes=8 * 1024 * 1024),
        cost_estimate=cost(0, 4 * replicas * rows * width),
    )(gathered)


def project(own_hbm, other_hbm, w_hbm, out_ref, own_ref, other_ref, w_ref, sems):
    blocks = out_ref.shape[0]
    rows = own_hbm.shape[0]
    step = rows // 2
    loads = [pltpu.make_async_copy(w_hbm.at[:, : 7 * HD], w_ref, sems.at[0])]
    for part in range(2):
        span = pl.ds(part * step, step)
        loads.append(pltpu.make_async_copy(own_hbm.at[span], own_ref.at[span], sems.at[1 + 2 * part]))
        loads.append(
            pltpu.make_async_copy(other_hbm.at[span], other_ref.at[span], sems.at[2 + 2 * part])
        )
    for load in loads:
        load.start()
    loads[0].wait()
    shared = w_ref[:, 3 * HD : 4 * HD]
    w_own = w_ref[:, : 4 * HD]
    swapped = pltpu.roll(shared.astype(jnp.float32), HALF, 1).astype(jnp.bfloat16)
    w_other = jnp.concatenate([w_ref[:, 4 * HD :], swapped], axis=1)
    size = rows // blocks
    low = lanes_below_half((size // 2, HD))
    for part in range(2):
        loads[1 + 2 * part].wait()
        loads[2 + 2 * part].wait()
        at = part * step
        value = jnp.dot(own_ref[at : at + step, :], w_own, preferred_element_type=jnp.float32)
        value = value + jnp.dot(
            other_ref[at : at + step, :], w_other, preferred_element_type=jnp.float32
        )
        for b in range(step // size):
            j = at // size + b
            piece = value[b * size : (b + 1) * size]
            for c in range(3):
                out_ref[j, c * size : (c + 1) * size] = piece[:, c * HD : (c + 1) * HD].astype(
                    jnp.bfloat16
                )
            last = piece[:, 3 * HD :]
            packed = jnp.where(low, last[: size // 2], pltpu.roll(last[size // 2 :], HALF, 1))
            out_ref[j, 3 * size :] = packed.astype(jnp.bfloat16)


def projected(own, other, gathered, blocks):
    rows, features = own.shape
    vmem = pl.BlockSpec(memory_space=pltpu.VMEM)
    hbm = pl.BlockSpec(memory_space=pltpu.HBM)
    return pl.pallas_call(
        project,
        out_shape=jax.ShapeDtypeStruct((blocks, 7 * rows // blocks // 2, HD), jnp.bfloat16),
        in_specs=[hbm, hbm, hbm],
        out_specs=vmem,
        scratch_shapes=[
            pltpu.VMEM(own.shape, own.dtype),
            pltpu.VMEM(own.shape, own.dtype),
            pltpu.VMEM((features, 7 * HD), own.dtype),
            pltpu.SemaphoreType.DMA((5,)),
        ],
        compiler_params=pltpu.CompilerParams(vmem_limit_bytes=62 * 1024 * 1024),
        cost_estimate=cost(4 * rows * features * 4 * HD, 4 * own.size + 2 * gathered.size),
    )(own, other, gathered)


def turned(value, cosine, sine):
    return value * cosine + pltpu.roll(value, HALF, 1) * sine


def added(ref, parity, rows):
    value = ref[parity, rows].astype(jnp.float32)
    for j in range(parity + 2, ref.shape[0], 2):
        value = value + ref[j, rows].astype(jnp.float32)
    return value


def keys_and_values(part_ref, bias_ref, cos_ref, sin_ref, out_ref):
    size = out_ref.shape[1] // 2
    rows = slice(0, size)
    key = added(part_ref, 0, rows) + bias_ref[SHARE : SHARE + 1]
    key = turned(key, cos_ref[...], sin_ref[...]).astype(jnp.bfloat16)
    val = (added(part_ref, 1, rows) + bias_ref[SHARE + 1 : SHARE + 2]).astype(jnp.bfloat16)
    for j in range(out_ref.shape[0]):
        out_ref[j, :size] = key
        out_ref[j, size:] = val


def attend(rank_ref, part_ref, kv_ref, bias_ref, cos_ref, sin_ref, seg_ref, mine_ref, out_ref):
    size = out_ref.shape[0]
    blocks = kv_ref.shape[0]
    window = min(WINDOW, blocks)
    rank = rank_ref[0]
    first = jnp.clip(rank - (window - 1), 0, blocks - window)
    low = lanes_below_half((size // 2, HD))
    left = added(part_ref, 0, slice(3 * size, 7 * size // 2))
    right = added(part_ref, 1, slice(3 * size, 7 * size // 2))
    middle = jnp.concatenate(
        [
            jnp.where(low, left, pltpu.roll(right, HALF, 1)),
            jnp.where(low, pltpu.roll(left, HALF, 1), right),
        ],
        axis=0,
    )
    heads = [
        added(part_ref, 0, slice(size, 2 * size)),
        added(part_ref, 0, slice(2 * size, 3 * size)),
        middle,
        added(part_ref, 1, slice(size, 2 * size)),
        added(part_ref, 1, slice(2 * size, 3 * size)),
    ]
    span = kv_ref[pl.ds(first, window)]
    keys = span[:, :size].reshape(window * size, HD)
    vals = span[:, size:].reshape(window * size, HD)
    row = rank * size + lax.broadcasted_iota(jnp.int32, (size, size), 0)
    lane = lax.broadcasted_iota(jnp.int32, (size, size), 1)
    masks = []
    for b in range(window):
        seg = seg_ref[pl.ds(first + b, 1), :]
        column = (first + b) * size + lane
        masks.append((mine_ref[...] == seg) & (column <= row))
    allowed = jnp.concatenate(masks, axis=1)
    cosine, sine = cos_ref[...], sin_ref[...]
    for h in range(SHARE):
        query = turned(heads[h] + bias_ref[h : h + 1], cosine, sine).astype(jnp.bfloat16)
        scores = lax.dot_general(
            query, keys, (((1,), (1,)), ((), ())), preferred_element_type=jnp.float32
        )
        scores = jnp.where(allowed, scores / jnp.sqrt(jnp.float32(HD)), -1e30)
        top = jnp.max(scores, axis=-1, keepdims=True)
        expo = jnp.exp(scores - top)
        weights = (expo / jnp.sum(expo, axis=-1, keepdims=True)).astype(jnp.bfloat16)
        context = jnp.dot(weights, vals, preferred_element_type=jnp.float32)
        out_ref[:, h * HD : (h + 1) * HD] = context.astype(jnp.bfloat16)


def body(tokens, ref_qkv, ref_bias, segment_ids, policy_key):
    replicas = lax.axis_size("rep")
    shards = lax.axis_size("fsdp")
    rows, features = tokens.shape
    mine = rows // replicas
    rank = lax.axis_index("rep")
    swap = [(i, i ^ 1) for i in range(replicas)]
    bf16, f32 = jnp.bfloat16, jnp.float32

    own_features = ref_qkv.shape[0]
    half = jax.ShapeDtypeStruct((own_features, 7 * HALF), bf16)
    keep, give = call(split, (half, half), 0, rank.reshape(1), ref_qkv, scalars=1)
    got = lax.ppermute(give, "rep", swap)
    other = lax.ppermute(tokens, "rep", swap)
    width = policy_key.shape[1]
    inner = exchanged(copies_of(policy_key, replicas), "rep")
    packed = jax.ShapeDtypeStruct((shards, own_features, 7 * HD + replicas * width), bf16)
    packed = call(pack, (packed,), 0, keep, got, inner)
    gathered = exchanged(packed, "fsdp").reshape(features, -1)
    whole = arranged(gathered, replicas, width).reshape(-1, width)

    seg = segment_ids[0]
    start = rank * mine
    my_seg = lax.dynamic_slice_in_dim(seg, start, mine, 0)
    before = jnp.sum((seg[None, :] < my_seg[:, None]).astype(jnp.int32), axis=1)
    pos = start + jnp.arange(mine, dtype=jnp.int32) - before
    freq = 1000000.0 ** (-2.0 * jnp.arange(HALF, dtype=f32) / HD)
    angle = pos.astype(f32)[:, None] * freq[None, :]
    cosine, sine = jnp.cos(angle), jnp.sin(angle)
    cosine = jnp.concatenate([cosine, cosine], axis=1)
    sine = jnp.concatenate([-sine, sine], axis=1)
    bias = ref_bias.reshape(SHARE + 2, HD)

    part = projected(tokens, other, gathered, replicas)
    part = exchanged(part, "rep")
    my_kv = call(
        keys_and_values,
        (jax.ShapeDtypeStruct((replicas, 2 * mine, HD), bf16),),
        16 * mine * HD,
        part,
        bias,
        cosine,
        sine,
    )
    all_kv = exchanged(my_kv, "rep")
    context = call(
        attend,
        (jax.ShapeDtypeStruct((mine, SHARE * HD), bf16),),
        4 * SHARE * mine * WINDOW * mine * HD,
        rank.reshape(1),
        part,
        all_kv,
        bias,
        cosine,
        sine,
        seg.reshape(replicas, mine),
        my_seg[:, None],
        scalars=1,
    )
    return (context, whole)


def solution(mesh):
    in_specs = (
        P("fsdp", "rep"),
        P(("rep", "fsdp"), "tp"),
        P("tp"),
        P("fsdp", None),
        P(("rep", "fsdp"), "tp"),
    )
    out_specs = (P(("fsdp", "rep"), "tp"), P(None, "tp"))
    return jax.shard_map(body, mesh=mesh, in_specs=in_specs, out_specs=out_specs, check_vma=False)
```

time: 162 us -> 152 us (0.938)
  the two profiles are of different devices: /device:TPU:34 before, /device:TPU:89 now
where the time goes in v3:
time: 152 us; the launch traced here: 151 us
  waiting for transfers between devices  94.2 us (62%)
  starting transfers between devices  37.6 us (25%)
  Pallas kernels  15.6 us (10%)
  local copies, waits for them, and re-layouts  2.37 us (2%)
    all_to_all x4, waiting for transfers between devices, exchanged(): return lax.all_to_all(blocks, axis, split_axis=0, concat_axis=0, tiled=True)  64.9 us
    all_to_all x4, starting transfers between devices, exchanged(): return lax.all_to_all(blocks, axis, split_axis=0, concat_axis=0, tiled=True)  32.1 us
    ppermute x1, waiting for transfers between devices, body(): other = lax.ppermute(tokens, 'rep', swap)  27.6 us
    pallas_call x4, Pallas kernels, call(): pl.pallas_call(kernel, out_shape=outs if len(outs) > 1 else outs[0], in_s...  5.57 us
    pallas_call x1, Pallas kernels, arranged(): pl.pallas_call(arrange, grid=(replicas,), out_shape=jax.ShapeDtypeStruct(...  5.31 us
    pallas_call x1, Pallas kernels, projected(): pl.pallas_call(project, out_shape=jax.ShapeDtypeStruct((blocks, 7 * rows...  4.7 us
    ppermute x1, starting transfers between devices, body(): got = lax.ppermute(give, 'rep', swap)  3.35 us
  transfers between devices with their start and end apart: 6, of which 6 were waited for; matrix products, arithmetic and copies ran while one was open for 0% of the time, Pallas kernels for 4%

profile of v3, /device:TPU:89, one launch (start us, length us, event | category | flops | bytes accessed | tf_op | source)
XLA Modules:
  0.0 151.1 jit_solution(13589195023455224609)
XLA Ops:
  0.6 1.3 broadcast_in_dim.4
  2.0 16.4 %all-to-all-start = ((bf16[8,40,128]{2,1,0:T(8,128)(2,1)}), bf16[8,40,128]{2,1,0:T(8,128)(2,1)S(1)}, u32[]{:S(2)}, u32[]{:S(2)}) async-start(bf16[8,40,128]{2,1,0:T(8,128)(2,1)} %broadcast_in_dim.4), calls=%async_computation | async-start | bytes 163840 | tf_op jit(solution)/shard_map/all_to_all | solution.py:22
  18.4 0.0 copy-start
  18.4 0.9 copy-done
  19.3 0.1 shard_map.68
  19.4 3.4 %collective-permute-start.1 = (bf16[40,448]{1,0:T(8,128)(2,1)S(1)}, bf16[40,448]{1,0:T(8,128)(2,1)S(1)}, u32[]{:S(2)}, u32[]{:S(2)}) collective-permute-start(bf16[40,448]{1,0:T(8,128)(2,1)S(1)} %get-tuple-element.5), channel_id=1, source_target_pairs={{0,1},{1,0},{2,3},{3,2},{4,5},{5,4},{6,7},{7,6},{8,9},{9,8},{10,11... | collective-permute-start | bytes 107528 | tf_op jit(solution)/shard_map/ppermute | solution.py:231
  22.7 1.7 %collective-permute-done.1.got_ref = bf16[40,448]{1,0:T(8,128)(2,1)S(1)} collective-permute-done((bf16[40,448]{1,0:T(8,128)(2,1)S(1)}, bf16[40,448]{1,0:T(8,128)(2,1)S(1)}, u32[]{:S(2)}, u32[]{:S(2)}) %collective-permute-start.1) | collective-permute-done | bytes 35872 | tf_op jit(solution)/shard_map/ppermute | solution.py:231
  24.4 1.5 all-to-all-done.inner_ref
  25.9 1.6 %shard_map.69 = bf16[16,40,1920]{2,1,0:T(8,128)(2,1)} custom-call(bf16[40,448]{1,0:T(8,128)(2,1)S(1)} %get-tuple-element.4.keep_ref, bf16[40,448]{1,0:T(8,128)(2,1)S(1)} %collective-permute-done.1.got_ref, bf16[8,40,128]{2,1,0:T(8,128)(2,1)S(1)} %all-to-all-done.inner_ref), custom_call_target="tpu_custom_call" | custom-call | bytes 2611200 | tf_op jit(solution)/shard_map/pallas_call | solution.py:33
  27.5 0.0 copy-start.3
  27.5 7.7 %all-to-all-start.1 = ((bf16[16,40,1920]{2,1,0:T(8,128)(2,1)}), bf16[16,40,1920]{2,1,0:T(8,128)(2,1)}, u32[]{:S(2)}, u32[]{:S(2)}) async-start(bf16[16,40,1920]{2,1,0:T(8,128)(2,1)} %shard_map.69), calls=%async_computation.1 | async-start | bytes 4915200 | tf_op jit(solution)/shard_map/all_to_all | solution.py:22
  35.2 0.0 copy-done.3
  35.2 2.1 %collective-permute-start = (bf16[1024,640]{1,0:T(8,128)(2,1)S(1)}, bf16[1024,640]{1,0:T(8,128)(2,1)}, u32[]{:S(2)}, u32[]{:S(2)}) collective-permute-start(bf16[1024,640]{1,0:T(8,128)(2,1)S(1)} %copy-done.3), channel_id=1, source_target_pairs={{0,1},{1,0},{2,3},{3,2},{4,5},{5,4},{6,7},{7,6},{8,9},{9,8},{10,11... | collective-permute-start | bytes 3932168 | tf_op jit(solution)/shard_map/ppermute | solution.py:232
  37.4 27.6 %collective-permute-done.other_hbm = bf16[1024,640]{1,0:T(8,128)(2,1)} collective-permute-done((bf16[1024,640]{1,0:T(8,128)(2,1)S(1)}, bf16[1024,640]{1,0:T(8,128)(2,1)}, u32[]{:S(2)}, u32[]{:S(2)}) %collective-permute-start) | collective-permute-done | bytes 1310752 | tf_op jit(solution)/shard_map/ppermute | solution.py:232
  65.0 25.3 %all-to-all-done.1 = bf16[16,40,1920]{2,1,0:T(8,128)(2,1)} async-done(((bf16[16,40,1920]{2,1,0:T(8,128)(2,1)}), bf16[16,40,1920]{2,1,0:T(8,128)(2,1)}, u32[]{:S(2)}, u32[]{:S(2)}) %all-to-all-start.1) | async-done | bytes 2457632 | tf_op jit(solution)/shard_map/all_to_all | solution.py:22
  90.3 4.7 %shard_map.70 = bf16[8,448,128]{2,1,0:T(8,128)(2,1)} custom-call(bf16[1024,640]{1,0:T(8,128)(2,1)} %own_hbm.1, bf16[1024,640]{1,0:T(8,128)(2,1)} %collective-permute-done.other_hbm, bf16[640,1920]{1,0:T(8,128)(2,1)} %bitcast.1.w_hbm.in_ref), custom_call_target="tpu_custom_call" | custom-call | flops 1342177280 | bytes 5079040 | tf_op jit(solution)/shard_map/pallas_call | solution.py:133
  95.0 0.0 copy-start.1
  95.0 0.0 copy-start.2
  95.0 4.5 %all-to-all-start.2 = ((bf16[8,448,128]{2,1,0:T(8,128)(2,1)}), bf16[8,448,128]{2,1,0:T(8,128)(2,1)S(1)}, u32[]{:S(2)}, u32[]{:S(2)}) async-start(bf16[8,448,128]{2,1,0:T(8,128)(2,1)} %shard_map.70), calls=%async_computation.2 | async-start | bytes 1835008 | tf_op jit(solution)/shard_map/all_to_all | solution.py:22
  99.5 0.0 copy-done.1
  99.5 0.2 convert_reduce_fusion
  99.7 0.3 fusion
  100.1 0.1 pad_maximum_fusion
  100.2 25.7 %all-to-all-done.2.part_ref = bf16[8,448,128]{2,1,0:T(8,128)(2,1)S(1)} async-done(((bf16[8,448,128]{2,1,0:T(8,128)(2,1)}), bf16[8,448,128]{2,1,0:T(8,128)(2,1)S(1)}, u32[]{:S(2)}, u32[]{:S(2)}) %all-to-all-start.2) | async-done | bytes 917536 | tf_op jit(solution)/shard_map/all_to_all | solution.py:22
  125.9 0.0 copy-done.2
  125.9 0.9 shard_map.71
  126.8 3.5 %all-to-all-start.3 = ((bf16[8,256,128]{2,1,0:T(8,128)(2,1)}), bf16[8,256,128]{2,1,0:T(8,128)(2,1)S(1)}, u32[]{:S(2)}, u32[]{:S(2)}) async-start(bf16[8,256,128]{2,1,0:T(8,128)(2,1)} %shard_map.71), calls=%async_computation.3 | async-start | bytes 1048576 | tf_op jit(solution)/shard_map/all_to_all | solution.py:22
  130.3 0.1 copy.8.mine_ref
  130.4 5.3 %shard_map.73 = bf16[8,640,128]{2,1,0:T(8,128)(2,1)} custom-call(bf16[640,1920]{1,0:T(8,128)(2,1)} %bitcast.1.w_hbm.in_ref), custom_call_target="tpu_custom_call" | custom-call | bytes 2621440 | tf_op jit(solution)/shard_map/pallas_call | solution.py:78
  135.7 12.5 %all-to-all-done.3.kv_ref = bf16[8,256,128]{2,1,0:T(8,128)(2,1)S(1)} async-done(((bf16[8,256,128]{2,1,0:T(8,128)(2,1)}), bf16[8,256,128]{2,1,0:T(8,128)(2,1)S(1)}, u32[]{:S(2)}, u32[]{:S(2)}) %all-to-all-start.3) | async-done | bytes 524320 | tf_op jit(solution)/shard_map/all_to_all | solution.py:22
  148.2 2.9 %shard_map.72 = bf16[128,640]{1,0:T(8,128)(2,1)} custom-call(s32[1]{0:T(128)} %bitcast.rank_ref, bf16[8,448,128]{2,1,0:T(8,128)(2,1)S(1)} %all-to-all-done.2.part_ref, bf16[8,256,128]{2,1,0:T(8,128)(2,1)S(1)} %all-to-all-done.3.kv_ref, f32[7,128]{1,0:T(8,128)S(1)} %bitcast.13, f32[128,128]{1,0:T(8,128)S(1)} %get-tuple-element.11.cos_ref, ...), custom_call_target="tpu_custom_call" | custom-call | flops 209715200 | bytes 1744900 | tf_op jit(solution)/shard_map/pallas_call | solution.py:33
  (3 shorter events, 0.0 us)
Async XLA Ops:
  2.0 23.9 %all-to-all-start = ((bf16[8,40,128]{2,1,0:T(8,128)(2,1)}), bf16[8,40,128]{2,1,0:T(8,128)(2,1)S(1)}, u32[]{:S(2)}, u32[]{:S(2)}) async-start(bf16[8,40,128]{2,1,0:T(8,128)(2,1)} %broadcast_in_dim.4), calls=%async_computation | async-start | bytes 163840 | tf_op jit(solution)/shard_map/all_to_all | solution.py:22
  18.4 0.9 copy-start
  19.4 5.0 %collective-permute-start.1 = (bf16[40,448]{1,0:T(8,128)(2,1)S(1)}, bf16[40,448]{1,0:T(8,128)(2,1)S(1)}, u32[]{:S(2)}, u32[]{:S(2)}) collective-permute-start(bf16[40,448]{1,0:T(8,128)(2,1)S(1)} %get-tuple-element.5), channel_id=1, source_target_pairs={{0,1},{1,0},{2,3},{3,2},{4,5},{5,4},{6,7},{7,6},{8,9},{9,8},{10,11... | collective-permute-start | bytes 107528 | tf_op jit(solution)/shard_map/ppermute | solution.py:231
  27.5 7.7 %copy-start.3 = (bf16[1024,640]{1,0:T(8,128)(2,1)S(1)}, bf16[1024,640]{1,0:T(8,128)(2,1)}, u32[]{:S(2)}) copy-start(bf16[1024,640]{1,0:T(8,128)(2,1)} %own_hbm.1) | copy-start | bytes 3932164
  27.5 62.8 %all-to-all-start.1 = ((bf16[16,40,1920]{2,1,0:T(8,128)(2,1)}), bf16[16,40,1920]{2,1,0:T(8,128)(2,1)}, u32[]{:S(2)}, u32[]{:S(2)}) async-start(bf16[16,40,1920]{2,1,0:T(8,128)(2,1)} %shard_map.69), calls=%async_computation.1 | async-start | bytes 4915200 | tf_op jit(solution)/shard_map/all_to_all | solution.py:22
  35.2 29.8 %collective-permute-start = (bf16[1024,640]{1,0:T(8,128)(2,1)S(1)}, bf16[1024,640]{1,0:T(8,128)(2,1)}, u32[]{:S(2)}, u32[]{:S(2)}) collective-permute-start(bf16[1024,640]{1,0:T(8,128)(2,1)S(1)} %copy-done.3), channel_id=1, source_target_pairs={{0,1},{1,0},{2,3},{3,2},{4,5},{5,4},{6,7},{7,6},{8,9},{9,8},{10,11... | collective-permute-start | bytes 3932168 | tf_op jit(solution)/shard_map/ppermute | solution.py:232
  95.0 4.5 %copy-start.1 = (s32[1,1024]{1,0:T(1,128)S(1)}, s32[1,1024]{1,0:T(1,128)}, u32[]{:S(2)}) copy-start(s32[1,1024]{1,0:T(1,128)} %param.8) | copy-start | bytes 12292
  95.0 30.9 %copy-start.2 = (f32[896]{0:T(1024)S(1)}, f32[896]{0:T(1024)}, u32[]{:S(2)}) copy-start(f32[896]{0:T(1024)} %param.7) | copy-start | bytes 10756
  95.0 30.9 %all-to-all-start.2 = ((bf16[8,448,128]{2,1,0:T(8,128)(2,1)}), bf16[8,448,128]{2,1,0:T(8,128)(2,1)S(1)}, u32[]{:S(2)}, u32[]{:S(2)}) async-start(bf16[8,448,128]{2,1,0:T(8,128)(2,1)} %shard_map.70), calls=%async_computation.2 | async-start | bytes 1835008 | tf_op jit(solution)/shard_map/all_to_all | solution.py:22
  126.8 21.4 %all-to-all-start.3 = ((bf16[8,256,128]{2,1,0:T(8,128)(2,1)}), bf16[8,256,128]{2,1,0:T(8,128)(2,1)S(1)}, u32[]{:S(2)}, u32[]{:S(2)}) async-start(bf16[8,256,128]{2,1,0:T(8,128)(2,1)} %shard_map.71), calls=%async_computation.3 | async-start | bytes 1048576 | tf_op jit(solution)/shard_map/all_to_all | solution.py:22

commit v4 on v3

--- a/solution.py
+++ b/solution.py
@@ -11,11 +11,8 @@
 HD = 128
 HALF = HD // 2
 SHARE = QH // KVH
+SIDES = 2
 WINDOW = 5
-
-
-def copies_of(array, count):
-    return jnp.broadcast_to(array, (count, *array.shape))
 
 
 def exchanged(blocks, axis):
@@ -44,7 +41,7 @@
     return lax.broadcasted_iota(jnp.int32, shape, len(shape) - 1) < HALF
 
 
-def split(rank_ref, w_ref, keep_ref, give_ref):
+def split(rank_ref, w_ref, policy_ref, keep_ref, give_ref):
     key, val = w_ref[:, 5 * HD : 6 * HD], w_ref[:, 6 * HD :]
     low, high = w_ref[:, : 2 * HD], w_ref[:, 3 * HD : 5 * HD]
     left, right = w_ref[:, 2 * HD : 2 * HD + HALF], w_ref[:, 2 * HD + HALF : 3 * HD]
@@ -53,53 +50,57 @@
     @pl.when(odd == 0)
     def _():
         keep_ref[...] = jnp.concatenate([key, low, left], axis=1)
-        give_ref[...] = jnp.concatenate([right, val, high], axis=1)
+        give_ref[...] = jnp.concatenate([right, val, high, policy_ref[...]], axis=1)
 
     @pl.when(odd == 1)
     def _():
         keep_ref[...] = jnp.concatenate([val, high, right], axis=1)
-        give_ref[...] = jnp.concatenate([left, key, low], axis=1)
-
-
-def pack(keep_ref, got_ref, inner_ref, out_ref):
-    parts = [keep_ref[...], got_ref[...]] + [inner_ref[j] for j in range(inner_ref.shape[0])]
-    row = jnp.concatenate(parts, axis=1)
+        give_ref[...] = jnp.concatenate([left, key, low, policy_ref[...]], axis=1)
+
+
+def pack(keep_ref, got_ref, policy_ref, out_ref, pair_ref):
+    row = jnp.concatenate([keep_ref[...], got_ref[:, : 7 * HALF]], axis=1)
     for j in range(out_ref.shape[0]):
         out_ref[j] = row
-
-
-def arrange(in_ref, out_ref):
-    out_ref[0] = in_ref[...]
-
-
-def arranged(gathered, replicas, width):
-    rows = gathered.shape[0]
-    first = 7 * HD // width
+    pair_ref[0] = policy_ref[...]
+    pair_ref[1] = got_ref[:, 7 * HALF :]
+
+
+def arrange(place_ref, *refs):
+    *parts, out_ref, sem = refs
+    x, y, z = place_ref[0], place_ref[1], place_ref[2]
+    length, sides, replicas = len(parts), out_ref.shape[1], out_ref.shape[0]
+    copies = []
+    for k, part in enumerate(parts):
+        distance = k if k <= length // 2 else k - length
+        column = jnp.bitwise_and(x - distance, length - 1)
+        for side in range(sides):
+            for b in range(replicas):
+                place = out_ref.at[z ^ b, y ^ side, column]
+                copies.append(pltpu.make_async_copy(part.at[side, b], place, sem))
+    for copy in copies:
+        copy.start()
+    pltpu.make_async_copy(out_ref, out_ref, sem).wait()
+
+
+def arranged(place, parts):
+    sides, replicas, rows, width = parts[0].shape
+    hbm = pl.BlockSpec(memory_space=pl.ANY)
     return pl.pallas_call(
         arrange,
-        grid=(replicas,),
-        out_shape=jax.ShapeDtypeStruct((replicas, rows, width), gathered.dtype),
-        in_specs=[pl.BlockSpec((rows, width), lambda j: (0, first + j))],
-        out_specs=pl.BlockSpec((1, rows, width), lambda j: (j, 0, 0)),
-        compiler_params=pltpu.CompilerParams(vmem_limit_bytes=8 * 1024 * 1024),
-        cost_estimate=cost(0, 4 * replicas * rows * width),
-    )(gathered)
-
-
-def project(own_hbm, other_hbm, w_hbm, out_ref, own_ref, other_ref, w_ref, sems):
+        out_shape=jax.ShapeDtypeStruct((replicas, sides, len(parts), rows, width), parts[0].dtype),
+        in_specs=[pl.BlockSpec(memory_space=pltpu.SMEM)] + [hbm] * len(parts),
+        out_specs=hbm,
+        scratch_shapes=[pltpu.SemaphoreType.DMA],
+        compiler_params=pltpu.CompilerParams(vmem_limit_bytes=1024 * 1024),
+        cost_estimate=cost(0, 4 * len(parts) * parts[0].size),
+    )(place, *parts)
+
+
+def project(own_ref, low_ref, high_ref, w_ref, out_ref):
     blocks = out_ref.shape[0]
-    rows = own_hbm.shape[0]
+    rows = own_ref.shape[0]
     step = rows // 2
-    loads = [pltpu.make_async_copy(w_hbm.at[:, : 7 * HD], w_ref, sems.at[0])]
-    for part in range(2):
-        span = pl.ds(part * step, step)
-        loads.append(pltpu.make_async_copy(own_hbm.at[span], own_ref.at[span], sems.at[1 + 2 * part]))
-        loads.append(
-            pltpu.make_async_copy(other_hbm.at[span], other_ref.at[span], sems.at[2 + 2 * part])
-        )
-    for load in loads:
-        load.start()
-    loads[0].wait()
     shared = w_ref[:, 3 * HD : 4 * HD]
     w_own = w_ref[:, : 4 * HD]
     swapped = pltpu.roll(shared.astype(jnp.float32), HALF, 1).astype(jnp.bfloat16)
@@ -107,12 +108,10 @@
     size = rows // blocks
     low = lanes_below_half((size // 2, HD))
     for part in range(2):
-        loads[1 + 2 * part].wait()
-        loads[2 + 2 * part].wait()
         at = part * step
         value = jnp.dot(own_ref[at : at + step, :], w_own, preferred_element_type=jnp.float32)
         value = value + jnp.dot(
-            other_ref[at : at + step, :], w_other, preferred_element_type=jnp.float32
+            (low_ref, high_ref)[part][...], w_other, preferred_element_type=jnp.float32
         )
         for b in range(step // size):
             j = at // size + b
@@ -126,26 +125,6 @@
             out_ref[j, 3 * size :] = packed.astype(jnp.bfloat16)
 
 
-def projected(own, other, gathered, blocks):
-    rows, features = own.shape
-    vmem = pl.BlockSpec(memory_space=pltpu.VMEM)
-    hbm = pl.BlockSpec(memory_space=pltpu.HBM)
-    return pl.pallas_call(
-        project,
-        out_shape=jax.ShapeDtypeStruct((blocks, 7 * rows // blocks // 2, HD), jnp.bfloat16),
-        in_specs=[hbm, hbm, hbm],
-        out_specs=vmem,
-        scratch_shapes=[
-            pltpu.VMEM(own.shape, own.dtype),
-            pltpu.VMEM(own.shape, own.dtype),
-            pltpu.VMEM((features, 7 * HD), own.dtype),
-            pltpu.SemaphoreType.DMA((5,)),
-        ],
-        compiler_params=pltpu.CompilerParams(vmem_limit_bytes=62 * 1024 * 1024),
-        cost_estimate=cost(4 * rows * features * 4 * HD, 4 * own.size + 2 * gathered.size),
-    )(own, other, gathered)
-
-
 def turned(value, cosine, sine):
     return value * cosine + pltpu.roll(value, HALF, 1) * sine
 
@@ -157,7 +136,8 @@
     return value
 
 
-def keys_and_values(part_ref, bias_ref, cos_ref, sin_ref, out_ref):
+def keys_and_values(part_ref, bias_ref, cos_ref, sin_ref, *rest):
+    out_ref = rest[-1]
     size = out_ref.shape[1] // 2
     rows = slice(0, size)
     key = added(part_ref, 0, rows) + bias_ref[SHARE : SHARE + 1]
@@ -222,20 +202,40 @@
     rows, features = tokens.shape
     mine = rows // replicas
     rank = lax.axis_index("rep")
-    swap = [(i, i ^ 1) for i in range(replicas)]
     bf16, f32 = jnp.bfloat16, jnp.float32
-
-    own_features = ref_qkv.shape[0]
+    length = shards // SIDES
+    shard = lax.axis_index("fsdp")
+
+    def swapped(value, axis, bit):
+        pairs = [(i, i ^ bit) for i in range(lax.axis_size(axis))]
+        return lax.ppermute(value, axis, pairs)
+
+    def passed(value, by):
+        pairs = [(i, i // length * length + (i + by) % length) for i in range(shards)]
+        return lax.ppermute(value, "fsdp", pairs)
+
+    own_features, width = policy_key.shape
     half = jax.ShapeDtypeStruct((own_features, 7 * HALF), bf16)
-    keep, give = call(split, (half, half), 0, rank.reshape(1), ref_qkv, scalars=1)
-    got = lax.ppermute(give, "rep", swap)
-    other = lax.ppermute(tokens, "rep", swap)
-    width = policy_key.shape[1]
-    inner = exchanged(copies_of(policy_key, replicas), "rep")
-    packed = jax.ShapeDtypeStruct((shards, own_features, 7 * HD + replicas * width), bf16)
-    packed = call(pack, (packed,), 0, keep, got, inner)
-    gathered = exchanged(packed, "fsdp").reshape(features, -1)
-    whole = arranged(gathered, replicas, width).reshape(-1, width)
+    more = jax.ShapeDtypeStruct((own_features, 7 * HALF + width), bf16)
+    keep, give = call(split, (half, more), 0, rank.reshape(1), ref_qkv, policy_key, scalars=1)
+    got = swapped(give, "rep", 1)
+    low = swapped(tokens[: rows // 2], "rep", 1)
+    copies = jax.ShapeDtypeStruct((shards, own_features, 7 * HD), bf16)
+    pair = jax.ShapeDtypeStruct((2, own_features, width), bf16)
+    copies, pair = call(pack, (copies, pair), 0, keep, got, policy_key)
+    column = pair
+    for bit in range(1, replicas.bit_length() - 1):
+        column = jnp.concatenate([column, swapped(column, "rep", 1 << bit)])
+    gathered = exchanged(copies, "fsdp").reshape(features, -1)
+    high = swapped(tokens[rows // 2 :], "rep", 1)
+    both = jnp.stack([column, swapped(column, "fsdp", length)])
+    up, down = [both], [both]
+    for k in range(1, length // 2 + 1):
+        up.append(passed(up[-1], 1))
+        if k < length // 2 or length == 1:
+            down.append(passed(down[-1], -1))
+    place = jnp.stack([shard % length, shard // length, rank]).astype(jnp.int32)
+    whole = arranged(place, up + down[:0:-1]).reshape(-1, width)
 
     seg = segment_ids[0]
     start = rank * mine
@@ -249,7 +249,8 @@
     sine = jnp.concatenate([-sine, sine], axis=1)
     bias = ref_bias.reshape(SHARE + 2, HD)
 
-    part = projected(tokens, other, gathered, replicas)
+    part = jax.ShapeDtypeStruct((replicas, 7 * mine // 2, HD), bf16)
+    part = call(project, (part,), 4 * rows * features * 4 * HD, tokens, low, high, gathered)
     part = exchanged(part, "rep")
     my_kv = call(
         keys_and_values,

time: 152 us -> 152 us (level)
  the two profiles are of different devices: /device:TPU:89 before, /device:TPU:40 now
where the time goes in v4:
time: 152 us; the launch traced here: 151 us
  starting transfers between devices  79.4 us (52%)
  waiting for transfers between devices  53.7 us (35%)
  local copies, waits for them, and re-layouts  8.45 us (6%)
  Pallas kernels  7.57 us (5%)
    ppermute x6, waiting for transfers between devices, swapped(): return lax.ppermute(value, axis, pairs)  41.3 us
    ppermute x6, starting transfers between devices, swapped(): return lax.ppermute(value, axis, pairs)  28.5 us
    all_to_all x3, starting transfers between devices, exchanged(): return lax.all_to_all(blocks, axis, split_axis=0, concat_axis=0, tiled=True)  27.1 us
    ppermute x7, starting transfers between devices, passed(): return lax.ppermute(value, 'fsdp', pairs)  23.7 us
    ppermute x7, waiting for transfers between devices, passed(): return lax.ppermute(value, 'fsdp', pairs)  12.4 us
    unnamed x26, local copies, waits for them, and re-layouts  8.2 us
    pallas_call x5, Pallas kernels, call(): pl.pallas_call(kernel, out_shape=outs if len(outs) > 1 else outs[0], in_s...  5.95 us
  transfers between devices with their start and end apart: 16, of which 10 were waited for; matrix products, arithmetic and copies ran while one was open for 1% of the time, Pallas kernels for 2%

profile of v4, /device:TPU:40, one launch (start us, length us, event | category | flops | bytes accessed | tf_op | source)
XLA Modules:
  0.0 150.7 jit_solution(10068813969374442461)
XLA Ops:
  0.6 0.0 copy-start
  0.6 0.0 copy-start.3
  0.7 1.0 copy-done.3
  1.6 0.0 copy-start.4
  1.6 0.7 copy-done.4
  2.3 0.1 shard_map.68
  2.4 5.2 %collective-permute-start.2 = (bf16[40,576]{1,0:T(8,128)(2,1)S(1)}, bf16[40,576]{1,0:T(8,128)(2,1)S(1)}, u32[]{:S(2)}, u32[]{:S(2)}) collective-permute-start(bf16[40,576]{1,0:T(8,128)(2,1)S(1)} %get-tuple-element.7), channel_id=1, source_target_pairs={{0,1},{1,0},{2,3},{3,2},{4,5},{5,4},{6,7},{7,6},{8,9},{9,8},{10,11... | collective-permute-start | bytes 138248 | tf_op jit(solution)/shard_map/ppermute | solution.py:211
  7.6 2.1 %collective-permute-done.2.got_ref = bf16[40,576]{1,0:T(8,128)(2,1)S(1)} collective-permute-done((bf16[40,576]{1,0:T(8,128)(2,1)S(1)}, bf16[40,576]{1,0:T(8,128)(2,1)S(1)}, u32[]{:S(2)}, u32[]{:S(2)}) %collective-permute-start.2) | collective-permute-done | bytes 46112 | tf_op jit(solution)/shard_map/ppermute | solution.py:211
  9.7 0.0 copy-start.5
  9.7 0.7 copy-done.5
  10.4 0.1 shard_map.69
  10.5 0.0 copy-start.1
  10.6 1.0 copy-done.1
  11.6 8.3 %all-to-all-start = ((bf16[16,40,896]{2,1,0:T(8,128)(2,1)}), bf16[16,40,896]{2,1,0:T(8,128)(2,1)S(1)}, u32[]{:S(2)}, u32[]{:S(2)}) async-start(bf16[16,40,896]{2,1,0:T(8,128)(2,1)} %copy-done.1), calls=%async_computation | async-start | bytes 2293760 | tf_op jit(solution)/shard_map/all_to_all | solution.py:19
  19.9 0.0 copy-done
  19.9 0.1 fusion.3
  20.0 3.9 %collective-permute-start = (bf16[512,640]{1,0:T(8,128)(2,1)S(1)}, bf16[512,640]{1,0:T(8,128)(2,1)S(1)}, u32[]{:S(2)}, u32[]{:S(2)}) collective-permute-start(bf16[512,640]{1,0:T(8,128)(2,1)S(1)} %get-tuple-element.11), channel_id=1, source_target_pairs={{0,1},{1,0},{2,3},{3,2},{4,5},{5,4},{6,7},{7,6},{8,9},{9,8},{10,11... | collective-permute-start | bytes 1966088 | tf_op jit(solution)/shard_map/ppermute | solution.py:211
  24.0 1.9 %collective-permute-start.1 = (bf16[512,640]{1,0:T(8,128)(2,1)S(1)}, bf16[512,640]{1,0:T(8,128)(2,1)S(1)}, u32[]{:S(2)}, u32[]{:S(2)}) collective-permute-start(bf16[512,640]{1,0:T(8,128)(2,1)S(1)} %get-tuple-element.10), channel_id=1, source_target_pairs={{0,1},{1,0},{2,3},{3,2},{4,5},{5,4},{6,7},{7,6},{8,9},{9,8},{10,11... | collective-permute-start | bytes 1966088 | tf_op jit(solution)/shard_map/ppermute | solution.py:211
  25.9 13.6 %collective-permute-done.low_ref = bf16[512,640]{1,0:T(8,128)(2,1)S(1)} collective-permute-done((bf16[512,640]{1,0:T(8,128)(2,1)S(1)}, bf16[512,640]{1,0:T(8,128)(2,1)S(1)}, u32[]{:S(2)}, u32[]{:S(2)}) %collective-permute-start) | collective-permute-done | bytes 655392 | tf_op jit(solution)/shard_map/ppermute | solution.py:211
  39.5 0.0 copy-start.8
  39.5 0.8 copy-done.8
  40.4 10.7 %collective-permute-done.1.high_ref = bf16[512,640]{1,0:T(8,128)(2,1)S(1)} collective-permute-done((bf16[512,640]{1,0:T(8,128)(2,1)S(1)}, bf16[512,640]{1,0:T(8,128)(2,1)S(1)}, u32[]{:S(2)}, u32[]{:S(2)}) %collective-permute-start.1) | collective-permute-done | bytes 655392 | tf_op jit(solution)/shard_map/ppermute | solution.py:211
  51.0 0.0 copy-start.10
  51.0 0.9 copy-done.10
  51.9 0.0 all-to-all-done
  51.9 1.1 copy-done.9
  53.0 1.1 copy-done.11
  54.1 1.9 %shard_map.70 = bf16[8,448,128]{2,1,0:T(8,128)(2,1)S(1)} custom-call(bf16[1024,640]{1,0:T(8,128)(2,1)S(1)} %copy-done, bf16[512,640]{1,0:T(8,128)(2,1)S(1)} %copy-done.9, bf16[512,640]{1,0:T(8,128)(2,1)S(1)} %copy-done.11, bf16[640,896]{1,0:T(8,128)(2,1)S(1)} %bitcast.14), custom_call_target="tpu_custom_call" | custom-call | flops 1342177280 | bytes 4685824 | tf_op jit(solution)/shard_map/pallas_call | solution.py:30
  56.0 0.0 copy-start.2
  56.0 0.9 copy-done.2
  56.9 15.3 %all-to-all-start.1 = ((bf16[8,448,128]{2,1,0:T(8,128)(2,1)}), bf16[8,448,128]{2,1,0:T(8,128)(2,1)S(1)}, u32[]{:S(2)}, u32[]{:S(2)}) async-start(bf16[8,448,128]{2,1,0:T(8,128)(2,1)} %copy-done.2), calls=%async_computation.1 | async-start | bytes 1835008 | tf_op jit(solution)/shard_map/all_to_all | solution.py:19
  72.2 0.0 copy-done.6
  72.2 0.2 convert_reduce_fusion
  72.4 0.3 fusion
  72.7 0.1 pad_maximum_fusion.1
  72.9 4.8 %collective-permute-start.3 = (bf16[2,40,128]{2,1,0:T(8,128)(2,1)S(1)}, bf16[2,40,128]{2,1,0:T(8,128)(2,1)S(1)}, u32[]{:S(2)}, u32[]{:S(2)}) collective-permute-start(bf16[2,40,128]{2,1,0:T(8,128)(2,1)S(1)} %get-tuple-element.9), channel_id=1, source_target_pairs={{0,2},{1,3},{2,0},{3,1},{4,6},{5,7},{6,4},{7,5},{8,10},{9,11},{10,... | collective-permute-start | bytes 61448 | tf_op jit(solution)/shard_map/ppermute | solution.py:211
  77.7 12.0 %collective-permute-done.3 = bf16[2,40,128]{2,1,0:T(8,128)(2,1)S(1)} collective-permute-done((bf16[2,40,128]{2,1,0:T(8,128)(2,1)S(1)}, bf16[2,40,128]{2,1,0:T(8,128)(2,1)S(1)}, u32[]{:S(2)}, u32[]{:S(2)}) %collective-permute-start.3) | collective-permute-done | bytes 20512 | tf_op jit(solution)/shard_map/ppermute | solution.py:211
  89.7 9.3 %collective-permute-start.4 = (bf16[4,40,128]{2,1,0:T(8,128)(2,1)S(1)}, bf16[4,40,128]{2,1,0:T(8,128)(2,1)S(1)}, u32[]{:S(2)}, u32[]{:S(2)}) collective-permute-start(bf16[4,40,128]{2,1,0:T(8,128)(2,1)S(1)} %pad_maximum_fusion.3), channel_id=1, source_target_pairs={{0,4},{1,5},{2,6},{3,7},{4,0},{5,1},{6,2},{7,3},{8,12},{9,13},{10,... | collective-permute-start | bytes 122888 | tf_op jit(solution)/shard_map/ppermute | solution.py:211
  99.0 0.0 all-to-all-done.1.part_ref
  99.0 0.0 copy-done.7
  99.0 0.9 shard_map.71
  99.9 3.5 %all-to-all-start.2 = ((bf16[8,256,128]{2,1,0:T(8,128)(2,1)}), bf16[8,256,128]{2,1,0:T(8,128)(2,1)S(1)}, u32[]{:S(2)}, u32[]{:S(2)}) async-start(bf16[8,256,128]{2,1,0:T(8,128)(2,1)} %shard_map.71), calls=%async_computation.2 | async-start | bytes 1048576 | tf_op jit(solution)/shard_map/all_to_all | solution.py:19
  103.4 0.0 collective-permute-done.4
  103.4 3.4 %collective-permute-start.5 = (bf16[8,40,128]{2,1,0:T(8,128)(2,1)S(1)}, bf16[8,40,128]{2,1,0:T(8,128)(2,1)S(1)}, u32[]{:S(2)}, u32[]{:S(2)}) collective-permute-start(bf16[8,40,128]{2,1,0:T(8,128)(2,1)S(1)} %constant_dynamic-update-slice_fusion), channel_id=1, source_target_pairs={{0,512},{64,576},{128,640},{192,704},{256,768},{320,832},{384,896}... | collective-permute-start | bytes 245768 | tf_op jit(solution)/shard_map/ppermute | solution.py:211
  106.8 3.0 %collective-permute-done.5 = bf16[8,40,128]{2,1,0:T(8,128)(2,1)S(1)} collective-permute-done((bf16[8,40,128]{2,1,0:T(8,128)(2,1)S(1)}, bf16[8,40,128]{2,1,0:T(8,128)(2,1)S(1)}, u32[]{:S(2)}, u32[]{:S(2)}) %collective-permute-start.5) | collective-permute-done | bytes 81952 | tf_op jit(solution)/shard_map/ppermute | solution.py:211
  109.8 2.5 %collective-permute-start.6 = (bf16[2,8,40,128]{3,2,1,0:T(8,128)(2,1)S(1)}, bf16[2,8,40,128]{3,2,1,0:T(8,128)(2,1)S(1)}, u32[]{:S(2)}, u32[]{:S(2)}) collective-permute-start(bf16[2,8,40,128]{3,2,1,0:T(8,128)(2,1)S(1)} %pad_maximum_fusion.refs_0_), channel_id=1, source_target_pairs={{0,64},{64,128},{128,192},{192,256},{256,320},{320,384},{384,448},... | collective-permute-start | bytes 491528 | tf_op jit(solution)/shard_map/ppermute | solution.py:215
  112.2 4.6 %collective-permute-start.10 = (bf16[2,8,40,128]{3,2,1,0:T(8,128)(2,1)S(1)}, bf16[2,8,40,128]{3,2,1,0:T(8,128)(2,1)S(1)}, u32[]{:S(2)}, u32[]{:S(2)}) collective-permute-start(bf16[2,8,40,128]{3,2,1,0:T(8,128)(2,1)S(1)} %pad_maximum_fusion.refs_0_), channel_id=1, source_target_pairs={{0,448},{64,0},{128,64},{192,128},{256,192},{320,256},{384,320},{4... | collective-permute-start | bytes 491528 | tf_op jit(solution)/shard_map/ppermute | solution.py:215
  116.8 1.7 %collective-permute-done.6.refs_1_ = bf16[2,8,40,128]{3,2,1,0:T(8,128)(2,1)S(1)} collective-permute-done((bf16[2,8,40,128]{3,2,1,0:T(8,128)(2,1)S(1)}, bf16[2,8,40,128]{3,2,1,0:T(8,128)(2,1)S(1)}, u32[]{:S(2)}, u32[]{:S(2)}) %collective-permute-start.6) | collective-permute-done | bytes 163872 | tf_op jit(solution)/shard_map/ppermute | solution.py:215
  118.5 1.9 %collective-permute-start.7 = (bf16[2,8,40,128]{3,2,1,0:T(8,128)(2,1)S(1)}, bf16[2,8,40,128]{3,2,1,0:T(8,128)(2,1)S(1)}, u32[]{:S(2)}, u32[]{:S(2)}) collective-permute-start(bf16[2,8,40,128]{3,2,1,0:T(8,128)(2,1)S(1)} %collective-permute-done.6.refs_1_), channel_id=1, source_target_pairs={{0,64},{64,128},{128,192},{192,256},{256,320},{320,384},{384,448},... | collective-permute-start | bytes 491528 | tf_op jit(solution)/shard_map/ppermute | solution.py:215
  120.5 0.0 collective-permute-done.10.refs_7_
  120.5 5.4 %collective-permute-start.11 = (bf16[2,8,40,128]{3,2,1,0:T(8,128)(2,1)S(1)}, bf16[2,8,40,128]{3,2,1,0:T(8,128)(2,1)S(1)}, u32[]{:S(2)}, u32[]{:S(2)}) collective-permute-start(bf16[2,8,40,128]{3,2,1,0:T(8,128)(2,1)S(1)} %collective-permute-done.10.refs_7_), channel_id=1, source_target_pairs={{0,448},{64,0},{128,64},{192,128},{256,192},{320,256},{384,320},{4... | collective-permute-start | bytes 491528 | tf_op jit(solution)/shard_map/ppermute | solution.py:215
  125.9 2.6 %collective-permute-done.7.refs_2_ = bf16[2,8,40,128]{3,2,1,0:T(8,128)(2,1)S(1)} collective-permute-done((bf16[2,8,40,128]{3,2,1,0:T(8,128)(2,1)S(1)}, bf16[2,8,40,128]{3,2,1,0:T(8,128)(2,1)S(1)}, u32[]{:S(2)}, u32[]{:S(2)}) %collective-permute-start.7) | collective-permute-done | bytes 163872 | tf_op jit(solution)/shard_map/ppermute | solution.py:215
  128.5 1.9 %collective-permute-start.8 = (bf16[2,8,40,128]{3,2,1,0:T(8,128)(2,1)S(1)}, bf16[2,8,40,128]{3,2,1,0:T(8,128)(2,1)S(1)}, u32[]{:S(2)}, u32[]{:S(2)}) collective-permute-start(bf16[2,8,40,128]{3,2,1,0:T(8,128)(2,1)S(1)} %collective-permute-done.7.refs_2_), channel_id=1, source_target_pairs={{0,64},{64,128},{128,192},{192,256},{256,320},{320,384},{384,448},... | collective-permute-start | bytes 491528 | tf_op jit(solution)/shard_map/ppermute | solution.py:215
  130.4 0.1 collective-permute-done.11.refs_6_
  130.4 5.6 %collective-permute-start.12 = (bf16[2,8,40,128]{3,2,1,0:T(8,128)(2,1)S(1)}, bf16[2,8,40,128]{3,2,1,0:T(8,128)(2,1)S(1)}, u32[]{:S(2)}, u32[]{:S(2)}) collective-permute-start(bf16[2,8,40,128]{3,2,1,0:T(8,128)(2,1)S(1)} %collective-permute-done.11.refs_6_), channel_id=1, source_target_pairs={{0,448},{64,0},{128,64},{192,128},{256,192},{320,256},{384,320},{4... | collective-permute-start | bytes 491528 | tf_op jit(solution)/shard_map/ppermute | solution.py:215
  136.0 1.8 %collective-permute-done.8.refs_3_ = bf16[2,8,40,128]{3,2,1,0:T(8,128)(2,1)S(1)} collective-permute-done((bf16[2,8,40,128]{3,2,1,0:T(8,128)(2,1)S(1)}, bf16[2,8,40,128]{3,2,1,0:T(8,128)(2,1)S(1)}, u32[]{:S(2)}, u32[]{:S(2)}) %collective-permute-start.8) | collective-permute-done | bytes 163872 | tf_op jit(solution)/shard_map/ppermute | solution.py:215
  137.8 1.9 %collective-permute-start.9 = (bf16[2,8,40,128]{3,2,1,0:T(8,128)(2,1)S(1)}, bf16[2,8,40,128]{3,2,1,0:T(8,128)(2,1)S(1)}, u32[]{:S(2)}, u32[]{:S(2)}) collective-permute-start(bf16[2,8,40,128]{3,2,1,0:T(8,128)(2,1)S(1)} %collective-permute-done.8.refs_3_), channel_id=1, source_target_pairs={{0,64},{64,128},{128,192},{192,256},{256,320},{320,384},{384,448},... | collective-permute-start | bytes 491528 | tf_op jit(solution)/shard_map/ppermute | solution.py:215
  139.7 0.1 copy.8.mine_ref
  139.8 0.1 pad_add_fusion.place_ref
  139.9 0.0 collective-permute-done.12.refs_5_
  139.9 6.3 %collective-permute-done.9.refs_4_ = bf16[2,8,40,128]{3,2,1,0:T(8,128)(2,1)S(1)} collective-permute-done((bf16[2,8,40,128]{3,2,1,0:T(8,128)(2,1)S(1)}, bf16[2,8,40,128]{3,2,1,0:T(8,128)(2,1)S(1)}, u32[]{:S(2)}, u32[]{:S(2)}) %collective-permute-start.9) | collective-permute-done | bytes 163872 | tf_op jit(solution)/shard_map/ppermute | solution.py:215
  146.2 1.6 %shard_map.73 = bf16[8,2,8,40,128]{4,3,2,1,0:T(8,128)(2,1)} custom-call(s32[3]{0:T(128)S(1)} %pad_add_fusion.place_ref, bf16[2,8,40,128]{3,2,1,0:T(8,128)(2,1)S(1)} %pad_maximum_fusion.refs_0_, bf16[2,8,40,128]{3,2,1,0:T(8,128)(2,1)S(1)} %collective-permute-done.6.refs_1_, bf16[2,8,40,128]{3,2,1,0:T(8,128)(2,1)S(1)} %collective-permute-done.7.refs_2_, ...), custom_call_target="tpu_custom_call" | custom-call | bytes 2621440 | tf_op jit(solution)/shard_map/pallas_call | solution.py:89
  147.8 0.0 all-to-all-done.2.kv_ref
  147.8 2.9 %shard_map.72 = bf16[128,640]{1,0:T(8,128)(2,1)} custom-call(s32[1]{0:T(128)} %bitcast.rank_ref, bf16[8,448,128]{2,1,0:T(8,128)(2,1)S(1)} %all-to-all-done.1.part_ref, bf16[8,256,128]{2,1,0:T(8,128)(2,1)S(1)} %all-to-all-done.2.kv_ref, f32[7,128]{1,0:T(8,128)S(1)} %bitcast.18, f32[128,128]{1,0:T(8,128)S(1)} %get-tuple-element.17.cos_ref, ...), custom_call_target="tpu_custom_call" | custom-call | flops 209715200 | bytes 1744900 | tf_op jit(solution)/shard_map/pallas_call | solution.py:30
  (12 shorter events, 0.1 us)
Async XLA Ops:
  0.6 19.3 %copy-start = (bf16[1024,640]{1,0:T(8,128)(2,1)S(1)}, bf16[1024,640]{1,0:T(8,128)(2,1)}, u32[]{:S(2)}) copy-start(bf16[1024,640]{1,0:T(8,128)(2,1)} %own_ref.1) | copy-start | bytes 3932164
  0.6 1.0 copy-start.3
  1.6 0.7 copy-start.4
  2.4 7.3 %collective-permute-start.2 = (bf16[40,576]{1,0:T(8,128)(2,1)S(1)}, bf16[40,576]{1,0:T(8,128)(2,1)S(1)}, u32[]{:S(2)}, u32[]{:S(2)}) collective-permute-start(bf16[40,576]{1,0:T(8,128)(2,1)S(1)} %get-tuple-element.7), channel_id=1, source_target_pairs={{0,1},{1,0},{2,3},{3,2},{4,5},{5,4},{6,7},{7,6},{8,9},{9,8},{10,11... | collective-permute-start | bytes 138248 | tf_op jit(solution)/shard_map/ppermute | solution.py:211
  9.7 0.7 copy-start.5
  10.5 1.0 copy-start.1
  11.6 40.3 %all-to-all-start = ((bf16[16,40,896]{2,1,0:T(8,128)(2,1)}), bf16[16,40,896]{2,1,0:T(8,128)(2,1)S(1)}, u32[]{:S(2)}, u32[]{:S(2)}) async-start(bf16[16,40,896]{2,1,0:T(8,128)(2,1)} %copy-done.1), calls=%async_computation | async-start | bytes 2293760 | tf_op jit(solution)/shard_map/all_to_all | solution.py:19
  20.0 19.5 %collective-permute-start = (bf16[512,640]{1,0:T(8,128)(2,1)S(1)}, bf16[512,640]{1,0:T(8,128)(2,1)S(1)}, u32[]{:S(2)}, u32[]{:S(2)}) collective-permute-start(bf16[512,640]{1,0:T(8,128)(2,1)S(1)} %get-tuple-element.11), channel_id=1, source_target_pairs={{0,1},{1,0},{2,3},{3,2},{4,5},{5,4},{6,7},{7,6},{8,9},{9,8},{10,11... | collective-permute-start | bytes 1966088 | tf_op jit(solution)/shard_map/ppermute | solution.py:211
  24.0 27.1 %collective-permute-start.1 = (bf16[512,640]{1,0:T(8,128)(2,1)S(1)}, bf16[512,640]{1,0:T(8,128)(2,1)S(1)}, u32[]{:S(2)}, u32[]{:S(2)}) collective-permute-start(bf16[512,640]{1,0:T(8,128)(2,1)S(1)} %get-tuple-element.10), channel_id=1, source_target_pairs={{0,1},{1,0},{2,3},{3,2},{4,5},{5,4},{6,7},{7,6},{8,9},{9,8},{10,11... | collective-permute-start | bytes 1966088 | tf_op jit(solution)/shard_map/ppermute | solution.py:211
  39.5 0.8 copy-start.8
  51.0 0.9 copy-start.10
  51.9 1.1 copy-start.9
  53.0 1.1 copy-start.11
  56.0 0.9 copy-start.2
  56.9 15.3 %copy-start.6 = (s32[1,1024]{1,0:T(1,128)S(1)}, s32[1,1024]{1,0:T(1,128)}, u32[]{:S(2)}) copy-start(s32[1,1024]{1,0:T(1,128)} %param.8) | copy-start | bytes 12292
  56.9 42.1 %copy-start.7 = (f32[896]{0:T(1024)S(1)}, f32[896]{0:T(1024)}, u32[]{:S(2)}) copy-start(f32[896]{0:T(1024)} %param.7) | copy-start | bytes 10756
  56.9 42.0 %all-to-all-start.1 = ((bf16[8,448,128]{2,1,0:T(8,128)(2,1)}), bf16[8,448,128]{2,1,0:T(8,128)(2,1)S(1)}, u32[]{:S(2)}, u32[]{:S(2)}) async-start(bf16[8,448,128]{2,1,0:T(8,128)(2,1)} %copy-done.2), calls=%async_computation.1 | async-start | bytes 1835008 | tf_op jit(solution)/shard_map/all_to_all | solution.py:19
  72.9 16.8 %collective-permute-start.3 = (bf16[2,40,128]{2,1,0:T(8,128)(2,1)S(1)}, bf16[2,40,128]{2,1,0:T(8,128)(2,1)S(1)}, u32[]{:S(2)}, u32[]{:S(2)}) collective-permute-start(bf16[2,40,128]{2,1,0:T(8,128)(2,1)S(1)} %get-tuple-element.9), channel_id=1, source_target_pairs={{0,2},{1,3},{2,0},{3,1},{4,6},{5,7},{6,4},{7,5},{8,10},{9,11},{10,... | collective-permute-start | bytes 61448 | tf_op jit(solution)/shard_map/ppermute | solution.py:211
  89.7 13.7 %collective-permute-start.4 = (bf16[4,40,128]{2,1,0:T(8,128)(2,1)S(1)}, bf16[4,40,128]{2,1,0:T(8,128)(2,1)S(1)}, u32[]{:S(2)}, u32[]{:S(2)}) collective-permute-start(bf16[4,40,128]{2,1,0:T(8,128)(2,1)S(1)} %pad_maximum_fusion.3), channel_id=1, source_target_pairs={{0,4},{1,5},{2,6},{3,7},{4,0},{5,1},{6,2},{7,3},{8,12},{9,13},{10,... | collective-permute-start | bytes 122888 | tf_op jit(solution)/shard_map/ppermute | solution.py:211
  99.9 48.0 %all-to-all-start.2 = ((bf16[8,256,128]{2,1,0:T(8,128)(2,1)}), bf16[8,256,128]{2,1,0:T(8,128)(2,1)S(1)}, u32[]{:S(2)}, u32[]{:S(2)}) async-start(bf16[8,256,128]{2,1,0:T(8,128)(2,1)} %shard_map.71), calls=%async_computation.2 | async-start | bytes 1048576 | tf_op jit(solution)/shard_map/all_to_all | solution.py:19
  103.4 6.3 %collective-permute-start.5 = (bf16[8,40,128]{2,1,0:T(8,128)(2,1)S(1)}, bf16[8,40,128]{2,1,0:T(8,128)(2,1)S(1)}, u32[]{:S(2)}, u32[]{:S(2)}) collective-permute-start(bf16[8,40,128]{2,1,0:T(8,128)(2,1)S(1)} %constant_dynamic-update-slice_fusion), channel_id=1, source_target_pairs={{0,512},{64,576},{128,640},{192,704},{256,768},{320,832},{384,896}... | collective-permute-start | bytes 245768 | tf_op jit(solution)/shard_map/ppermute | solution.py:211
  109.8 8.8 %collective-permute-start.6 = (bf16[2,8,40,128]{3,2,1,0:T(8,128)(2,1)S(1)}, bf16[2,8,40,128]{3,2,1,0:T(8,128)(2,1)S(1)}, u32[]{:S(2)}, u32[]{:S(2)}) collective-permute-start(bf16[2,8,40,128]{3,2,1,0:T(8,128)(2,1)S(1)} %pad_maximum_fusion.refs_0_), channel_id=1, source_target_pairs={{0,64},{64,128},{128,192},{192,256},{256,320},{320,384},{384,448},... | collective-permute-start | bytes 491528 | tf_op jit(solution)/shard_map/ppermute | solution.py:215
  112.2 8.2 %collective-permute-start.10 = (bf16[2,8,40,128]{3,2,1,0:T(8,128)(2,1)S(1)}, bf16[2,8,40,128]{3,2,1,0:T(8,128)(2,1)S(1)}, u32[]{:S(2)}, u32[]{:S(2)}) collective-permute-start(bf16[2,8,40,128]{3,2,1,0:T(8,128)(2,1)S(1)} %pad_maximum_fusion.refs_0_), channel_id=1, source_target_pairs={{0,448},{64,0},{128,64},{192,128},{256,192},{320,256},{384,320},{4... | collective-permute-start | bytes 491528 | tf_op jit(solution)/shard_map/ppermute | solution.py:215
  118.5 9.9 %collective-permute-start.7 = (bf16[2,8,40,128]{3,2,1,0:T(8,128)(2,1)S(1)}, bf16[2,8,40,128]{3,2,1,0:T(8,128)(2,1)S(1)}, u32[]{:S(2)}, u32[]{:S(2)}) collective-permute-start(bf16[2,8,40,128]{3,2,1,0:T(8,128)(2,1)S(1)} %collective-permute-done.6.refs_1_), channel_id=1, source_target_pairs={{0,64},{64,128},{128,192},{192,256},{256,320},{320,384},{384,448},... | collective-permute-start | bytes 491528 | tf_op jit(solution)/shard_map/ppermute | solution.py:215
  120.5 10.0 %collective-permute-start.11 = (bf16[2,8,40,128]{3,2,1,0:T(8,128)(2,1)S(1)}, bf16[2,8,40,128]{3,2,1,0:T(8,128)(2,1)S(1)}, u32[]{:S(2)}, u32[]{:S(2)}) collective-permute-start(bf16[2,8,40,128]{3,2,1,0:T(8,128)(2,1)S(1)} %collective-permute-done.10.refs_7_), channel_id=1, source_target_pairs={{0,448},{64,0},{128,64},{192,128},{256,192},{320,256},{384,320},{4... | collective-permute-start | bytes 491528 | tf_op jit(solution)/shard_map/ppermute | solution.py:215
  128.5 9.3 %collective-permute-start.8 = (bf16[2,8,40,128]{3,2,1,0:T(8,128)(2,1)S(1)}, bf16[2,8,40,128]{3,2,1,0:T(8,128)(2,1)S(1)}, u32[]{:S(2)}, u32[]{:S(2)}) collective-permute-start(bf16[2,8,40,128]{3,2,1,0:T(8,128)(2,1)S(1)} %collective-permute-done.7.refs_2_), channel_id=1, source_target_pairs={{0,64},{64,128},{128,192},{192,256},{256,320},{320,384},{384,448},... | collective-permute-start | bytes 491528 | tf_op jit(solution)/shard_map/ppermute | solution.py:215
  130.4 9.5 %collective-permute-start.12 = (bf16[2,8,40,128]{3,2,1,0:T(8,128)(2,1)S(1)}, bf16[2,8,40,128]{3,2,1,0:T(8,128)(2,1)S(1)}, u32[]{:S(2)}, u32[]{:S(2)}) collective-permute-start(bf16[2,8,40,128]{3,2,1,0:T(8,128)(2,1)S(1)} %collective-permute-done.11.refs_6_), channel_id=1, source_target_pairs={{0,448},{64,0},{128,64},{192,128},{256,192},{320,256},{384,320},{4... | collective-permute-start | bytes 491528 | tf_op jit(solution)/shard_map/ppermute | solution.py:215
  137.8 8.4 %collective-permute-start.9 = (bf16[2,8,40,128]{3,2,1,0:T(8,128)(2,1)S(1)}, bf16[2,8,40,128]{3,2,1,0:T(8,128)(2,1)S(1)}, u32[]{:S(2)}, u32[]{:S(2)}) collective-permute-start(bf16[2,8,40,128]{3,2,1,0:T(8,128)(2,1)S(1)} %collective-permute-done.8.refs_3_), channel_id=1, source_target_pairs={{0,64},{64,128},{128,192},{192,256},{256,320},{320,384},{384,448},... | collective-permute-start | bytes 491528 | tf_op jit(solution)/shard_map/ppermute | solution.py:215

commit v5 on v4

--- a/solution.py
+++ b/solution.py
@@ -41,7 +41,15 @@
     return lax.broadcasted_iota(jnp.int32, shape, len(shape) - 1) < HALF
 
 
-def split(rank_ref, w_ref, policy_ref, keep_ref, give_ref):
+def split(rank_ref, w_hbm, policy_hbm, keep_ref, give_ref, w_ref, policy_ref, sems):
+    loads = [
+        pltpu.make_async_copy(w_hbm, w_ref, sems.at[0]),
+        pltpu.make_async_copy(policy_hbm, policy_ref, sems.at[1]),
+    ]
+    for load in loads:
+        load.start()
+    for load in loads:
+        load.wait()
     key, val = w_ref[:, 5 * HD : 6 * HD], w_ref[:, 6 * HD :]
     low, high = w_ref[:, : 2 * HD], w_ref[:, 3 * HD : 5 * HD]
     left, right = w_ref[:, 2 * HD : 2 * HD + HALF], w_ref[:, 2 * HD + HALF : 3 * HD]
@@ -49,20 +57,39 @@
 
     @pl.when(odd == 0)
     def _():
-        keep_ref[...] = jnp.concatenate([key, low, left], axis=1)
+        keep_ref[...] = jnp.concatenate([key, low, left, policy_ref[...]], axis=1)
         give_ref[...] = jnp.concatenate([right, val, high, policy_ref[...]], axis=1)
 
     @pl.when(odd == 1)
     def _():
-        keep_ref[...] = jnp.concatenate([val, high, right], axis=1)
+        keep_ref[...] = jnp.concatenate([val, high, right, policy_ref[...]], axis=1)
         give_ref[...] = jnp.concatenate([left, key, low, policy_ref[...]], axis=1)
 
 
-def pack(keep_ref, got_ref, policy_ref, out_ref, pair_ref):
-    row = jnp.concatenate([keep_ref[...], got_ref[:, : 7 * HALF]], axis=1)
+def split_columns(rank, w, policy):
+    vmem = pl.BlockSpec(memory_space=pltpu.VMEM)
+    hbm = pl.BlockSpec(memory_space=pltpu.HBM)
+    rows = w.shape[0]
+    return pl.pallas_call(
+        split,
+        out_shape=(jax.ShapeDtypeStruct((rows, 7 * HALF + policy.shape[1]), w.dtype),) * 2,
+        in_specs=[pl.BlockSpec(memory_space=pltpu.SMEM), hbm, hbm],
+        out_specs=(vmem, vmem),
+        scratch_shapes=[
+            pltpu.VMEM(w.shape, w.dtype),
+            pltpu.VMEM(policy.shape, policy.dtype),
+            pltpu.SemaphoreType.DMA((2,)),
+        ],
+        compiler_params=pltpu.CompilerParams(vmem_limit_bytes=67_000_000),
+        cost_estimate=cost(0, 8 * w.size),
+    )(rank.reshape(1), w, policy)
+
+
+def pack(keep_ref, got_ref, out_ref, pair_ref):
+    row = jnp.concatenate([keep_ref[:, : 7 * HALF], got_ref[:, : 7 * HALF]], axis=1)
     for j in range(out_ref.shape[0]):
         out_ref[j] = row
-    pair_ref[0] = policy_ref[...]
+    pair_ref[0] = keep_ref[:, 7 * HALF :]
     pair_ref[1] = got_ref[:, 7 * HALF :]
 
 
@@ -97,21 +124,31 @@
     )(place, *parts)
 
 
-def project(own_ref, low_ref, high_ref, w_ref, out_ref):
+def project(own_hbm, other_ref, w_ref, out_ref, own_ref, sems):
     blocks = out_ref.shape[0]
-    rows = own_ref.shape[0]
+    rows = own_hbm.shape[0]
+    size = rows // blocks
     step = rows // 2
+    spans = [pl.ds(part * step, step) for part in range(2)]
+    loads = [
+        pltpu.make_async_copy(own_hbm.at[span], own_ref.at[span], sems.at[part])
+        for part, span in enumerate(spans)
+    ]
+    for load in loads:
+        load.start()
     shared = w_ref[:, 3 * HD : 4 * HD]
     w_own = w_ref[:, : 4 * HD]
     swapped = pltpu.roll(shared.astype(jnp.float32), HALF, 1).astype(jnp.bfloat16)
     w_other = jnp.concatenate([w_ref[:, 4 * HD :], swapped], axis=1)
-    size = rows // blocks
     low = lanes_below_half((size // 2, HD))
+    values = [
+        jnp.dot(other_ref[span, :], w_other, preferred_element_type=jnp.float32) for span in spans
+    ]
     for part in range(2):
         at = part * step
-        value = jnp.dot(own_ref[at : at + step, :], w_own, preferred_element_type=jnp.float32)
-        value = value + jnp.dot(
-            (low_ref, high_ref)[part][...], w_other, preferred_element_type=jnp.float32
+        loads[part].wait()
+        value = values[part] + jnp.dot(
+            own_ref[spans[part], :], w_own, preferred_element_type=jnp.float32
         )
         for b in range(step // size):
             j = at // size + b
@@ -125,6 +162,20 @@
             out_ref[j, 3 * size :] = packed.astype(jnp.bfloat16)
 
 
+def projected(own, other, gathered, blocks):
+    rows, features = own.shape
+    vmem = pl.BlockSpec(memory_space=pltpu.VMEM)
+    return pl.pallas_call(
+        project,
+        out_shape=jax.ShapeDtypeStruct((blocks, 7 * rows // blocks // 2, HD), jnp.bfloat16),
+        in_specs=[pl.BlockSpec(memory_space=pltpu.HBM), vmem, vmem],
+        out_specs=vmem,
+        scratch_shapes=[pltpu.VMEM(own.shape, own.dtype), pltpu.SemaphoreType.DMA((2,))],
+        compiler_params=pltpu.CompilerParams(vmem_limit_bytes=24 * 1024 * 1024),
+        cost_estimate=cost(4 * rows * features * 4 * HD, 4 * own.size + 2 * gathered.size),
+    )(own, other, gathered)
+
+
 def turned(value, cosine, sine):
     return value * cosine + pltpu.roll(value, HALF, 1) * sine
 
@@ -148,12 +199,16 @@
         out_ref[j, size:] = val
 
 
-def attend(rank_ref, part_ref, kv_ref, bias_ref, cos_ref, sin_ref, seg_ref, mine_ref, out_ref):
-    size = out_ref.shape[0]
-    blocks = kv_ref.shape[0]
-    window = min(WINDOW, blocks)
+def first_block(rank, blocks, window):
+    return jnp.clip(rank - (window - 1), 0, blocks - window)
+
+
+def queries(rank_ref, part_ref, bias_ref, cos_ref, sin_ref, seg_ref, mine_ref, out_ref, mask_ref):
+    size = out_ref.shape[1]
+    blocks = seg_ref.shape[0]
+    window = mask_ref.shape[1] // size
     rank = rank_ref[0]
-    first = jnp.clip(rank - (window - 1), 0, blocks - window)
+    first = first_block(rank, blocks, window)
     low = lanes_below_half((size // 2, HD))
     left = added(part_ref, 0, slice(3 * size, 7 * size // 2))
     right = added(part_ref, 1, slice(3 * size, 7 * size // 2))
@@ -171,27 +226,36 @@
         added(part_ref, 1, slice(size, 2 * size)),
         added(part_ref, 1, slice(2 * size, 3 * size)),
     ]
+    cosine, sine = cos_ref[...], sin_ref[...]
+    for h in range(SHARE):
+        query = turned(heads[h] + bias_ref[h : h + 1], cosine, sine)
+        out_ref[h] = query.astype(jnp.bfloat16)
+    row = rank * size + lax.broadcasted_iota(jnp.int32, (size, size), 0)
+    lane = lax.broadcasted_iota(jnp.int32, (size, size), 1)
+    for b in range(window):
+        seg = seg_ref[pl.ds(first + b, 1), :]
+        allowed = (mine_ref[...] == seg) & ((first + b) * size + lane <= row)
+        mask_ref[:, b * size : (b + 1) * size] = jnp.where(allowed, 0.0, -1e30)
+
+
+def attend(rank_ref, q_ref, mask_ref, kv_ref, out_ref):
+    size = out_ref.shape[0]
+    blocks = kv_ref.shape[0]
+    window = mask_ref.shape[1] // size
+    first = first_block(rank_ref[0], blocks, window)
     span = kv_ref[pl.ds(first, window)]
     keys = span[:, :size].reshape(window * size, HD)
     vals = span[:, size:].reshape(window * size, HD)
-    row = rank * size + lax.broadcasted_iota(jnp.int32, (size, size), 0)
-    lane = lax.broadcasted_iota(jnp.int32, (size, size), 1)
-    masks = []
-    for b in range(window):
-        seg = seg_ref[pl.ds(first + b, 1), :]
-        column = (first + b) * size + lane
-        masks.append((mine_ref[...] == seg) & (column <= row))
-    allowed = jnp.concatenate(masks, axis=1)
-    cosine, sine = cos_ref[...], sin_ref[...]
+    mask = mask_ref[...]
     for h in range(SHARE):
-        query = turned(heads[h] + bias_ref[h : h + 1], cosine, sine).astype(jnp.bfloat16)
         scores = lax.dot_general(
-            query, keys, (((1,), (1,)), ((), ())), preferred_element_type=jnp.float32
+            q_ref[h], keys, (((1,), (1,)), ((), ())), preferred_element_type=jnp.float32
         )
-        scores = jnp.where(allowed, scores / jnp.sqrt(jnp.float32(HD)), -1e30)
+        scores = scores * (1.0 / HD**0.5) + mask
         top = jnp.max(scores, axis=-1, keepdims=True)
         expo = jnp.exp(scores - top)
-        weights = (expo / jnp.sum(expo, axis=-1, keepdims=True)).astype(jnp.bfloat16)
+        share = 1.0 / jnp.sum(expo, axis=-1, keepdims=True)
+        weights = (expo * share).astype(jnp.bfloat16)
         context = jnp.dot(weights, vals, preferred_element_type=jnp.float32)
         out_ref[:, h * HD : (h + 1) * HD] = context.astype(jnp.bfloat16)
 
@@ -215,19 +279,16 @@
         return lax.ppermute(value, "fsdp", pairs)
 
     own_features, width = policy_key.shape
-    half = jax.ShapeDtypeStruct((own_features, 7 * HALF), bf16)
-    more = jax.ShapeDtypeStruct((own_features, 7 * HALF + width), bf16)
-    keep, give = call(split, (half, more), 0, rank.reshape(1), ref_qkv, policy_key, scalars=1)
+    keep, give = split_columns(rank, ref_qkv, policy_key)
     got = swapped(give, "rep", 1)
-    low = swapped(tokens[: rows // 2], "rep", 1)
+    other = swapped(tokens, "rep", 1)
     copies = jax.ShapeDtypeStruct((shards, own_features, 7 * HD), bf16)
     pair = jax.ShapeDtypeStruct((2, own_features, width), bf16)
-    copies, pair = call(pack, (copies, pair), 0, keep, got, policy_key)
+    copies, pair = call(pack, (copies, pair), 0, keep, got)
     column = pair
     for bit in range(1, replicas.bit_length() - 1):
         column = jnp.concatenate([column, swapped(column, "rep", 1 << bit)])
     gathered = exchanged(copies, "fsdp").reshape(features, -1)
-    high = swapped(tokens[rows // 2 :], "rep", 1)
     both = jnp.stack([column, swapped(column, "fsdp", length)])
     up, down = [both], [both]
     for k in range(1, length // 2 + 1):
@@ -249,8 +310,7 @@
     sine = jnp.concatenate([-sine, sine], axis=1)
     bias = ref_bias.reshape(SHARE + 2, HD)
 
-    part = jax.ShapeDtypeStruct((replicas, 7 * mine // 2, HD), bf16)
-    part = call(project, (part,), 4 * rows * features * 4 * HD, tokens, low, high, gathered)
+    part = projected(tokens, other, gathered, replicas)
     part = exchanged(part, "rep")
     my_kv = call(
         keys_and_values,
@@ -262,18 +322,31 @@
         sine,
     )
     all_kv = exchanged(my_kv, "rep")
-    context = call(
-        attend,
-        (jax.ShapeDtypeStruct((mine, SHARE * HD), bf16),),
-        4 * SHARE * mine * WINDOW * mine * HD,
+    window = min(WINDOW, replicas)
+    query, mask = call(
+        queries,
+        (
+            jax.ShapeDtypeStruct((SHARE, mine, HD), bf16),
+            jax.ShapeDtypeStruct((mine, window * mine), f32),
+        ),
+        32 * SHARE * mine * HD,
         rank.reshape(1),
         part,
-        all_kv,
         bias,
         cosine,
         sine,
         seg.reshape(replicas, mine),
         my_seg[:, None],
+        scalars=1,
+    )
+    context = call(
+        attend,
+        (jax.ShapeDtypeStruct((mine, SHARE * HD), bf16),),
+        4 * SHARE * mine * window * mine * HD,
+        rank.reshape(1),
+        query,
+        mask,
+        all_kv,
         scalars=1,
     )
     return (context, whole)

time: 152 us -> 152 us (level)
  local copies, waits for them, and re-layouts: 8.45 us -> 3.34 us
  Pallas kernels: 7.57 us -> 12.1 us
  waiting for transfers between devices: 53.7 us -> 56.6 us
  starting transfers between devices: 79.4 us -> 77.3 us
    pallas_call x0 -> x2, Pallas kernels: none -> 5.29 us  [the longest x1 3.65 us: projected(): pl.pallas_call(project, out_shape=jax.ShapeDtypeStruct((blocks, 7 * rows...]
    unnamed x26 -> x14, local copies, waits for them, and re-layouts: 8.2 us -> 3.21 us
    ppermute x6 -> x5, waiting for transfers between devices: 41.3 us -> 44.2 us  [swapped(): return lax.ppermute(value, axis, pairs)]
    ppermute x6 -> x5, starting transfers between devices: 28.5 us -> 26.6 us  [swapped(): return lax.ppermute(value, axis, pairs)]
    pallas_call x5 -> x4, Pallas kernels: 5.95 us -> 5.18 us  [call(): pl.pallas_call(kernel, out_shape=outs if len(outs) > 1 else outs[0], in_s...]
  transfers between devices with their start and end apart: 16 -> 15, of which waited for: 10 -> 9; matrix products, arithmetic and copies ran while one was open for 1% -> 1% of each run, Pallas kernels for 2% -> 2%
where the time goes in v5:
time: 152 us; the launch traced here: 151 us
  starting transfers between devices  77.3 us (51%)
  waiting for transfers between devices  56.6 us (37%)
  Pallas kernels  12.1 us (8%)
  local copies, waits for them, and re-layouts  3.34 us (2%)
    ppermute x5, waiting for transfers between devices, swapped(): return lax.ppermute(value, axis, pairs)  44.2 us
    all_to_all x3, starting transfers between devices, exchanged(): return lax.all_to_all(blocks, axis, split_axis=0, concat_axis=0, tiled=True)  27 us
    ppermute x5, starting transfers between devices, swapped(): return lax.ppermute(value, axis, pairs)  26.6 us
    ppermute x7, starting transfers between devices, passed(): return lax.ppermute(value, 'fsdp', pairs)  23.7 us
    ppermute x7, waiting for transfers between devices, passed(): return lax.ppermute(value, 'fsdp', pairs)  12.4 us
    pallas_call x4, Pallas kernels, call(): pl.pallas_call(kernel, out_shape=outs if len(outs) > 1 else outs[0], in_s...  5.18 us
    pallas_call x1, Pallas kernels, projected(): pl.pallas_call(project, out_shape=jax.ShapeDtypeStruct((blocks, 7 * rows...  3.65 us
    unnamed x14, local copies, waits for them, and re-layouts  3.21 us
  transfers between devices with their start and end apart: 15, of which 9 were waited for; matrix products, arithmetic and copies ran while one was open for 1% of the time, Pallas kernels for 2%

profile of v5, /device:TPU:40, one launch (start us, length us, event | category | flops | bytes accessed | tf_op | source)
XLA Modules:
  0.0 151.1 jit_solution(9364170139478094185)
XLA Ops:
  0.6 1.6 %shard_map.68 = (bf16[40,576]{1,0:T(8,128)(2,1)}, bf16[40,576]{1,0:T(8,128)(2,1)}) custom-call(s32[1]{0:T(128)} %bitcast.rank_ref, bf16[40,896]{1,0:T(8,128)(2,1)} %w_hbm.1, bf16[40,128]{1,0:T(8,128)(2,1)} %policy_hbm.1), custom_call_target="tpu_custom_call" | custom-call | bytes 286720 | tf_op jit(solution)/shard_map/pallas_call | solution.py:73
  2.3 5.2 %collective-permute-start.1 = (bf16[40,576]{1,0:T(8,128)(2,1)}, bf16[40,576]{1,0:T(8,128)(2,1)S(1)}, u32[]{:S(2)}, u32[]{:S(2)}) collective-permute-start(bf16[40,576]{1,0:T(8,128)(2,1)} %get-tuple-element.9), channel_id=1, source_target_pairs={{0,1},{1,0},{2,3},{3,2},{4,5},{5,4},{6,7},{7,6},{8,9},{9,8},{10,11... | collective-permute-start | bytes 138248 | tf_op jit(solution)/shard_map/ppermute | solution.py:275
  7.5 2.3 %collective-permute-done.1.got_ref = bf16[40,576]{1,0:T(8,128)(2,1)S(1)} collective-permute-done((bf16[40,576]{1,0:T(8,128)(2,1)}, bf16[40,576]{1,0:T(8,128)(2,1)S(1)}, u32[]{:S(2)}, u32[]{:S(2)}) %collective-permute-start.1) | collective-permute-done | bytes 46112 | tf_op jit(solution)/shard_map/ppermute | solution.py:275
  9.8 0.0 copy-start
  9.8 0.8 copy-done
  10.6 0.0 copy-start.3
  10.6 1.2 shard_map.69
  11.7 8.3 %all-to-all-start = ((bf16[16,40,896]{2,1,0:T(8,128)(2,1)}), bf16[16,40,896]{2,1,0:T(8,128)(2,1)S(1)}, u32[]{:S(2)}, u32[]{:S(2)}) async-start(bf16[16,40,896]{2,1,0:T(8,128)(2,1)} %get-tuple-element.10), calls=%async_computation | async-start | bytes 2293760 | tf_op jit(solution)/shard_map/all_to_all | solution.py:19
  20.1 0.0 copy-done.3
  20.1 3.9 %collective-permute-start = (bf16[1024,640]{1,0:T(8,128)(2,1)S(1)}, bf16[1024,640]{1,0:T(8,128)(2,1)S(1)}, u32[]{:S(2)}, u32[]{:S(2)}) collective-permute-start(bf16[1024,640]{1,0:T(8,128)(2,1)S(1)} %copy-done.3), channel_id=1, source_target_pairs={{0,1},{1,0},{2,3},{3,2},{4,5},{5,4},{6,7},{7,6},{8,9},{9,8},{10,11... | collective-permute-start | bytes 3932168 | tf_op jit(solution)/shard_map/ppermute | solution.py:275
  24.0 27.1 %collective-permute-done.other_ref = bf16[1024,640]{1,0:T(8,128)(2,1)S(1)} collective-permute-done((bf16[1024,640]{1,0:T(8,128)(2,1)S(1)}, bf16[1024,640]{1,0:T(8,128)(2,1)S(1)}, u32[]{:S(2)}, u32[]{:S(2)}) %collective-permute-start) | collective-permute-done | bytes 1310752 | tf_op jit(solution)/shard_map/ppermute | solution.py:275
  51.1 0.0 copy-start.4
  51.1 1.1 copy-done.4
  52.1 0.0 all-to-all-done
  52.1 0.0 copy-start.5
  52.1 1.3 copy-done.5
  53.4 3.7 %shard_map.70 = bf16[8,448,128]{2,1,0:T(8,128)(2,1)} custom-call(bf16[1024,640]{1,0:T(8,128)(2,1)S(1)} %copy-done.3, bf16[1024,640]{1,0:T(8,128)(2,1)S(1)} %copy-done.5, bf16[640,896]{1,0:T(8,128)(2,1)S(1)} %bitcast.14), custom_call_target="tpu_custom_call" | custom-call | flops 1342177280 | bytes 3768320 | tf_op jit(solution)/shard_map/pallas_call | solution.py:168
  57.1 0.0 copy-start.1
  57.1 0.0 copy-start.2
  57.1 15.1 %all-to-all-start.1 = ((bf16[8,448,128]{2,1,0:T(8,128)(2,1)}), bf16[8,448,128]{2,1,0:T(8,128)(2,1)S(1)}, u32[]{:S(2)}, u32[]{:S(2)}) async-start(bf16[8,448,128]{2,1,0:T(8,128)(2,1)} %shard_map.70), calls=%async_computation.1 | async-start | bytes 1835008 | tf_op jit(solution)/shard_map/all_to_all | solution.py:19
  72.3 0.0 copy-done.1
  72.3 0.2 convert_reduce_fusion
  72.5 0.3 fusion
  72.9 0.1 pad_maximum_fusion.1
  73.0 4.8 %collective-permute-start.2 = (bf16[2,40,128]{2,1,0:T(8,128)(2,1)S(1)}, bf16[2,40,128]{2,1,0:T(8,128)(2,1)S(1)}, u32[]{:S(2)}, u32[]{:S(2)}) collective-permute-start(bf16[2,40,128]{2,1,0:T(8,128)(2,1)S(1)} %get-tuple-element.13), channel_id=1, source_target_pairs={{0,2},{1,3},{2,0},{3,1},{4,6},{5,7},{6,4},{7,5},{8,10},{9,11},{10,... | collective-permute-start | bytes 61448 | tf_op jit(solution)/shard_map/ppermute | solution.py:275
  77.8 12.0 %collective-permute-done.2 = bf16[2,40,128]{2,1,0:T(8,128)(2,1)S(1)} collective-permute-done((bf16[2,40,128]{2,1,0:T(8,128)(2,1)S(1)}, bf16[2,40,128]{2,1,0:T(8,128)(2,1)S(1)}, u32[]{:S(2)}, u32[]{:S(2)}) %collective-permute-start.2) | collective-permute-done | bytes 20512 | tf_op jit(solution)/shard_map/ppermute | solution.py:275
  89.8 9.3 %collective-permute-start.3 = (bf16[4,40,128]{2,1,0:T(8,128)(2,1)S(1)}, bf16[4,40,128]{2,1,0:T(8,128)(2,1)S(1)}, u32[]{:S(2)}, u32[]{:S(2)}) collective-permute-start(bf16[4,40,128]{2,1,0:T(8,128)(2,1)S(1)} %pad_maximum_fusion.3), channel_id=1, source_target_pairs={{0,4},{1,5},{2,6},{3,7},{4,0},{5,1},{6,2},{7,3},{8,12},{9,13},{10,... | collective-permute-start | bytes 122888 | tf_op jit(solution)/shard_map/ppermute | solution.py:275
  99.1 0.0 all-to-all-done.1.part_ref
  99.1 0.0 copy-done.2
  99.1 0.9 shard_map.72
  100.0 3.5 %all-to-all-start.2 = ((bf16[8,256,128]{2,1,0:T(8,128)(2,1)}), bf16[8,256,128]{2,1,0:T(8,128)(2,1)S(1)}, u32[]{:S(2)}, u32[]{:S(2)}) async-start(bf16[8,256,128]{2,1,0:T(8,128)(2,1)} %shard_map.72), calls=%async_computation.2 | async-start | bytes 1048576 | tf_op jit(solution)/shard_map/all_to_all | solution.py:19
  103.5 0.0 collective-permute-done.3
  103.5 3.4 %collective-permute-start.4 = (bf16[8,40,128]{2,1,0:T(8,128)(2,1)S(1)}, bf16[8,40,128]{2,1,0:T(8,128)(2,1)S(1)}, u32[]{:S(2)}, u32[]{:S(2)}) collective-permute-start(bf16[8,40,128]{2,1,0:T(8,128)(2,1)S(1)} %constant_dynamic-update-slice_fusion), channel_id=1, source_target_pairs={{0,512},{64,576},{128,640},{192,704},{256,768},{320,832},{384,896}... | collective-permute-start | bytes 245768 | tf_op jit(solution)/shard_map/ppermute | solution.py:275
  106.9 3.0 %collective-permute-done.4 = bf16[8,40,128]{2,1,0:T(8,128)(2,1)S(1)} collective-permute-done((bf16[8,40,128]{2,1,0:T(8,128)(2,1)S(1)}, bf16[8,40,128]{2,1,0:T(8,128)(2,1)S(1)}, u32[]{:S(2)}, u32[]{:S(2)}) %collective-permute-start.4) | collective-permute-done | bytes 81952 | tf_op jit(solution)/shard_map/ppermute | solution.py:275
  109.9 2.5 %collective-permute-start.5 = (bf16[2,8,40,128]{3,2,1,0:T(8,128)(2,1)S(1)}, bf16[2,8,40,128]{3,2,1,0:T(8,128)(2,1)S(1)}, u32[]{:S(2)}, u32[]{:S(2)}) collective-permute-start(bf16[2,8,40,128]{3,2,1,0:T(8,128)(2,1)S(1)} %pad_maximum_fusion.refs_0_), channel_id=1, source_target_pairs={{0,64},{64,128},{128,192},{192,256},{256,320},{320,384},{384,448},... | collective-permute-start | bytes 491528 | tf_op jit(solution)/shard_map/ppermute | solution.py:279
  112.4 4.6 %collective-permute-start.9 = (bf16[2,8,40,128]{3,2,1,0:T(8,128)(2,1)S(1)}, bf16[2,8,40,128]{3,2,1,0:T(8,128)(2,1)S(1)}, u32[]{:S(2)}, u32[]{:S(2)}) collective-permute-start(bf16[2,8,40,128]{3,2,1,0:T(8,128)(2,1)S(1)} %pad_maximum_fusion.refs_0_), channel_id=1, source_target_pairs={{0,448},{64,0},{128,64},{192,128},{256,192},{320,256},{384,320},{4... | collective-permute-start | bytes 491528 | tf_op jit(solution)/shard_map/ppermute | solution.py:279
  117.0 1.7 %collective-permute-done.5.refs_1_ = bf16[2,8,40,128]{3,2,1,0:T(8,128)(2,1)S(1)} collective-permute-done((bf16[2,8,40,128]{3,2,1,0:T(8,128)(2,1)S(1)}, bf16[2,8,40,128]{3,2,1,0:T(8,128)(2,1)S(1)}, u32[]{:S(2)}, u32[]{:S(2)}) %collective-permute-start.5) | collective-permute-done | bytes 163872 | tf_op jit(solution)/shard_map/ppermute | solution.py:279
  118.7 1.9 %collective-permute-start.6 = (bf16[2,8,40,128]{3,2,1,0:T(8,128)(2,1)S(1)}, bf16[2,8,40,128]{3,2,1,0:T(8,128)(2,1)S(1)}, u32[]{:S(2)}, u32[]{:S(2)}) collective-permute-start(bf16[2,8,40,128]{3,2,1,0:T(8,128)(2,1)S(1)} %collective-permute-done.5.refs_1_), channel_id=1, source_target_pairs={{0,64},{64,128},{128,192},{192,256},{256,320},{320,384},{384,448},... | collective-permute-start | bytes 491528 | tf_op jit(solution)/shard_map/ppermute | solution.py:279
  120.6 0.0 collective-permute-done.9.refs_7_
  120.6 5.4 %collective-permute-start.10 = (bf16[2,8,40,128]{3,2,1,0:T(8,128)(2,1)S(1)}, bf16[2,8,40,128]{3,2,1,0:T(8,128)(2,1)S(1)}, u32[]{:S(2)}, u32[]{:S(2)}) collective-permute-start(bf16[2,8,40,128]{3,2,1,0:T(8,128)(2,1)S(1)} %collective-permute-done.9.refs_7_), channel_id=1, source_target_pairs={{0,448},{64,0},{128,64},{192,128},{256,192},{320,256},{384,320},{4... | collective-permute-start | bytes 491528 | tf_op jit(solution)/shard_map/ppermute | solution.py:279
  126.0 2.6 %collective-permute-done.6.refs_2_ = bf16[2,8,40,128]{3,2,1,0:T(8,128)(2,1)S(1)} collective-permute-done((bf16[2,8,40,128]{3,2,1,0:T(8,128)(2,1)S(1)}, bf16[2,8,40,128]{3,2,1,0:T(8,128)(2,1)S(1)}, u32[]{:S(2)}, u32[]{:S(2)}) %collective-permute-start.6) | collective-permute-done | bytes 163872 | tf_op jit(solution)/shard_map/ppermute | solution.py:279
  128.6 1.9 %collective-permute-start.7 = (bf16[2,8,40,128]{3,2,1,0:T(8,128)(2,1)S(1)}, bf16[2,8,40,128]{3,2,1,0:T(8,128)(2,1)S(1)}, u32[]{:S(2)}, u32[]{:S(2)}) collective-permute-start(bf16[2,8,40,128]{3,2,1,0:T(8,128)(2,1)S(1)} %collective-permute-done.6.refs_2_), channel_id=1, source_target_pairs={{0,64},{64,128},{128,192},{192,256},{256,320},{320,384},{384,448},... | collective-permute-start | bytes 491528 | tf_op jit(solution)/shard_map/ppermute | solution.py:279
  130.5 0.1 collective-permute-done.10.refs_6_
  130.6 5.6 %collective-permute-start.11 = (bf16[2,8,40,128]{3,2,1,0:T(8,128)(2,1)S(1)}, bf16[2,8,40,128]{3,2,1,0:T(8,128)(2,1)S(1)}, u32[]{:S(2)}, u32[]{:S(2)}) collective-permute-start(bf16[2,8,40,128]{3,2,1,0:T(8,128)(2,1)S(1)} %collective-permute-done.10.refs_6_), channel_id=1, source_target_pairs={{0,448},{64,0},{128,64},{192,128},{256,192},{320,256},{384,320},{4... | collective-permute-start | bytes 491528 | tf_op jit(solution)/shard_map/ppermute | solution.py:279
  136.1 1.8 %collective-permute-done.7.refs_3_ = bf16[2,8,40,128]{3,2,1,0:T(8,128)(2,1)S(1)} collective-permute-done((bf16[2,8,40,128]{3,2,1,0:T(8,128)(2,1)S(1)}, bf16[2,8,40,128]{3,2,1,0:T(8,128)(2,1)S(1)}, u32[]{:S(2)}, u32[]{:S(2)}) %collective-permute-start.7) | collective-permute-done | bytes 163872 | tf_op jit(solution)/shard_map/ppermute | solution.py:279
  137.9 1.9 %collective-permute-start.8 = (bf16[2,8,40,128]{3,2,1,0:T(8,128)(2,1)S(1)}, bf16[2,8,40,128]{3,2,1,0:T(8,128)(2,1)S(1)}, u32[]{:S(2)}, u32[]{:S(2)}) collective-permute-start(bf16[2,8,40,128]{3,2,1,0:T(8,128)(2,1)S(1)} %collective-permute-done.7.refs_3_), channel_id=1, source_target_pairs={{0,64},{64,128},{128,192},{192,256},{256,320},{320,384},{384,448},... | collective-permute-start | bytes 491528 | tf_op jit(solution)/shard_map/ppermute | solution.py:279
  139.8 0.1 copy.8.mine_ref
  140.0 0.1 pad_add_fusion.place_ref
  140.0 0.0 collective-permute-done.11.refs_5_
  140.0 6.3 %collective-permute-done.8.refs_4_ = bf16[2,8,40,128]{3,2,1,0:T(8,128)(2,1)S(1)} collective-permute-done((bf16[2,8,40,128]{3,2,1,0:T(8,128)(2,1)S(1)}, bf16[2,8,40,128]{3,2,1,0:T(8,128)(2,1)S(1)}, u32[]{:S(2)}, u32[]{:S(2)}) %collective-permute-start.8) | collective-permute-done | bytes 163872 | tf_op jit(solution)/shard_map/ppermute | solution.py:279
  146.3 1.6 %shard_map.74 = bf16[8,2,8,40,128]{4,3,2,1,0:T(8,128)(2,1)} custom-call(s32[3]{0:T(128)S(1)} %pad_add_fusion.place_ref, bf16[2,8,40,128]{3,2,1,0:T(8,128)(2,1)S(1)} %pad_maximum_fusion.refs_0_, bf16[2,8,40,128]{3,2,1,0:T(8,128)(2,1)S(1)} %collective-permute-done.5.refs_1_, bf16[2,8,40,128]{3,2,1,0:T(8,128)(2,1)S(1)} %collective-permute-done.6.refs_2_, ...), custom_call_target="tpu_custom_call" | custom-call | bytes 2621440 | tf_op jit(solution)/shard_map/pallas_call | solution.py:116
  147.9 0.3 shard_map.71
  148.2 0.0 all-to-all-done.2.kv_ref
  148.2 2.8 %shard_map.73 = bf16[128,640]{1,0:T(8,128)(2,1)} custom-call(s32[1]{0:T(128)} %bitcast.rank_ref, bf16[5,128,128]{2,1,0:T(8,128)(2,1)S(1)} %get-tuple-element.11.q_ref, f32[128,640]{1,0:T(8,128)S(1)} %get-tuple-element.12.mask_ref, bf16[8,256,128]{2,1,0:T(8,128)(2,1)S(1)} %all-to-all-done.2.kv_ref), custom_call_target="tpu_custom_call" | custom-call | flops 209715200 | bytes 1179652 | tf_op jit(solution)/shard_map/pallas_call | solution.py:30
  (8 shorter events, 0.1 us)
Async XLA Ops:
  2.3 7.5 %collective-permute-start.1 = (bf16[40,576]{1,0:T(8,128)(2,1)}, bf16[40,576]{1,0:T(8,128)(2,1)S(1)}, u32[]{:S(2)}, u32[]{:S(2)}) collective-permute-start(bf16[40,576]{1,0:T(8,128)(2,1)} %get-tuple-element.9), channel_id=1, source_target_pairs={{0,1},{1,0},{2,3},{3,2},{4,5},{5,4},{6,7},{7,6},{8,9},{9,8},{10,11... | collective-permute-start | bytes 138248 | tf_op jit(solution)/shard_map/ppermute | solution.py:275
  9.8 0.8 copy-start
  10.6 9.5 %copy-start.3 = (bf16[1024,640]{1,0:T(8,128)(2,1)S(1)}, bf16[1024,640]{1,0:T(8,128)(2,1)}, u32[]{:S(2)}) copy-start(bf16[1024,640]{1,0:T(8,128)(2,1)} %own_hbm.1) | copy-start | bytes 3932164
  11.7 40.4 %all-to-all-start = ((bf16[16,40,896]{2,1,0:T(8,128)(2,1)}), bf16[16,40,896]{2,1,0:T(8,128)(2,1)S(1)}, u32[]{:S(2)}, u32[]{:S(2)}) async-start(bf16[16,40,896]{2,1,0:T(8,128)(2,1)} %get-tuple-element.10), calls=%async_computation | async-start | bytes 2293760 | tf_op jit(solution)/shard_map/all_to_all | solution.py:19
  20.1 31.0 %collective-permute-start = (bf16[1024,640]{1,0:T(8,128)(2,1)S(1)}, bf16[1024,640]{1,0:T(8,128)(2,1)S(1)}, u32[]{:S(2)}, u32[]{:S(2)}) collective-permute-start(bf16[1024,640]{1,0:T(8,128)(2,1)S(1)} %copy-done.3), channel_id=1, source_target_pairs={{0,1},{1,0},{2,3},{3,2},{4,5},{5,4},{6,7},{7,6},{8,9},{9,8},{10,11... | collective-permute-start | bytes 3932168 | tf_op jit(solution)/shard_map/ppermute | solution.py:275
  51.1 1.1 copy-start.4
  52.1 1.3 copy-start.5
  57.1 15.2 %copy-start.1 = (s32[1,1024]{1,0:T(1,128)S(1)}, s32[1,1024]{1,0:T(1,128)}, u32[]{:S(2)}) copy-start(s32[1,1024]{1,0:T(1,128)} %param.8) | copy-start | bytes 12292
  57.1 42.0 %copy-start.2 = (f32[896]{0:T(1024)S(1)}, f32[896]{0:T(1024)}, u32[]{:S(2)}) copy-start(f32[896]{0:T(1024)} %param.7) | copy-start | bytes 10756
  57.1 41.9 %all-to-all-start.1 = ((bf16[8,448,128]{2,1,0:T(8,128)(2,1)}), bf16[8,448,128]{2,1,0:T(8,128)(2,1)S(1)}, u32[]{:S(2)}, u32[]{:S(2)}) async-start(bf16[8,448,128]{2,1,0:T(8,128)(2,1)} %shard_map.70), calls=%async_computation.1 | async-start | bytes 1835008 | tf_op jit(solution)/shard_map/all_to_all | solution.py:19
  73.0 16.8 %collective-permute-start.2 = (bf16[2,40,128]{2,1,0:T(8,128)(2,1)S(1)}, bf16[2,40,128]{2,1,0:T(8,128)(2,1)S(1)}, u32[]{:S(2)}, u32[]{:S(2)}) collective-permute-start(bf16[2,40,128]{2,1,0:T(8,128)(2,1)S(1)} %get-tuple-element.13), channel_id=1, source_target_pairs={{0,2},{1,3},{2,0},{3,1},{4,6},{5,7},{6,4},{7,5},{8,10},{9,11},{10,... | collective-permute-start | bytes 61448 | tf_op jit(solution)/shard_map/ppermute | solution.py:275
  89.8 13.7 %collective-permute-start.3 = (bf16[4,40,128]{2,1,0:T(8,128)(2,1)S(1)}, bf16[4,40,128]{2,1,0:T(8,128)(2,1)S(1)}, u32[]{:S(2)}, u32[]{:S(2)}) collective-permute-start(bf16[4,40,128]{2,1,0:T(8,128)(2,1)S(1)} %pad_maximum_fusion.3), channel_id=1, source_target_pairs={{0,4},{1,5},{2,6},{3,7},{4,0},{5,1},{6,2},{7,3},{8,12},{9,13},{10,... | collective-permute-start | bytes 122888 | tf_op jit(solution)/shard_map/ppermute | solution.py:275
  100.0 48.2 %all-to-all-start.2 = ((bf16[8,256,128]{2,1,0:T(8,128)(2,1)}), bf16[8,256,128]{2,1,0:T(8,128)(2,1)S(1)}, u32[]{:S(2)}, u32[]{:S(2)}) async-start(bf16[8,256,128]{2,1,0:T(8,128)(2,1)} %shard_map.72), calls=%async_computation.2 | async-start | bytes 1048576 | tf_op jit(solution)/shard_map/all_to_all | solution.py:19
  103.5 6.3 %collective-permute-start.4 = (bf16[8,40,128]{2,1,0:T(8,128)(2,1)S(1)}, bf16[8,40,128]{2,1,0:T(8,128)(2,1)S(1)}, u32[]{:S(2)}, u32[]{:S(2)}) collective-permute-start(bf16[8,40,128]{2,1,0:T(8,128)(2,1)S(1)} %constant_dynamic-update-slice_fusion), channel_id=1, source_target_pairs={{0,512},{64,576},{128,640},{192,704},{256,768},{320,832},{384,896}... | collective-permute-start | bytes 245768 | tf_op jit(solution)/shard_map/ppermute | solution.py:275
  109.9 8.8 %collective-permute-start.5 = (bf16[2,8,40,128]{3,2,1,0:T(8,128)(2,1)S(1)}, bf16[2,8,40,128]{3,2,1,0:T(8,128)(2,1)S(1)}, u32[]{:S(2)}, u32[]{:S(2)}) collective-permute-start(bf16[2,8,40,128]{3,2,1,0:T(8,128)(2,1)S(1)} %pad_maximum_fusion.refs_0_), channel_id=1, source_target_pairs={{0,64},{64,128},{128,192},{192,256},{256,320},{320,384},{384,448},... | collective-permute-start | bytes 491528 | tf_op jit(solution)/shard_map/ppermute | solution.py:279
  112.4 8.2 %collective-permute-start.9 = (bf16[2,8,40,128]{3,2,1,0:T(8,128)(2,1)S(1)}, bf16[2,8,40,128]{3,2,1,0:T(8,128)(2,1)S(1)}, u32[]{:S(2)}, u32[]{:S(2)}) collective-permute-start(bf16[2,8,40,128]{3,2,1,0:T(8,128)(2,1)S(1)} %pad_maximum_fusion.refs_0_), channel_id=1, source_target_pairs={{0,448},{64,0},{128,64},{192,128},{256,192},{320,256},{384,320},{4... | collective-permute-start | bytes 491528 | tf_op jit(solution)/shard_map/ppermute | solution.py:279
  118.7 9.9 %collective-permute-start.6 = (bf16[2,8,40,128]{3,2,1,0:T(8,128)(2,1)S(1)}, bf16[2,8,40,128]{3,2,1,0:T(8,128)(2,1)S(1)}, u32[]{:S(2)}, u32[]{:S(2)}) collective-permute-start(bf16[2,8,40,128]{3,2,1,0:T(8,128)(2,1)S(1)} %collective-permute-done.5.refs_1_), channel_id=1, source_target_pairs={{0,64},{64,128},{128,192},{192,256},{256,320},{320,384},{384,448},... | collective-permute-start | bytes 491528 | tf_op jit(solution)/shard_map/ppermute | solution.py:279
  120.6 10.0 %collective-permute-start.10 = (bf16[2,8,40,128]{3,2,1,0:T(8,128)(2,1)S(1)}, bf16[2,8,40,128]{3,2,1,0:T(8,128)(2,1)S(1)}, u32[]{:S(2)}, u32[]{:S(2)}) collective-permute-start(bf16[2,8,40,128]{3,2,1,0:T(8,128)(2,1)S(1)} %collective-permute-done.9.refs_7_), channel_id=1, source_target_pairs={{0,448},{64,0},{128,64},{192,128},{256,192},{320,256},{384,320},{4... | collective-permute-start | bytes 491528 | tf_op jit(solution)/shard_map/ppermute | solution.py:279
  128.6 9.3 %collective-permute-start.7 = (bf16[2,8,40,128]{3,2,1,0:T(8,128)(2,1)S(1)}, bf16[2,8,40,128]{3,2,1,0:T(8,128)(2,1)S(1)}, u32[]{:S(2)}, u32[]{:S(2)}) collective-permute-start(bf16[2,8,40,128]{3,2,1,0:T(8,128)(2,1)S(1)} %collective-permute-done.6.refs_2_), channel_id=1, source_target_pairs={{0,64},{64,128},{128,192},{192,256},{256,320},{320,384},{384,448},... | collective-permute-start | bytes 491528 | tf_op jit(solution)/shard_map/ppermute | solution.py:279
  130.6 9.5 %collective-permute-start.11 = (bf16[2,8,40,128]{3,2,1,0:T(8,128)(2,1)S(1)}, bf16[2,8,40,128]{3,2,1,0:T(8,128)(2,1)S(1)}, u32[]{:S(2)}, u32[]{:S(2)}) collective-permute-start(bf16[2,8,40,128]{3,2,1,0:T(8,128)(2,1)S(1)} %collective-permute-done.10.refs_6_), channel_id=1, source_target_pairs={{0,448},{64,0},{128,64},{192,128},{256,192},{320,256},{384,320},{4... | collective-permute-start | bytes 491528 | tf_op jit(solution)/shard_map/ppermute | solution.py:279
  137.9 8.4 %collective-permute-start.8 = (bf16[2,8,40,128]{3,2,1,0:T(8,128)(2,1)S(1)}, bf16[2,8,40,128]{3,2,1,0:T(8,128)(2,1)S(1)}, u32[]{:S(2)}, u32[]{:S(2)}) collective-permute-start(bf16[2,8,40,128]{3,2,1,0:T(8,128)(2,1)S(1)} %collective-permute-done.7.refs_3_), channel_id=1, source_target_pairs={{0,64},{64,128},{128,192},{192,256},{256,320},{320,384},{384,448},... | collective-permute-start | bytes 491528 | tf_op jit(solution)/shard_map/ppermute | solution.py:279

commit v6 on v5

--- a/solution.py
+++ b/solution.py
@@ -96,6 +96,7 @@
 def arrange(place_ref, *refs):
     *parts, out_ref, sem = refs
     x, y, z = place_ref[0], place_ref[1], place_ref[2]
+    way = 1 - 2 * jnp.bitwise_and(z, 1)
     length, sides, replicas = len(parts), out_ref.shape[1], out_ref.shape[0]
     copies = []
     for k, part in enumerate(parts):
@@ -103,7 +104,8 @@
         column = jnp.bitwise_and(x - distance, length - 1)
         for side in range(sides):
             for b in range(replicas):
-                place = out_ref.at[z ^ b, y ^ side, column]
+                source = jnp.bitwise_and(z + way * (b - b % 2), replicas - 1) ^ (b % 2)
+                place = out_ref.at[source, y ^ side, column]
                 copies.append(pltpu.make_async_copy(part.at[side, b], place, sem))
     for copy in copies:
         copy.start()
@@ -124,31 +126,21 @@
     )(place, *parts)
 
 
-def project(own_hbm, other_ref, w_ref, out_ref, own_ref, sems):
+def project(own_ref, other_ref, w_ref, out_ref):
     blocks = out_ref.shape[0]
-    rows = own_hbm.shape[0]
-    size = rows // blocks
+    rows = own_ref.shape[0]
     step = rows // 2
-    spans = [pl.ds(part * step, step) for part in range(2)]
-    loads = [
-        pltpu.make_async_copy(own_hbm.at[span], own_ref.at[span], sems.at[part])
-        for part, span in enumerate(spans)
-    ]
-    for load in loads:
-        load.start()
     shared = w_ref[:, 3 * HD : 4 * HD]
     w_own = w_ref[:, : 4 * HD]
     swapped = pltpu.roll(shared.astype(jnp.float32), HALF, 1).astype(jnp.bfloat16)
     w_other = jnp.concatenate([w_ref[:, 4 * HD :], swapped], axis=1)
+    size = rows // blocks
     low = lanes_below_half((size // 2, HD))
-    values = [
-        jnp.dot(other_ref[span, :], w_other, preferred_element_type=jnp.float32) for span in spans
-    ]
     for part in range(2):
         at = part * step
-        loads[part].wait()
-        value = values[part] + jnp.dot(
-            own_ref[spans[part], :], w_own, preferred_element_type=jnp.float32
+        value = jnp.dot(own_ref[at : at + step, :], w_own, preferred_element_type=jnp.float32)
+        value = value + jnp.dot(
+            other_ref[at : at + step, :], w_other, preferred_element_type=jnp.float32
         )
         for b in range(step // size):
             j = at // size + b
@@ -160,20 +152,6 @@
             last = piece[:, 3 * HD :]
             packed = jnp.where(low, last[: size // 2], pltpu.roll(last[size // 2 :], HALF, 1))
             out_ref[j, 3 * size :] = packed.astype(jnp.bfloat16)
-
-
-def projected(own, other, gathered, blocks):
-    rows, features = own.shape
-    vmem = pl.BlockSpec(memory_space=pltpu.VMEM)
-    return pl.pallas_call(
-        project,
-        out_shape=jax.ShapeDtypeStruct((blocks, 7 * rows // blocks // 2, HD), jnp.bfloat16),
-        in_specs=[pl.BlockSpec(memory_space=pltpu.HBM), vmem, vmem],
-        out_specs=vmem,
-        scratch_shapes=[pltpu.VMEM(own.shape, own.dtype), pltpu.SemaphoreType.DMA((2,))],
-        compiler_params=pltpu.CompilerParams(vmem_limit_bytes=24 * 1024 * 1024),
-        cost_estimate=cost(4 * rows * features * 4 * HD, 4 * own.size + 2 * gathered.size),
-    )(own, other, gathered)
 
 
 def turned(value, cosine, sine):
@@ -286,8 +264,9 @@
     pair = jax.ShapeDtypeStruct((2, own_features, width), bf16)
     copies, pair = call(pack, (copies, pair), 0, keep, got)
     column = pair
-    for bit in range(1, replicas.bit_length() - 1):
-        column = jnp.concatenate([column, swapped(column, "rep", 1 << bit)])
+    for step in (1 << bit for bit in range(1, replicas.bit_length() - 1)):
+        pairs = [((i - step if i % 2 else i + step) % replicas, i) for i in range(replicas)]
+        column = jnp.concatenate([column, lax.ppermute(column, "rep", pairs)])
     gathered = exchanged(copies, "fsdp").reshape(features, -1)
     both = jnp.stack([column, swapped(column, "fsdp", length)])
     up, down = [both], [both]
@@ -310,7 +289,8 @@
     sine = jnp.concatenate([-sine, sine], axis=1)
     bias = ref_bias.reshape(SHARE + 2, HD)
 
-    part = projected(tokens, other, gathered, replicas)
+    part = jax.ShapeDtypeStruct((replicas, 7 * mine // 2, HD), bf16)
+    part = call(project, (part,), 4 * rows * features * 4 * HD, tokens, other, gathered)
     part = exchanged(part, "rep")
     my_kv = call(
         keys_and_values,

time: 152 us -> 151 us (level)
  the two profiles are of different devices: /device:TPU:40 before, /device:TPU:32 now
where the time goes in v6:
time: 151 us; the launch traced here: 150 us
  starting transfers between devices  76.9 us (51%)
  waiting for transfers between devices  56.6 us (37%)
  Pallas kernels  11.3 us (7%)
  local copies, waits for them, and re-layouts  3.34 us (2%)
    ppermute x3, waiting for transfers between devices, swapped(): return lax.ppermute(value, axis, pairs)  32.5 us
    all_to_all x3, starting transfers between devices, exchanged(): return lax.all_to_all(blocks, axis, split_axis=0, concat_axis=0, tiled=True)  28.1 us
    ppermute x7, starting transfers between devices, passed(): return lax.ppermute(value, 'fsdp', pairs)  22.7 us
    ppermute x2, starting transfers between devices, body(): column = jnp.concatenate([column, lax.ppermute(column, 'rep', pairs)])  13.7 us
    ppermute x7, waiting for transfers between devices, passed(): return lax.ppermute(value, 'fsdp', pairs)  13.1 us
    ppermute x3, starting transfers between devices, swapped(): return lax.ppermute(value, axis, pairs)  12.5 us
    ppermute x2, waiting for transfers between devices, body(): column = jnp.concatenate([column, lax.ppermute(column, 'rep', pairs)])  11 us
    pallas_call x5, Pallas kernels, call(): pl.pallas_call(kernel, out_shape=outs if len(outs) > 1 else outs[0], in_s...  8.01 us
  transfers between devices with their start and end apart: 15, of which 10 were waited for; matrix products, arithmetic and copies ran while one was open for 1% of the time, Pallas kernels for 2%

profile of v6, /device:TPU:32, one launch (start us, length us, event | category | flops | bytes accessed | tf_op | source)
XLA Modules:
  0.0 149.8 jit_solution(853605435446326613)
XLA Ops:
  0.6 1.6 %shard_map.68 = (bf16[40,576]{1,0:T(8,128)(2,1)}, bf16[40,576]{1,0:T(8,128)(2,1)}) custom-call(s32[1]{0:T(128)} %bitcast.rank_ref, bf16[40,896]{1,0:T(8,128)(2,1)} %w_hbm.1, bf16[40,128]{1,0:T(8,128)(2,1)} %policy_hbm.1), custom_call_target="tpu_custom_call" | custom-call | bytes 286720 | tf_op jit(solution)/shard_map/pallas_call | solution.py:73
  2.3 5.2 %collective-permute-start.1 = (bf16[40,576]{1,0:T(8,128)(2,1)}, bf16[40,576]{1,0:T(8,128)(2,1)S(1)}, u32[]{:S(2)}, u32[]{:S(2)}) collective-permute-start(bf16[40,576]{1,0:T(8,128)(2,1)} %get-tuple-element.9), channel_id=1, source_target_pairs={{0,1},{1,0},{2,3},{3,2},{4,5},{5,4},{6,7},{7,6},{8,9},{9,8},{10,11... | collective-permute-start | bytes 138248 | tf_op jit(solution)/shard_map/ppermute | solution.py:253
  7.5 2.3 %collective-permute-done.1.got_ref = bf16[40,576]{1,0:T(8,128)(2,1)S(1)} collective-permute-done((bf16[40,576]{1,0:T(8,128)(2,1)}, bf16[40,576]{1,0:T(8,128)(2,1)S(1)}, u32[]{:S(2)}, u32[]{:S(2)}) %collective-permute-start.1) | collective-permute-done | bytes 46112 | tf_op jit(solution)/shard_map/ppermute | solution.py:253
  9.8 0.0 copy-start
  9.8 0.8 copy-done
  10.6 0.0 copy-start.3
  10.6 1.2 shard_map.69
  11.7 8.0 %all-to-all-start = ((bf16[16,40,896]{2,1,0:T(8,128)(2,1)}), bf16[16,40,896]{2,1,0:T(8,128)(2,1)S(1)}, u32[]{:S(2)}, u32[]{:S(2)}) async-start(bf16[16,40,896]{2,1,0:T(8,128)(2,1)} %get-tuple-element.10), calls=%async_computation | async-start | bytes 2293760 | tf_op jit(solution)/shard_map/all_to_all | solution.py:19
  19.7 0.0 copy-done.3
  19.7 3.9 %collective-permute-start = (bf16[1024,640]{1,0:T(8,128)(2,1)S(1)}, bf16[1024,640]{1,0:T(8,128)(2,1)S(1)}, u32[]{:S(2)}, u32[]{:S(2)}) collective-permute-start(bf16[1024,640]{1,0:T(8,128)(2,1)S(1)} %copy-done.3), channel_id=1, source_target_pairs={{0,1},{1,0},{2,3},{3,2},{4,5},{5,4},{6,7},{7,6},{8,9},{9,8},{10,11... | collective-permute-start | bytes 3932168 | tf_op jit(solution)/shard_map/ppermute | solution.py:253
  23.7 27.3 %collective-permute-done.other_ref = bf16[1024,640]{1,0:T(8,128)(2,1)S(1)} collective-permute-done((bf16[1024,640]{1,0:T(8,128)(2,1)S(1)}, bf16[1024,640]{1,0:T(8,128)(2,1)S(1)}, u32[]{:S(2)}, u32[]{:S(2)}) %collective-permute-start) | collective-permute-done | bytes 1310752 | tf_op jit(solution)/shard_map/ppermute | solution.py:253
  51.0 0.0 copy-start.4
  51.0 1.1 copy-done.4
  52.1 0.0 all-to-all-done
  52.1 0.0 copy-start.5
  52.1 1.3 copy-done.5
  53.4 2.8 %shard_map.70 = bf16[8,448,128]{2,1,0:T(8,128)(2,1)} custom-call(bf16[1024,640]{1,0:T(8,128)(2,1)S(1)} %copy-done.3, bf16[1024,640]{1,0:T(8,128)(2,1)S(1)} %copy-done.5, bf16[640,896]{1,0:T(8,128)(2,1)S(1)} %bitcast.14), custom_call_target="tpu_custom_call" | custom-call | flops 1342177280 | bytes 4685824 | tf_op jit(solution)/shard_map/pallas_call | solution.py:30
  56.2 0.0 copy-start.1
  56.2 0.0 copy-start.2
  56.2 15.3 %all-to-all-start.1 = ((bf16[8,448,128]{2,1,0:T(8,128)(2,1)}), bf16[8,448,128]{2,1,0:T(8,128)(2,1)S(1)}, u32[]{:S(2)}, u32[]{:S(2)}) async-start(bf16[8,448,128]{2,1,0:T(8,128)(2,1)} %shard_map.70), calls=%async_computation.1 | async-start | bytes 1835008 | tf_op jit(solution)/shard_map/all_to_all | solution.py:19
  71.5 0.0 copy-done.1
  71.5 0.2 convert_reduce_fusion
  71.7 0.3 fusion
  72.1 0.1 pad_maximum_fusion.1
  72.2 6.0 %collective-permute-start.2 = (bf16[2,40,128]{2,1,0:T(8,128)(2,1)S(1)}, bf16[2,40,128]{2,1,0:T(8,128)(2,1)S(1)}, u32[]{:S(2)}, u32[]{:S(2)}) collective-permute-start(bf16[2,40,128]{2,1,0:T(8,128)(2,1)S(1)} %get-tuple-element.13), channel_id=1, source_target_pairs={{2,0},{7,1},{4,2},{1,3},{6,4},{3,5},{0,6},{5,7},{10,8},{15,9},{12,... | collective-permute-start | bytes 61448 | tf_op jit(solution)/shard_map/ppermute | solution.py:269
  78.2 11.0 %collective-permute-done.2 = bf16[2,40,128]{2,1,0:T(8,128)(2,1)S(1)} collective-permute-done((bf16[2,40,128]{2,1,0:T(8,128)(2,1)S(1)}, bf16[2,40,128]{2,1,0:T(8,128)(2,1)S(1)}, u32[]{:S(2)}, u32[]{:S(2)}) %collective-permute-start.2) | collective-permute-done | bytes 20512 | tf_op jit(solution)/shard_map/ppermute | solution.py:269
  89.3 7.6 %collective-permute-start.3 = (bf16[4,40,128]{2,1,0:T(8,128)(2,1)S(1)}, bf16[4,40,128]{2,1,0:T(8,128)(2,1)S(1)}, u32[]{:S(2)}, u32[]{:S(2)}) collective-permute-start(bf16[4,40,128]{2,1,0:T(8,128)(2,1)S(1)} %pad_maximum_fusion.3), channel_id=1, source_target_pairs={{4,0},{5,1},{6,2},{7,3},{0,4},{1,5},{2,6},{3,7},{12,8},{13,9},{14,... | collective-permute-start | bytes 122888 | tf_op jit(solution)/shard_map/ppermute | solution.py:269
  96.9 0.0 all-to-all-done.1.part_ref
  96.9 0.0 copy-done.2
  96.9 0.9 shard_map.72
  97.8 4.8 %all-to-all-start.2 = ((bf16[8,256,128]{2,1,0:T(8,128)(2,1)}), bf16[8,256,128]{2,1,0:T(8,128)(2,1)S(1)}, u32[]{:S(2)}, u32[]{:S(2)}) async-start(bf16[8,256,128]{2,1,0:T(8,128)(2,1)} %shard_map.72), calls=%async_computation.2 | async-start | bytes 1048576 | tf_op jit(solution)/shard_map/all_to_all | solution.py:19
  102.7 0.0 collective-permute-done.3
  102.7 3.4 %collective-permute-start.4 = (bf16[8,40,128]{2,1,0:T(8,128)(2,1)S(1)}, bf16[8,40,128]{2,1,0:T(8,128)(2,1)S(1)}, u32[]{:S(2)}, u32[]{:S(2)}) collective-permute-start(bf16[8,40,128]{2,1,0:T(8,128)(2,1)S(1)} %constant_dynamic-update-slice_fusion), channel_id=1, source_target_pairs={{0,512},{64,576},{128,640},{192,704},{256,768},{320,832},{384,896}... | collective-permute-start | bytes 245768 | tf_op jit(solution)/shard_map/ppermute | solution.py:253
  106.1 2.9 %collective-permute-done.4 = bf16[8,40,128]{2,1,0:T(8,128)(2,1)S(1)} collective-permute-done((bf16[8,40,128]{2,1,0:T(8,128)(2,1)S(1)}, bf16[8,40,128]{2,1,0:T(8,128)(2,1)S(1)}, u32[]{:S(2)}, u32[]{:S(2)}) %collective-permute-start.4) | collective-permute-done | bytes 81952 | tf_op jit(solution)/shard_map/ppermute | solution.py:253
  109.0 3.4 %collective-permute-start.5 = (bf16[2,8,40,128]{3,2,1,0:T(8,128)(2,1)S(1)}, bf16[2,8,40,128]{3,2,1,0:T(8,128)(2,1)S(1)}, u32[]{:S(2)}, u32[]{:S(2)}) collective-permute-start(bf16[2,8,40,128]{3,2,1,0:T(8,128)(2,1)S(1)} %pad_maximum_fusion.refs_0_), channel_id=1, source_target_pairs={{0,64},{64,128},{128,192},{192,256},{256,320},{320,384},{384,448},... | collective-permute-start | bytes 491528 | tf_op jit(solution)/shard_map/ppermute | solution.py:257
  112.4 3.6 %collective-permute-start.9 = (bf16[2,8,40,128]{3,2,1,0:T(8,128)(2,1)S(1)}, bf16[2,8,40,128]{3,2,1,0:T(8,128)(2,1)S(1)}, u32[]{:S(2)}, u32[]{:S(2)}) collective-permute-start(bf16[2,8,40,128]{3,2,1,0:T(8,128)(2,1)S(1)} %pad_maximum_fusion.refs_0_), channel_id=1, source_target_pairs={{0,448},{64,0},{128,64},{192,128},{256,192},{320,256},{384,320},{4... | collective-permute-start | bytes 491528 | tf_op jit(solution)/shard_map/ppermute | solution.py:257
  116.1 1.4 collective-permute-done.5.refs_1_
  117.5 2.9 %collective-permute-start.6 = (bf16[2,8,40,128]{3,2,1,0:T(8,128)(2,1)S(1)}, bf16[2,8,40,128]{3,2,1,0:T(8,128)(2,1)S(1)}, u32[]{:S(2)}, u32[]{:S(2)}) collective-permute-start(bf16[2,8,40,128]{3,2,1,0:T(8,128)(2,1)S(1)} %collective-permute-done.5.refs_1_), channel_id=1, source_target_pairs={{0,64},{64,128},{128,192},{192,256},{256,320},{320,384},{384,448},... | collective-permute-start | bytes 491528 | tf_op jit(solution)/shard_map/ppermute | solution.py:257
  120.4 0.3 collective-permute-done.9.refs_7_
  120.7 3.8 %collective-permute-start.10 = (bf16[2,8,40,128]{3,2,1,0:T(8,128)(2,1)S(1)}, bf16[2,8,40,128]{3,2,1,0:T(8,128)(2,1)S(1)}, u32[]{:S(2)}, u32[]{:S(2)}) collective-permute-start(bf16[2,8,40,128]{3,2,1,0:T(8,128)(2,1)S(1)} %collective-permute-done.9.refs_7_), channel_id=1, source_target_pairs={{0,448},{64,0},{128,64},{192,128},{256,192},{320,256},{384,320},{4... | collective-permute-start | bytes 491528 | tf_op jit(solution)/shard_map/ppermute | solution.py:257
  124.5 2.0 %collective-permute-done.6.refs_2_ = bf16[2,8,40,128]{3,2,1,0:T(8,128)(2,1)S(1)} collective-permute-done((bf16[2,8,40,128]{3,2,1,0:T(8,128)(2,1)S(1)}, bf16[2,8,40,128]{3,2,1,0:T(8,128)(2,1)S(1)}, u32[]{:S(2)}, u32[]{:S(2)}) %collective-permute-start.6) | collective-permute-done | bytes 163872 | tf_op jit(solution)/shard_map/ppermute | solution.py:257
  126.6 2.4 %collective-permute-start.7 = (bf16[2,8,40,128]{3,2,1,0:T(8,128)(2,1)S(1)}, bf16[2,8,40,128]{3,2,1,0:T(8,128)(2,1)S(1)}, u32[]{:S(2)}, u32[]{:S(2)}) collective-permute-start(bf16[2,8,40,128]{3,2,1,0:T(8,128)(2,1)S(1)} %collective-permute-done.6.refs_2_), channel_id=1, source_target_pairs={{0,64},{64,128},{128,192},{192,256},{256,320},{320,384},{384,448},... | collective-permute-start | bytes 491528 | tf_op jit(solution)/shard_map/ppermute | solution.py:257
  129.0 0.4 collective-permute-done.10.refs_6_
  129.4 4.5 %collective-permute-start.11 = (bf16[2,8,40,128]{3,2,1,0:T(8,128)(2,1)S(1)}, bf16[2,8,40,128]{3,2,1,0:T(8,128)(2,1)S(1)}, u32[]{:S(2)}, u32[]{:S(2)}) collective-permute-start(bf16[2,8,40,128]{3,2,1,0:T(8,128)(2,1)S(1)} %collective-permute-done.10.refs_6_), channel_id=1, source_target_pairs={{0,448},{64,0},{128,64},{192,128},{256,192},{320,256},{384,320},{4... | collective-permute-start | bytes 491528 | tf_op jit(solution)/shard_map/ppermute | solution.py:257
  133.9 2.7 %collective-permute-done.7.refs_3_ = bf16[2,8,40,128]{3,2,1,0:T(8,128)(2,1)S(1)} collective-permute-done((bf16[2,8,40,128]{3,2,1,0:T(8,128)(2,1)S(1)}, bf16[2,8,40,128]{3,2,1,0:T(8,128)(2,1)S(1)}, u32[]{:S(2)}, u32[]{:S(2)}) %collective-permute-start.7) | collective-permute-done | bytes 163872 | tf_op jit(solution)/shard_map/ppermute | solution.py:257
  136.6 1.9 %collective-permute-start.8 = (bf16[2,8,40,128]{3,2,1,0:T(8,128)(2,1)S(1)}, bf16[2,8,40,128]{3,2,1,0:T(8,128)(2,1)S(1)}, u32[]{:S(2)}, u32[]{:S(2)}) collective-permute-start(bf16[2,8,40,128]{3,2,1,0:T(8,128)(2,1)S(1)} %collective-permute-done.7.refs_3_), channel_id=1, source_target_pairs={{0,64},{64,128},{128,192},{192,256},{256,320},{320,384},{384,448},... | collective-permute-start | bytes 491528 | tf_op jit(solution)/shard_map/ppermute | solution.py:257
  138.6 0.1 copy.8.mine_ref
  138.7 0.1 pad_add_fusion.place_ref
  138.8 0.0 collective-permute-done.11.refs_5_
  138.8 6.3 %collective-permute-done.8.refs_4_ = bf16[2,8,40,128]{3,2,1,0:T(8,128)(2,1)S(1)} collective-permute-done((bf16[2,8,40,128]{3,2,1,0:T(8,128)(2,1)S(1)}, bf16[2,8,40,128]{3,2,1,0:T(8,128)(2,1)S(1)}, u32[]{:S(2)}, u32[]{:S(2)}) %collective-permute-start.8) | collective-permute-done | bytes 163872 | tf_op jit(solution)/shard_map/ppermute | solution.py:257
  145.1 1.6 %shard_map.74 = bf16[8,2,8,40,128]{4,3,2,1,0:T(8,128)(2,1)} custom-call(s32[3]{0:T(128)S(1)} %pad_add_fusion.place_ref, bf16[2,8,40,128]{3,2,1,0:T(8,128)(2,1)S(1)} %pad_maximum_fusion.refs_0_, bf16[2,8,40,128]{3,2,1,0:T(8,128)(2,1)S(1)} %collective-permute-done.5.refs_1_, bf16[2,8,40,128]{3,2,1,0:T(8,128)(2,1)S(1)} %collective-permute-done.6.refs_2_, ...), custom_call_target="tpu_custom_call" | custom-call | bytes 2621440 | tf_op jit(solution)/shard_map/pallas_call | solution.py:118
  146.7 0.3 shard_map.71
  147.0 0.0 all-to-all-done.2.kv_ref
  147.0 2.8 %shard_map.73 = bf16[128,640]{1,0:T(8,128)(2,1)} custom-call(s32[1]{0:T(128)} %bitcast.rank_ref, bf16[5,128,128]{2,1,0:T(8,128)(2,1)S(1)} %get-tuple-element.11.q_ref, f32[128,640]{1,0:T(8,128)S(1)} %get-tuple-element.12.mask_ref, bf16[8,256,128]{2,1,0:T(8,128)(2,1)S(1)} %all-to-all-done.2.kv_ref), custom_call_target="tpu_custom_call" | custom-call | flops 209715200 | bytes 1179652 | tf_op jit(solution)/shard_map/pallas_call | solution.py:30
  (8 shorter events, 0.1 us)
Async XLA Ops:
  2.3 7.5 %collective-permute-start.1 = (bf16[40,576]{1,0:T(8,128)(2,1)}, bf16[40,576]{1,0:T(8,128)(2,1)S(1)}, u32[]{:S(2)}, u32[]{:S(2)}) collective-permute-start(bf16[40,576]{1,0:T(8,128)(2,1)} %get-tuple-element.9), channel_id=1, source_target_pairs={{0,1},{1,0},{2,3},{3,2},{4,5},{5,4},{6,7},{7,6},{8,9},{9,8},{10,11... | collective-permute-start | bytes 138248 | tf_op jit(solution)/shard_map/ppermute | solution.py:253
  9.8 0.8 copy-start
  10.6 9.2 %copy-start.3 = (bf16[1024,640]{1,0:T(8,128)(2,1)S(1)}, bf16[1024,640]{1,0:T(8,128)(2,1)}, u32[]{:S(2)}) copy-start(bf16[1024,640]{1,0:T(8,128)(2,1)} %own_ref.1) | copy-start | bytes 3932164
  11.7 40.3 %all-to-all-start = ((bf16[16,40,896]{2,1,0:T(8,128)(2,1)}), bf16[16,40,896]{2,1,0:T(8,128)(2,1)S(1)}, u32[]{:S(2)}, u32[]{:S(2)}) async-start(bf16[16,40,896]{2,1,0:T(8,128)(2,1)} %get-tuple-element.10), calls=%async_computation | async-start | bytes 2293760 | tf_op jit(solution)/shard_map/all_to_all | solution.py:19
  19.7 31.3 %collective-permute-start = (bf16[1024,640]{1,0:T(8,128)(2,1)S(1)}, bf16[1024,640]{1,0:T(8,128)(2,1)S(1)}, u32[]{:S(2)}, u32[]{:S(2)}) collective-permute-start(bf16[1024,640]{1,0:T(8,128)(2,1)S(1)} %copy-done.3), channel_id=1, source_target_pairs={{0,1},{1,0},{2,3},{3,2},{4,5},{5,4},{6,7},{7,6},{8,9},{9,8},{10,11... | collective-permute-start | bytes 3932168 | tf_op jit(solution)/shard_map/ppermute | solution.py:253
  51.0 1.1 copy-start.4
  52.1 1.3 copy-start.5
  56.2 15.3 %copy-start.1 = (s32[1,1024]{1,0:T(1,128)S(1)}, s32[1,1024]{1,0:T(1,128)}, u32[]{:S(2)}) copy-start(s32[1,1024]{1,0:T(1,128)} %param.8) | copy-start | bytes 12292
  56.2 40.7 %copy-start.2 = (f32[896]{0:T(1024)S(1)}, f32[896]{0:T(1024)}, u32[]{:S(2)}) copy-start(f32[896]{0:T(1024)} %param.7) | copy-start | bytes 10756
  56.2 40.7 %all-to-all-start.1 = ((bf16[8,448,128]{2,1,0:T(8,128)(2,1)}), bf16[8,448,128]{2,1,0:T(8,128)(2,1)S(1)}, u32[]{:S(2)}, u32[]{:S(2)}) async-start(bf16[8,448,128]{2,1,0:T(8,128)(2,1)} %shard_map.70), calls=%async_computation.1 | async-start | bytes 1835008 | tf_op jit(solution)/shard_map/all_to_all | solution.py:19
  72.2 17.1 %collective-permute-start.2 = (bf16[2,40,128]{2,1,0:T(8,128)(2,1)S(1)}, bf16[2,40,128]{2,1,0:T(8,128)(2,1)S(1)}, u32[]{:S(2)}, u32[]{:S(2)}) collective-permute-start(bf16[2,40,128]{2,1,0:T(8,128)(2,1)S(1)} %get-tuple-element.13), channel_id=1, source_target_pairs={{2,0},{7,1},{4,2},{1,3},{6,4},{3,5},{0,6},{5,7},{10,8},{15,9},{12,... | collective-permute-start | bytes 61448 | tf_op jit(solution)/shard_map/ppermute | solution.py:269
  89.3 13.4 %collective-permute-start.3 = (bf16[4,40,128]{2,1,0:T(8,128)(2,1)S(1)}, bf16[4,40,128]{2,1,0:T(8,128)(2,1)S(1)}, u32[]{:S(2)}, u32[]{:S(2)}) collective-permute-start(bf16[4,40,128]{2,1,0:T(8,128)(2,1)S(1)} %pad_maximum_fusion.3), channel_id=1, source_target_pairs={{4,0},{5,1},{6,2},{7,3},{0,4},{1,5},{2,6},{3,7},{12,8},{13,9},{14,... | collective-permute-start | bytes 122888 | tf_op jit(solution)/shard_map/ppermute | solution.py:269
  97.8 49.2 %all-to-all-start.2 = ((bf16[8,256,128]{2,1,0:T(8,128)(2,1)}), bf16[8,256,128]{2,1,0:T(8,128)(2,1)S(1)}, u32[]{:S(2)}, u32[]{:S(2)}) async-start(bf16[8,256,128]{2,1,0:T(8,128)(2,1)} %shard_map.72), calls=%async_computation.2 | async-start | bytes 1048576 | tf_op jit(solution)/shard_map/all_to_all | solution.py:19
  102.7 6.3 %collective-permute-start.4 = (bf16[8,40,128]{2,1,0:T(8,128)(2,1)S(1)}, bf16[8,40,128]{2,1,0:T(8,128)(2,1)S(1)}, u32[]{:S(2)}, u32[]{:S(2)}) collective-permute-start(bf16[8,40,128]{2,1,0:T(8,128)(2,1)S(1)} %constant_dynamic-update-slice_fusion), channel_id=1, source_target_pairs={{0,512},{64,576},{128,640},{192,704},{256,768},{320,832},{384,896}... | collective-permute-start | bytes 245768 | tf_op jit(solution)/shard_map/ppermute | solution.py:253
  109.0 8.4 %collective-permute-start.5 = (bf16[2,8,40,128]{3,2,1,0:T(8,128)(2,1)S(1)}, bf16[2,8,40,128]{3,2,1,0:T(8,128)(2,1)S(1)}, u32[]{:S(2)}, u32[]{:S(2)}) collective-permute-start(bf16[2,8,40,128]{3,2,1,0:T(8,128)(2,1)S(1)} %pad_maximum_fusion.refs_0_), channel_id=1, source_target_pairs={{0,64},{64,128},{128,192},{192,256},{256,320},{320,384},{384,448},... | collective-permute-start | bytes 491528 | tf_op jit(solution)/shard_map/ppermute | solution.py:257
  112.4 8.2 %collective-permute-start.9 = (bf16[2,8,40,128]{3,2,1,0:T(8,128)(2,1)S(1)}, bf16[2,8,40,128]{3,2,1,0:T(8,128)(2,1)S(1)}, u32[]{:S(2)}, u32[]{:S(2)}) collective-permute-start(bf16[2,8,40,128]{3,2,1,0:T(8,128)(2,1)S(1)} %pad_maximum_fusion.refs_0_), channel_id=1, source_target_pairs={{0,448},{64,0},{128,64},{192,128},{256,192},{320,256},{384,320},{4... | collective-permute-start | bytes 491528 | tf_op jit(solution)/shard_map/ppermute | solution.py:257
  117.5 9.1 %collective-permute-start.6 = (bf16[2,8,40,128]{3,2,1,0:T(8,128)(2,1)S(1)}, bf16[2,8,40,128]{3,2,1,0:T(8,128)(2,1)S(1)}, u32[]{:S(2)}, u32[]{:S(2)}) collective-permute-start(bf16[2,8,40,128]{3,2,1,0:T(8,128)(2,1)S(1)} %collective-permute-done.5.refs_1_), channel_id=1, source_target_pairs={{0,64},{64,128},{128,192},{192,256},{256,320},{320,384},{384,448},... | collective-permute-start | bytes 491528 | tf_op jit(solution)/shard_map/ppermute | solution.py:257
  120.7 8.8 %collective-permute-start.10 = (bf16[2,8,40,128]{3,2,1,0:T(8,128)(2,1)S(1)}, bf16[2,8,40,128]{3,2,1,0:T(8,128)(2,1)S(1)}, u32[]{:S(2)}, u32[]{:S(2)}) collective-permute-start(bf16[2,8,40,128]{3,2,1,0:T(8,128)(2,1)S(1)} %collective-permute-done.9.refs_7_), channel_id=1, source_target_pairs={{0,448},{64,0},{128,64},{192,128},{256,192},{320,256},{384,320},{4... | collective-permute-start | bytes 491528 | tf_op jit(solution)/shard_map/ppermute | solution.py:257
  126.6 10.1 %collective-permute-start.7 = (bf16[2,8,40,128]{3,2,1,0:T(8,128)(2,1)S(1)}, bf16[2,8,40,128]{3,2,1,0:T(8,128)(2,1)S(1)}, u32[]{:S(2)}, u32[]{:S(2)}) collective-permute-start(bf16[2,8,40,128]{3,2,1,0:T(8,128)(2,1)S(1)} %collective-permute-done.6.refs_2_), channel_id=1, source_target_pairs={{0,64},{64,128},{128,192},{192,256},{256,320},{320,384},{384,448},... | collective-permute-start | bytes 491528 | tf_op jit(solution)/shard_map/ppermute | solution.py:257
  129.4 9.4 %collective-permute-start.11 = (bf16[2,8,40,128]{3,2,1,0:T(8,128)(2,1)S(1)}, bf16[2,8,40,128]{3,2,1,0:T(8,128)(2,1)S(1)}, u32[]{:S(2)}, u32[]{:S(2)}) collective-permute-start(bf16[2,8,40,128]{3,2,1,0:T(8,128)(2,1)S(1)} %collective-permute-done.10.refs_6_), channel_id=1, source_target_pairs={{0,448},{64,0},{128,64},{192,128},{256,192},{320,256},{384,320},{4... | collective-permute-start | bytes 491528 | tf_op jit(solution)/shard_map/ppermute | solution.py:257
  136.6 8.4 %collective-permute-start.8 = (bf16[2,8,40,128]{3,2,1,0:T(8,128)(2,1)S(1)}, bf16[2,8,40,128]{3,2,1,0:T(8,128)(2,1)S(1)}, u32[]{:S(2)}, u32[]{:S(2)}) collective-permute-start(bf16[2,8,40,128]{3,2,1,0:T(8,128)(2,1)S(1)} %collective-permute-done.7.refs_3_), channel_id=1, source_target_pairs={{0,64},{64,128},{128,192},{192,256},{256,320},{320,384},{384,448},... | collective-permute-start | bytes 491528 | tf_op jit(solution)/shard_map/ppermute | solution.py:257

commit v7 on v6

--- a/solution.py
+++ b/solution.py
@@ -11,12 +11,16 @@
 HD = 128
 HALF = HD // 2
 SHARE = QH // KVH
-SIDES = 2
+LENGTH = 8
 WINDOW = 5
 
 
 def exchanged(blocks, axis):
     return lax.all_to_all(blocks, axis, split_axis=0, concat_axis=0, tiled=True)
+
+
+def in_hbm(array):
+    return pltpu.with_memory_space_constraint(array, pltpu.HBM)
 
 
 def cost(flops, moved):
@@ -80,7 +84,7 @@
             pltpu.VMEM(policy.shape, policy.dtype),
             pltpu.SemaphoreType.DMA((2,)),
         ],
-        compiler_params=pltpu.CompilerParams(vmem_limit_bytes=67_000_000),
+        compiler_params=pltpu.CompilerParams(vmem_limit_bytes=4 * 1024 * 1024),
         cost_estimate=cost(0, 8 * w.size),
     )(rank.reshape(1), w, policy)
 
@@ -93,22 +97,27 @@
     pair_ref[1] = got_ref[:, 7 * HALF :]
 
 
-def arrange(place_ref, *refs):
-    *parts, out_ref, sem = refs
+def arrange(place_ref, own_ref, up_ref, across_ref, down_ref, ups_ref, downs_ref, out_ref, sem):
     x, y, z = place_ref[0], place_ref[1], place_ref[2]
     way = 1 - 2 * jnp.bitwise_and(z, 1)
-    length, sides, replicas = len(parts), out_ref.shape[1], out_ref.shape[0]
-    copies = []
-    for k, part in enumerate(parts):
-        distance = k if k <= length // 2 else k - length
+    replicas, sides, length = out_ref.shape[:3]
+    parts = [
+        (own_ref, 0),
+        (up_ref, 1),
+        (ups_ref.at[0], 2),
+        (ups_ref.at[1], 3),
+        (across_ref, 4),
+        (downs_ref.at[1], 5),
+        (downs_ref.at[0], 6),
+        (down_ref, 7),
+    ]
+    for part, distance in parts:
         column = jnp.bitwise_and(x - distance, length - 1)
         for side in range(sides):
             for b in range(replicas):
                 source = jnp.bitwise_and(z + way * (b - b % 2), replicas - 1) ^ (b % 2)
                 place = out_ref.at[source, y ^ side, column]
-                copies.append(pltpu.make_async_copy(part.at[side, b], place, sem))
-    for copy in copies:
-        copy.start()
+                pltpu.make_async_copy(part.at[side, b], place, sem).start()
     pltpu.make_async_copy(out_ref, out_ref, sem).wait()
 
 
@@ -117,12 +126,12 @@
     hbm = pl.BlockSpec(memory_space=pl.ANY)
     return pl.pallas_call(
         arrange,
-        out_shape=jax.ShapeDtypeStruct((replicas, sides, len(parts), rows, width), parts[0].dtype),
+        out_shape=jax.ShapeDtypeStruct((replicas, sides, LENGTH, rows, width), parts[0].dtype),
         in_specs=[pl.BlockSpec(memory_space=pltpu.SMEM)] + [hbm] * len(parts),
         out_specs=hbm,
         scratch_shapes=[pltpu.SemaphoreType.DMA],
         compiler_params=pltpu.CompilerParams(vmem_limit_bytes=1024 * 1024),
-        cost_estimate=cost(0, 4 * len(parts) * parts[0].size),
+        cost_estimate=cost(0, 4 * LENGTH * parts[0].size),
     )(place, *parts)
 
 
@@ -245,7 +254,7 @@
     mine = rows // replicas
     rank = lax.axis_index("rep")
     bf16, f32 = jnp.bfloat16, jnp.float32
-    length = shards // SIDES
+    length = LENGTH
     shard = lax.axis_index("fsdp")
 
     def swapped(value, axis, bit):
@@ -257,7 +266,7 @@
         return lax.ppermute(value, "fsdp", pairs)
 
     own_features, width = policy_key.shape
-    keep, give = split_columns(rank, ref_qkv, policy_key)
+    keep, give = split_columns(rank, in_hbm(ref_qkv), in_hbm(policy_key))
     got = swapped(give, "rep", 1)
     other = swapped(tokens, "rep", 1)
     copies = jax.ShapeDtypeStruct((shards, own_features, 7 * HD), bf16)
@@ -269,13 +278,12 @@
         column = jnp.concatenate([column, lax.ppermute(column, "rep", pairs)])
     gathered = exchanged(copies, "fsdp").reshape(features, -1)
     both = jnp.stack([column, swapped(column, "fsdp", length)])
-    up, down = [both], [both]
-    for k in range(1, length // 2 + 1):
-        up.append(passed(up[-1], 1))
-        if k < length // 2 or length == 1:
-            down.append(passed(down[-1], -1))
+    up, down = passed(both, 1), passed(both, -1)
+    across = passed(both, length // 2)
+    ups = passed(jnp.stack([both, up]), 2)
+    downs = passed(jnp.stack([both, down]), -2)
     place = jnp.stack([shard % length, shard // length, rank]).astype(jnp.int32)
-    whole = arranged(place, up + down[:0:-1]).reshape(-1, width)
+    whole = arranged(place, [both, up, across, down, ups, downs]).reshape(-1, width)
 
     seg = segment_ids[0]
     start = rank * mine
@@ -290,7 +298,7 @@
     bias = ref_bias.reshape(SHARE + 2, HD)
 
     part = jax.ShapeDtypeStruct((replicas, 7 * mine // 2, HD), bf16)
-    part = call(project, (part,), 4 * rows * features * 4 * HD, tokens, other, gathered)
+    part = call(project, (part,), 4 * rows * features * 4 * HD, tokens, other, in_hbm(gathered))
     part = exchanged(part, "rep")
     my_kv = call(
         keys_and_values,

time: 151 us -> 154 us (1.020)
  waiting for transfers between devices: 56.6 us -> 59.9 us
    ppermute x7 -> x5, waiting for transfers between devices: 13.1 us -> 16.6 us  [passed(): return lax.ppermute(value, 'fsdp', pairs)]
    ppermute x7 -> x5, starting transfers between devices: 22.7 us -> 21.6 us  [passed(): return lax.ppermute(value, 'fsdp', pairs)]
  transfers between devices with their start and end apart: 15 -> 13, of which waited for: 10 -> 8; matrix products, arithmetic and copies ran while one was open for 1% -> 1% of each run, Pallas kernels for 2% -> 2%
where the time goes in v7:
time: 154 us
  starting transfers between devices  75.8 us (49%)
  waiting for transfers between devices  59.9 us (39%)
  Pallas kernels  12 us (8%)
  local copies, waits for them, and re-layouts  3.56 us (2%)
    ppermute x3, waiting for transfers between devices, swapped(): return lax.ppermute(value, axis, pairs)  32.3 us
    all_to_all x3, starting transfers between devices, exchanged(): return lax.all_to_all(blocks, axis, split_axis=0, concat_axis=0, tiled=True)  28.1 us
    ppermute x5, starting transfers between devices, passed(): return lax.ppermute(value, 'fsdp', pairs)  21.6 us
    ppermute x5, waiting for transfers between devices, passed(): return lax.ppermute(value, 'fsdp', pairs)  16.6 us
    ppermute x2, starting transfers between devices, body(): column = jnp.concatenate([column, lax.ppermute(column, 'rep', pairs)])  13.7 us
    ppermute x3, starting transfers between devices, swapped(): return lax.ppermute(value, axis, pairs)  12.5 us
    ppermute x2, waiting for transfers between devices, body(): column = jnp.concatenate([column, lax.ppermute(column, 'rep', pairs)])  11 us
    pallas_call x5, Pallas kernels, call(): pl.pallas_call(kernel, out_shape=outs if len(outs) > 1 else outs[0], in_s...  9.25 us
  transfers between devices with their start and end apart: 13, of which 8 were waited for; matrix products, arithmetic and copies ran while one was open for 1% of the time, Pallas kernels for 2%

profile of v7, /device:TPU:32, one launch (start us, length us, event | category | flops | bytes accessed | tf_op | source)
XLA Modules:
  0.0 153.7 jit_solution(16487586273645691287)
XLA Ops:
  0.6 0.0 copy-start.2
  0.6 1.1 shard_map.68
  1.7 5.2 %collective-permute-start.1 = (bf16[40,576]{1,0:T(8,128)(2,1)S(1)}, bf16[40,576]{1,0:T(8,128)(2,1)S(1)}, u32[]{:S(2)}, u32[]{:S(2)}) collective-permute-start(bf16[40,576]{1,0:T(8,128)(2,1)S(1)} %get-tuple-element.9), channel_id=1, source_target_pairs={{0,1},{1,0},{2,3},{3,2},{4,5},{5,4},{6,7},{7,6},{8,9},{9,8},{10,11... | collective-permute-start | bytes 138248 | tf_op jit(solution)/shard_map/ppermute | solution.py:262
  6.9 2.1 %collective-permute-done.1.got_ref = bf16[40,576]{1,0:T(8,128)(2,1)S(1)} collective-permute-done((bf16[40,576]{1,0:T(8,128)(2,1)S(1)}, bf16[40,576]{1,0:T(8,128)(2,1)S(1)}, u32[]{:S(2)}, u32[]{:S(2)}) %collective-permute-start.1) | collective-permute-done | bytes 46112 | tf_op jit(solution)/shard_map/ppermute | solution.py:262
  9.0 1.2 shard_map.69
  10.2 8.0 %all-to-all-start = ((bf16[16,40,896]{2,1,0:T(8,128)(2,1)}), bf16[16,40,896]{2,1,0:T(8,128)(2,1)S(1)}, u32[]{:S(2)}, u32[]{:S(2)}) async-start(bf16[16,40,896]{2,1,0:T(8,128)(2,1)} %get-tuple-element.10), calls=%async_computation | async-start | bytes 2293760 | tf_op jit(solution)/shard_map/all_to_all | solution.py:19
  18.2 0.0 copy-done.2
  18.2 3.9 %collective-permute-start = (bf16[1024,640]{1,0:T(8,128)(2,1)S(1)}, bf16[1024,640]{1,0:T(8,128)(2,1)S(1)}, u32[]{:S(2)}, u32[]{:S(2)}) collective-permute-start(bf16[1024,640]{1,0:T(8,128)(2,1)S(1)} %copy-done.2), channel_id=1, source_target_pairs={{0,1},{1,0},{2,3},{3,2},{4,5},{5,4},{6,7},{7,6},{8,9},{9,8},{10,11... | collective-permute-start | bytes 3932168 | tf_op jit(solution)/shard_map/ppermute | solution.py:262
  22.1 27.3 %collective-permute-done.other_ref = bf16[1024,640]{1,0:T(8,128)(2,1)S(1)} collective-permute-done((bf16[1024,640]{1,0:T(8,128)(2,1)S(1)}, bf16[1024,640]{1,0:T(8,128)(2,1)S(1)}, u32[]{:S(2)}, u32[]{:S(2)}) %collective-permute-start) | collective-permute-done | bytes 1310752 | tf_op jit(solution)/shard_map/ppermute | solution.py:262
  49.5 0.0 copy-start.3
  49.5 1.1 copy-done.3
  50.5 0.0 all-to-all-done
  50.5 0.0 copy-start.5
  50.5 1.0 copy-done.5
  51.6 0.0 copy-start.4
  51.6 1.3 copy-done.4
  52.9 4.1 %shard_map.70 = bf16[8,448,128]{2,1,0:T(8,128)(2,1)} custom-call(bf16[1024,640]{1,0:T(8,128)(2,1)S(1)} %copy-done.2, bf16[1024,640]{1,0:T(8,128)(2,1)S(1)} %copy-done.4, bf16[640,896]{1,0:T(8,128)(2,1)} %bitcast.25), custom_call_target="tpu_custom_call" | custom-call | flops 1342177280 | bytes 4685824 | tf_op jit(solution)/shard_map/pallas_call | solution.py:34
  57.0 0.0 copy-start
  57.0 0.0 copy-start.1
  57.0 15.3 %all-to-all-start.1 = ((bf16[8,448,128]{2,1,0:T(8,128)(2,1)}), bf16[8,448,128]{2,1,0:T(8,128)(2,1)S(1)}, u32[]{:S(2)}, u32[]{:S(2)}) async-start(bf16[8,448,128]{2,1,0:T(8,128)(2,1)} %shard_map.70), calls=%async_computation.1 | async-start | bytes 1835008 | tf_op jit(solution)/shard_map/all_to_all | solution.py:19
  72.2 0.0 copy-done
  72.3 0.2 convert_reduce_fusion
  72.5 0.3 fusion
  72.8 0.1 pad_maximum_fusion.3
  72.9 6.0 %collective-permute-start.2 = (bf16[2,40,128]{2,1,0:T(8,128)(2,1)S(1)}, bf16[2,40,128]{2,1,0:T(8,128)(2,1)S(1)}, u32[]{:S(2)}, u32[]{:S(2)}) collective-permute-start(bf16[2,40,128]{2,1,0:T(8,128)(2,1)S(1)} %get-tuple-element.13), channel_id=1, source_target_pairs={{2,0},{7,1},{4,2},{1,3},{6,4},{3,5},{0,6},{5,7},{10,8},{15,9},{12,... | collective-permute-start | bytes 61448 | tf_op jit(solution)/shard_map/ppermute | solution.py:278
  79.0 11.0 %collective-permute-done.2 = bf16[2,40,128]{2,1,0:T(8,128)(2,1)S(1)} collective-permute-done((bf16[2,40,128]{2,1,0:T(8,128)(2,1)S(1)}, bf16[2,40,128]{2,1,0:T(8,128)(2,1)S(1)}, u32[]{:S(2)}, u32[]{:S(2)}) %collective-permute-start.2) | collective-permute-done | bytes 20512 | tf_op jit(solution)/shard_map/ppermute | solution.py:278
  90.0 7.6 %collective-permute-start.3 = (bf16[4,40,128]{2,1,0:T(8,128)(2,1)S(1)}, bf16[4,40,128]{2,1,0:T(8,128)(2,1)S(1)}, u32[]{:S(2)}, u32[]{:S(2)}) collective-permute-start(bf16[4,40,128]{2,1,0:T(8,128)(2,1)S(1)} %pad_maximum_fusion.5), channel_id=1, source_target_pairs={{4,0},{5,1},{6,2},{7,3},{0,4},{1,5},{2,6},{3,7},{12,8},{13,9},{14,... | collective-permute-start | bytes 122888 | tf_op jit(solution)/shard_map/ppermute | solution.py:278
  97.6 0.0 all-to-all-done.1.part_ref
  97.6 0.0 copy-done.1
  97.7 0.9 shard_map.72
  98.6 4.8 %all-to-all-start.2 = ((bf16[8,256,128]{2,1,0:T(8,128)(2,1)}), bf16[8,256,128]{2,1,0:T(8,128)(2,1)S(1)}, u32[]{:S(2)}, u32[]{:S(2)}) async-start(bf16[8,256,128]{2,1,0:T(8,128)(2,1)} %shard_map.72), calls=%async_computation.2 | async-start | bytes 1048576 | tf_op jit(solution)/shard_map/all_to_all | solution.py:19
  103.4 0.0 collective-permute-done.3
  103.4 3.4 %collective-permute-start.4 = (bf16[8,40,128]{2,1,0:T(8,128)(2,1)S(1)}, bf16[8,40,128]{2,1,0:T(8,128)(2,1)S(1)}, u32[]{:S(2)}, u32[]{:S(2)}) collective-permute-start(bf16[8,40,128]{2,1,0:T(8,128)(2,1)S(1)} %constant_dynamic-update-slice_fusion), channel_id=1, source_target_pairs={{0,512},{64,576},{128,640},{192,704},{256,768},{320,832},{384,896}... | collective-permute-start | bytes 245768 | tf_op jit(solution)/shard_map/ppermute | solution.py:262
  106.8 2.9 %collective-permute-done.4 = bf16[8,40,128]{2,1,0:T(8,128)(2,1)S(1)} collective-permute-done((bf16[8,40,128]{2,1,0:T(8,128)(2,1)S(1)}, bf16[8,40,128]{2,1,0:T(8,128)(2,1)S(1)}, u32[]{:S(2)}, u32[]{:S(2)}) %collective-permute-start.4) | collective-permute-done | bytes 81952 | tf_op jit(solution)/shard_map/ppermute | solution.py:262
  109.8 3.4 %collective-permute-start.5 = (bf16[2,8,40,128]{3,2,1,0:T(8,128)(2,1)S(1)}, bf16[2,8,40,128]{3,2,1,0:T(8,128)(2,1)S(1)}, u32[]{:S(2)}, u32[]{:S(2)}) collective-permute-start(bf16[2,8,40,128]{3,2,1,0:T(8,128)(2,1)S(1)} %get-tuple-element.17.own_ref), channel_id=1, source_target_pairs={{0,64},{64,128},{128,192},{192,256},{256,320},{320,384},{384,448},... | collective-permute-start | bytes 491528 | tf_op jit(solution)/shard_map/ppermute | solution.py:266
  113.2 3.7 %collective-permute-start.7 = (bf16[2,8,40,128]{3,2,1,0:T(8,128)(2,1)S(1)}, bf16[2,8,40,128]{3,2,1,0:T(8,128)(2,1)S(1)}, u32[]{:S(2)}, u32[]{:S(2)}) collective-permute-start(bf16[2,8,40,128]{3,2,1,0:T(8,128)(2,1)S(1)} %get-tuple-element.17.own_ref), channel_id=1, source_target_pairs={{0,448},{64,0},{128,64},{192,128},{256,192},{320,256},{384,320},{4... | collective-permute-start | bytes 491528 | tf_op jit(solution)/shard_map/ppermute | solution.py:266
  116.9 1.4 collective-permute-done.5.up_ref
  118.2 2.2 %collective-permute-done.7.down_ref = bf16[2,8,40,128]{3,2,1,0:T(8,128)(2,1)S(1)} collective-permute-done((bf16[2,8,40,128]{3,2,1,0:T(8,128)(2,1)S(1)}, bf16[2,8,40,128]{3,2,1,0:T(8,128)(2,1)S(1)}, u32[]{:S(2)}, u32[]{:S(2)}) %collective-permute-start.7) | collective-permute-done | bytes 163872 | tf_op jit(solution)/shard_map/ppermute | solution.py:266
  120.4 0.8 pad_maximum_fusion
  121.2 4.9 %collective-permute-start.8 = (bf16[2,2,8,40,128]{4,3,2,1,0:T(8,128)(2,1)}, bf16[2,2,8,40,128]{4,3,2,1,0:T(8,128)(2,1)S(1)}, u32[]{:S(2)}, u32[]{:S(2)}) collective-permute-start(bf16[2,2,8,40,128]{4,3,2,1,0:T(8,128)(2,1)} %get-tuple-element.15), channel_id=1, source_target_pairs={{0,128},{64,192},{128,256},{192,320},{256,384},{320,448},{384,0},{... | collective-permute-start | bytes 983048 | tf_op jit(solution)/shard_map/ppermute | solution.py:266
  126.1 3.0 %collective-permute-start.9 = (bf16[2,2,8,40,128]{4,3,2,1,0:T(8,128)(2,1)S(1)}, bf16[2,2,8,40,128]{4,3,2,1,0:T(8,128)(2,1)S(1)}, u32[]{:S(2)}, u32[]{:S(2)}) collective-permute-start(bf16[2,2,8,40,128]{4,3,2,1,0:T(8,128)(2,1)S(1)} %get-tuple-element.14), channel_id=1, source_target_pairs={{0,384},{64,448},{128,0},{192,64},{256,128},{320,192},{384,256},{4... | collective-permute-start | bytes 983048 | tf_op jit(solution)/shard_map/ppermute | solution.py:266
  129.1 6.6 %collective-permute-start.6 = (bf16[2,8,40,128]{3,2,1,0:T(8,128)(2,1)S(1)}, bf16[2,8,40,128]{3,2,1,0:T(8,128)(2,1)S(1)}, u32[]{:S(2)}, u32[]{:S(2)}) collective-permute-start(bf16[2,8,40,128]{3,2,1,0:T(8,128)(2,1)S(1)} %get-tuple-element.17.own_ref), channel_id=1, source_target_pairs={{0,256},{64,320},{128,384},{192,448},{256,0},{320,64},{384,128},{4... | collective-permute-start | bytes 491528 | tf_op jit(solution)/shard_map/ppermute | solution.py:266
  135.7 0.1 copy.8.mine_ref
  135.9 0.1 pad_add_fusion.place_ref
  135.9 11.2 %collective-permute-done.6.across_ref = bf16[2,8,40,128]{3,2,1,0:T(8,128)(2,1)S(1)} collective-permute-done((bf16[2,8,40,128]{3,2,1,0:T(8,128)(2,1)S(1)}, bf16[2,8,40,128]{3,2,1,0:T(8,128)(2,1)S(1)}, u32[]{:S(2)}, u32[]{:S(2)}) %collective-permute-start.6) | collective-permute-done | bytes 163872 | tf_op jit(solution)/shard_map/ppermute | solution.py:266
  147.1 0.0 collective-permute-done.8.ups_ref
  147.1 1.9 %collective-permute-done.9.downs_ref = bf16[2,2,8,40,128]{4,3,2,1,0:T(8,128)(2,1)S(1)} collective-permute-done((bf16[2,2,8,40,128]{4,3,2,1,0:T(8,128)(2,1)S(1)}, bf16[2,2,8,40,128]{4,3,2,1,0:T(8,128)(2,1)S(1)}, u32[]{:S(2)}, u32[]{:S(2)}) %collective-permute-start.9) | collective-permute-done | bytes 327712 | tf_op jit(solution)/shard_map/ppermute | solution.py:266
  149.0 1.6 %shard_map.74 = bf16[8,2,8,40,128]{4,3,2,1,0:T(8,128)(2,1)} custom-call(s32[3]{0:T(128)S(1)} %pad_add_fusion.place_ref, bf16[2,8,40,128]{3,2,1,0:T(8,128)(2,1)S(1)} %get-tuple-element.17.own_ref, bf16[2,8,40,128]{3,2,1,0:T(8,128)(2,1)S(1)} %collective-permute-done.5.up_ref, bf16[2,8,40,128]{3,2,1,0:T(8,128)(2,1)S(1)} %collective-permute-done.6.across_ref, ...), custom_call_target="tpu_custom_call" | custom-call | bytes 2621440 | tf_op jit(solution)/shard_map/pallas_call | solution.py:127
  150.6 0.3 shard_map.71
  150.9 0.0 all-to-all-done.2.kv_ref
  150.9 2.8 %shard_map.73 = bf16[128,640]{1,0:T(8,128)(2,1)} custom-call(s32[1]{0:T(128)} %bitcast.rank_ref, bf16[5,128,128]{2,1,0:T(8,128)(2,1)S(1)} %get-tuple-element.11.q_ref, f32[128,640]{1,0:T(8,128)S(1)} %get-tuple-element.12.mask_ref, bf16[8,256,128]{2,1,0:T(8,128)(2,1)S(1)} %all-to-all-done.2.kv_ref), custom_call_target="tpu_custom_call" | custom-call | flops 209715200 | bytes 1179652 | tf_op jit(solution)/shard_map/pallas_call | solution.py:34
  (8 shorter events, 0.1 us)
Async XLA Ops:
  0.6 17.6 %copy-start.2 = (bf16[1024,640]{1,0:T(8,128)(2,1)S(1)}, bf16[1024,640]{1,0:T(8,128)(2,1)}, u32[]{:S(2)}) copy-start(bf16[1024,640]{1,0:T(8,128)(2,1)} %own_ref.1) | copy-start | bytes 3932164
  1.7 7.3 %collective-permute-start.1 = (bf16[40,576]{1,0:T(8,128)(2,1)S(1)}, bf16[40,576]{1,0:T(8,128)(2,1)S(1)}, u32[]{:S(2)}, u32[]{:S(2)}) collective-permute-start(bf16[40,576]{1,0:T(8,128)(2,1)S(1)} %get-tuple-element.9), channel_id=1, source_target_pairs={{0,1},{1,0},{2,3},{3,2},{4,5},{5,4},{6,7},{7,6},{8,9},{9,8},{10,11... | collective-permute-start | bytes 138248 | tf_op jit(solution)/shard_map/ppermute | solution.py:262
  10.2 40.3 %all-to-all-start = ((bf16[16,40,896]{2,1,0:T(8,128)(2,1)}), bf16[16,40,896]{2,1,0:T(8,128)(2,1)S(1)}, u32[]{:S(2)}, u32[]{:S(2)}) async-start(bf16[16,40,896]{2,1,0:T(8,128)(2,1)} %get-tuple-element.10), calls=%async_computation | async-start | bytes 2293760 | tf_op jit(solution)/shard_map/all_to_all | solution.py:19
  18.2 31.3 %collective-permute-start = (bf16[1024,640]{1,0:T(8,128)(2,1)S(1)}, bf16[1024,640]{1,0:T(8,128)(2,1)S(1)}, u32[]{:S(2)}, u32[]{:S(2)}) collective-permute-start(bf16[1024,640]{1,0:T(8,128)(2,1)S(1)} %copy-done.2), channel_id=1, source_target_pairs={{0,1},{1,0},{2,3},{3,2},{4,5},{5,4},{6,7},{7,6},{8,9},{9,8},{10,11... | collective-permute-start | bytes 3932168 | tf_op jit(solution)/shard_map/ppermute | solution.py:262
  49.5 1.1 copy-start.3
  50.5 1.0 copy-start.5
  51.6 1.3 copy-start.4
  57.0 15.3 %copy-start = (s32[1,1024]{1,0:T(1,128)S(1)}, s32[1,1024]{1,0:T(1,128)}, u32[]{:S(2)}) copy-start(s32[1,1024]{1,0:T(1,128)} %param.8) | copy-start | bytes 12292
  57.0 40.7 %copy-start.1 = (f32[896]{0:T(1024)S(1)}, f32[896]{0:T(1024)}, u32[]{:S(2)}) copy-start(f32[896]{0:T(1024)} %param.7) | copy-start | bytes 10756
  57.0 40.7 %all-to-all-start.1 = ((bf16[8,448,128]{2,1,0:T(8,128)(2,1)}), bf16[8,448,128]{2,1,0:T(8,128)(2,1)S(1)}, u32[]{:S(2)}, u32[]{:S(2)}) async-start(bf16[8,448,128]{2,1,0:T(8,128)(2,1)} %shard_map.70), calls=%async_computation.1 | async-start | bytes 1835008 | tf_op jit(solution)/shard_map/all_to_all | solution.py:19
  72.9 17.1 %collective-permute-start.2 = (bf16[2,40,128]{2,1,0:T(8,128)(2,1)S(1)}, bf16[2,40,128]{2,1,0:T(8,128)(2,1)S(1)}, u32[]{:S(2)}, u32[]{:S(2)}) collective-permute-start(bf16[2,40,128]{2,1,0:T(8,128)(2,1)S(1)} %get-tuple-element.13), channel_id=1, source_target_pairs={{2,0},{7,1},{4,2},{1,3},{6,4},{3,5},{0,6},{5,7},{10,8},{15,9},{12,... | collective-permute-start | bytes 61448 | tf_op jit(solution)/shard_map/ppermute | solution.py:278
  90.0 13.4 %collective-permute-start.3 = (bf16[4,40,128]{2,1,0:T(8,128)(2,1)S(1)}, bf16[4,40,128]{2,1,0:T(8,128)(2,1)S(1)}, u32[]{:S(2)}, u32[]{:S(2)}) collective-permute-start(bf16[4,40,128]{2,1,0:T(8,128)(2,1)S(1)} %pad_maximum_fusion.5), channel_id=1, source_target_pairs={{4,0},{5,1},{6,2},{7,3},{0,4},{1,5},{2,6},{3,7},{12,8},{13,9},{14,... | collective-permute-start | bytes 122888 | tf_op jit(solution)/shard_map/ppermute | solution.py:278
  98.6 52.3 %all-to-all-start.2 = ((bf16[8,256,128]{2,1,0:T(8,128)(2,1)}), bf16[8,256,128]{2,1,0:T(8,128)(2,1)S(1)}, u32[]{:S(2)}, u32[]{:S(2)}) async-start(bf16[8,256,128]{2,1,0:T(8,128)(2,1)} %shard_map.72), calls=%async_computation.2 | async-start | bytes 1048576 | tf_op jit(solution)/shard_map/all_to_all | solution.py:19
  103.4 6.3 %collective-permute-start.4 = (bf16[8,40,128]{2,1,0:T(8,128)(2,1)S(1)}, bf16[8,40,128]{2,1,0:T(8,128)(2,1)S(1)}, u32[]{:S(2)}, u32[]{:S(2)}) collective-permute-start(bf16[8,40,128]{2,1,0:T(8,128)(2,1)S(1)} %constant_dynamic-update-slice_fusion), channel_id=1, source_target_pairs={{0,512},{64,576},{128,640},{192,704},{256,768},{320,832},{384,896}... | collective-permute-start | bytes 245768 | tf_op jit(solution)/shard_map/ppermute | solution.py:262
  109.8 8.4 %collective-permute-start.5 = (bf16[2,8,40,128]{3,2,1,0:T(8,128)(2,1)S(1)}, bf16[2,8,40,128]{3,2,1,0:T(8,128)(2,1)S(1)}, u32[]{:S(2)}, u32[]{:S(2)}) collective-permute-start(bf16[2,8,40,128]{3,2,1,0:T(8,128)(2,1)S(1)} %get-tuple-element.17.own_ref), channel_id=1, source_target_pairs={{0,64},{64,128},{128,192},{192,256},{256,320},{320,384},{384,448},... | collective-permute-start | bytes 491528 | tf_op jit(solution)/shard_map/ppermute | solution.py:266
  113.2 7.2 %collective-permute-start.7 = (bf16[2,8,40,128]{3,2,1,0:T(8,128)(2,1)S(1)}, bf16[2,8,40,128]{3,2,1,0:T(8,128)(2,1)S(1)}, u32[]{:S(2)}, u32[]{:S(2)}) collective-permute-start(bf16[2,8,40,128]{3,2,1,0:T(8,128)(2,1)S(1)} %get-tuple-element.17.own_ref), channel_id=1, source_target_pairs={{0,448},{64,0},{128,64},{192,128},{256,192},{320,256},{384,320},{4... | collective-permute-start | bytes 491528 | tf_op jit(solution)/shard_map/ppermute | solution.py:266
  121.2 25.9 %collective-permute-start.8 = (bf16[2,2,8,40,128]{4,3,2,1,0:T(8,128)(2,1)}, bf16[2,2,8,40,128]{4,3,2,1,0:T(8,128)(2,1)S(1)}, u32[]{:S(2)}, u32[]{:S(2)}) collective-permute-start(bf16[2,2,8,40,128]{4,3,2,1,0:T(8,128)(2,1)} %get-tuple-element.15), channel_id=1, source_target_pairs={{0,128},{64,192},{128,256},{192,320},{256,384},{320,448},{384,0},{... | collective-permute-start | bytes 983048 | tf_op jit(solution)/shard_map/ppermute | solution.py:266
  126.1 22.9 %collective-permute-start.9 = (bf16[2,2,8,40,128]{4,3,2,1,0:T(8,128)(2,1)S(1)}, bf16[2,2,8,40,128]{4,3,2,1,0:T(8,128)(2,1)S(1)}, u32[]{:S(2)}, u32[]{:S(2)}) collective-permute-start(bf16[2,2,8,40,128]{4,3,2,1,0:T(8,128)(2,1)S(1)} %get-tuple-element.14), channel_id=1, source_target_pairs={{0,384},{64,448},{128,0},{192,64},{256,128},{320,192},{384,256},{4... | collective-permute-start | bytes 983048 | tf_op jit(solution)/shard_map/ppermute | solution.py:266
  129.1 18.0 %collective-permute-start.6 = (bf16[2,8,40,128]{3,2,1,0:T(8,128)(2,1)S(1)}, bf16[2,8,40,128]{3,2,1,0:T(8,128)(2,1)S(1)}, u32[]{:S(2)}, u32[]{:S(2)}) collective-permute-start(bf16[2,8,40,128]{3,2,1,0:T(8,128)(2,1)S(1)} %get-tuple-element.17.own_ref), channel_id=1, source_target_pairs={{0,256},{64,320},{128,384},{192,448},{256,0},{320,64},{384,128},{4... | collective-permute-start | bytes 491528 | tf_op jit(solution)/shard_map/ppermute | solution.py:266

commit v8 on v6

--- a/solution.py
+++ b/solution.py
@@ -17,6 +17,10 @@
 
 def exchanged(blocks, axis):
     return lax.all_to_all(blocks, axis, split_axis=0, concat_axis=0, tiled=True)
+
+
+def in_hbm(array):
+    return pltpu.with_memory_space_constraint(array, pltpu.HBM)
 
 
 def cost(flops, moved):
@@ -80,7 +84,7 @@
             pltpu.VMEM(policy.shape, policy.dtype),
             pltpu.SemaphoreType.DMA((2,)),
         ],
-        compiler_params=pltpu.CompilerParams(vmem_limit_bytes=67_000_000),
+        compiler_params=pltpu.CompilerParams(vmem_limit_bytes=4 * 1024 * 1024),
         cost_estimate=cost(0, 8 * w.size),
     )(rank.reshape(1), w, policy)
 
@@ -126,10 +130,19 @@
     )(place, *parts)
 
 
-def project(own_ref, other_ref, w_ref, out_ref):
+def project(own_hbm, other_hbm, w_ref, out_ref, own_ref, other_ref, sems):
     blocks = out_ref.shape[0]
-    rows = own_ref.shape[0]
+    rows = own_hbm.shape[0]
     step = rows // 2
+    loads = []
+    for part in range(2):
+        span = pl.ds(part * step, step)
+        for side, (source, target) in enumerate([(own_hbm, own_ref), (other_hbm, other_ref)]):
+            loads.append(
+                pltpu.make_async_copy(source.at[span], target.at[span], sems.at[2 * part + side])
+            )
+    for load in loads:
+        load.start()
     shared = w_ref[:, 3 * HD : 4 * HD]
     w_own = w_ref[:, : 4 * HD]
     swapped = pltpu.roll(shared.astype(jnp.float32), HALF, 1).astype(jnp.bfloat16)
@@ -138,6 +151,8 @@
     low = lanes_below_half((size // 2, HD))
     for part in range(2):
         at = part * step
+        loads[2 * part].wait()
+        loads[2 * part + 1].wait()
         value = jnp.dot(own_ref[at : at + step, :], w_own, preferred_element_type=jnp.float32)
         value = value + jnp.dot(
             other_ref[at : at + step, :], w_other, preferred_element_type=jnp.float32
@@ -152,6 +167,25 @@
             last = piece[:, 3 * HD :]
             packed = jnp.where(low, last[: size // 2], pltpu.roll(last[size // 2 :], HALF, 1))
             out_ref[j, 3 * size :] = packed.astype(jnp.bfloat16)
+
+
+def projected(own, other, gathered, blocks):
+    rows, features = own.shape
+    vmem = pl.BlockSpec(memory_space=pltpu.VMEM)
+    hbm = pl.BlockSpec(memory_space=pltpu.HBM)
+    return pl.pallas_call(
+        project,
+        out_shape=jax.ShapeDtypeStruct((blocks, 7 * rows // blocks // 2, HD), jnp.bfloat16),
+        in_specs=[hbm, hbm, vmem],
+        out_specs=vmem,
+        scratch_shapes=[
+            pltpu.VMEM(own.shape, own.dtype),
+            pltpu.VMEM(own.shape, own.dtype),
+            pltpu.SemaphoreType.DMA((4,)),
+        ],
+        compiler_params=pltpu.CompilerParams(vmem_limit_bytes=24 * 1024 * 1024),
+        cost_estimate=cost(4 * rows * features * 4 * HD, 4 * own.size + 2 * gathered.size),
+    )(in_hbm(own), in_hbm(other), gathered)
 
 
 def turned(value, cosine, sine):
@@ -257,7 +291,7 @@
         return lax.ppermute(value, "fsdp", pairs)
 
     own_features, width = policy_key.shape
-    keep, give = split_columns(rank, ref_qkv, policy_key)
+    keep, give = split_columns(rank, in_hbm(ref_qkv), in_hbm(policy_key))
     got = swapped(give, "rep", 1)
     other = swapped(tokens, "rep", 1)
     copies = jax.ShapeDtypeStruct((shards, own_features, 7 * HD), bf16)
@@ -289,8 +323,7 @@
     sine = jnp.concatenate([-sine, sine], axis=1)
     bias = ref_bias.reshape(SHARE + 2, HD)
 
-    part = jax.ShapeDtypeStruct((replicas, 7 * mine // 2, HD), bf16)
-    part = call(project, (part,), 4 * rows * features * 4 * HD, tokens, other, gathered)
+    part = projected(tokens, other, gathered, replicas)
     part = exchanged(part, "rep")
     my_kv = call(
         keys_and_values,

time: 151 us -> 148 us (0.980)
  local copies, waits for them, and re-layouts: 3.34 us -> 0.17 us
    pallas_call x0 -> x1, Pallas kernels: none -> 4.35 us  [projected(): pl.pallas_call(project, out_shape=jax.ShapeDtypeStruct((blocks, 7 * rows...]
    unnamed x14 -> x8, local copies, waits for them, and re-layouts: 3.2 us -> 0.03 us
    pallas_call x5 -> x4, Pallas kernels: 8.01 us -> 5.12 us  [call(): pl.pallas_call(kernel, out_shape=outs if len(outs) > 1 else outs[0], in_s...]
where the time goes in v8:
time: 148 us; the launch traced here: 147 us
  starting transfers between devices  76.8 us (52%)
  waiting for transfers between devices  56.5 us (38%)
  Pallas kernels  12.2 us (8%)
    ppermute x3, waiting for transfers between devices, swapped(): return lax.ppermute(value, axis, pairs)  32.4 us
    all_to_all x3, starting transfers between devices, exchanged(): return lax.all_to_all(blocks, axis, split_axis=0, concat_axis=0, tiled=True)  28 us
    ppermute x7, starting transfers between devices, passed(): return lax.ppermute(value, 'fsdp', pairs)  22.7 us
    ppermute x2, starting transfers between devices, body(): column = jnp.concatenate([column, lax.ppermute(column, 'rep', pairs)])  13.7 us
    ppermute x7, waiting for transfers between devices, passed(): return lax.ppermute(value, 'fsdp', pairs)  13.1 us
    ppermute x3, starting transfers between devices, swapped(): return lax.ppermute(value, axis, pairs)  12.5 us
    ppermute x2, waiting for transfers between devices, body(): column = jnp.concatenate([column, lax.ppermute(column, 'rep', pairs)])  11 us
    pallas_call x4, Pallas kernels, call(): pl.pallas_call(kernel, out_shape=outs if len(outs) > 1 else outs[0], in_s...  5.12 us
  transfers between devices with their start and end apart: 15, of which 10 were waited for; matrix products, arithmetic and copies ran while one was open for 1% of the time, Pallas kernels for 2%

profile of v8, /device:TPU:32, one launch (start us, length us, event | category | flops | bytes accessed | tf_op | source)
XLA Modules:
  0.0 147.4 jit_solution(11661197969392453930)
XLA Ops:
  0.6 0.0 copy-start.2
  0.6 1.1 shard_map.68
  1.8 5.2 %collective-permute-start.1 = (bf16[40,576]{1,0:T(8,128)(2,1)S(1)}, bf16[40,576]{1,0:T(8,128)(2,1)S(1)}, u32[]{:S(2)}, u32[]{:S(2)}) collective-permute-start(bf16[40,576]{1,0:T(8,128)(2,1)S(1)} %get-tuple-element.9), channel_id=1, source_target_pairs={{0,1},{1,0},{2,3},{3,2},{4,5},{5,4},{6,7},{7,6},{8,9},{9,8},{10,11... | collective-permute-start | bytes 138248 | tf_op jit(solution)/shard_map/ppermute | solution.py:287
  7.0 2.1 %collective-permute-done.1.got_ref = bf16[40,576]{1,0:T(8,128)(2,1)S(1)} collective-permute-done((bf16[40,576]{1,0:T(8,128)(2,1)S(1)}, bf16[40,576]{1,0:T(8,128)(2,1)S(1)}, u32[]{:S(2)}, u32[]{:S(2)}) %collective-permute-start.1) | collective-permute-done | bytes 46112 | tf_op jit(solution)/shard_map/ppermute | solution.py:287
  9.0 1.1 shard_map.69
  10.2 8.0 %all-to-all-start = ((bf16[16,40,896]{2,1,0:T(8,128)(2,1)}), bf16[16,40,896]{2,1,0:T(8,128)(2,1)S(1)}, u32[]{:S(2)}, u32[]{:S(2)}) async-start(bf16[16,40,896]{2,1,0:T(8,128)(2,1)} %get-tuple-element.10), calls=%async_computation | async-start | bytes 2293760 | tf_op jit(solution)/shard_map/all_to_all | solution.py:19
  18.2 0.0 copy-done.2
  18.2 3.9 %collective-permute-start = (bf16[1024,640]{1,0:T(8,128)(2,1)S(1)}, bf16[1024,640]{1,0:T(8,128)(2,1)}, u32[]{:S(2)}, u32[]{:S(2)}) collective-permute-start(bf16[1024,640]{1,0:T(8,128)(2,1)S(1)} %copy-done.2), channel_id=1, source_target_pairs={{0,1},{1,0},{2,3},{3,2},{4,5},{5,4},{6,7},{7,6},{8,9},{9,8},{10,11... | collective-permute-start | bytes 3932168 | tf_op jit(solution)/shard_map/ppermute | solution.py:287
  22.1 27.4 %collective-permute-done.other_hbm = bf16[1024,640]{1,0:T(8,128)(2,1)} collective-permute-done((bf16[1024,640]{1,0:T(8,128)(2,1)S(1)}, bf16[1024,640]{1,0:T(8,128)(2,1)}, u32[]{:S(2)}, u32[]{:S(2)}) %collective-permute-start) | collective-permute-done | bytes 1310752 | tf_op jit(solution)/shard_map/ppermute | solution.py:287
  49.5 0.0 all-to-all-done
  49.5 4.3 %shard_map.70 = bf16[8,448,128]{2,1,0:T(8,128)(2,1)} custom-call(bf16[1024,640]{1,0:T(8,128)(2,1)} %own_hbm.1, bf16[1024,640]{1,0:T(8,128)(2,1)} %collective-permute-done.other_hbm, bf16[640,896]{1,0:T(8,128)(2,1)S(1)} %bitcast.14), custom_call_target="tpu_custom_call" | custom-call | flops 1342177280 | bytes 3768320 | tf_op jit(solution)/shard_map/pallas_call | solution.py:176
  53.9 0.0 copy-start
  53.9 0.0 copy-start.1
  53.9 15.1 %all-to-all-start.1 = ((bf16[8,448,128]{2,1,0:T(8,128)(2,1)}), bf16[8,448,128]{2,1,0:T(8,128)(2,1)S(1)}, u32[]{:S(2)}, u32[]{:S(2)}) async-start(bf16[8,448,128]{2,1,0:T(8,128)(2,1)} %shard_map.70), calls=%async_computation.1 | async-start | bytes 1835008 | tf_op jit(solution)/shard_map/all_to_all | solution.py:19
  69.1 0.0 copy-done
  69.1 0.2 convert_reduce_fusion
  69.3 0.3 fusion
  69.6 0.1 pad_maximum_fusion.1
  69.7 6.0 %collective-permute-start.2 = (bf16[2,40,128]{2,1,0:T(8,128)(2,1)S(1)}, bf16[2,40,128]{2,1,0:T(8,128)(2,1)S(1)}, u32[]{:S(2)}, u32[]{:S(2)}) collective-permute-start(bf16[2,40,128]{2,1,0:T(8,128)(2,1)S(1)} %get-tuple-element.13), channel_id=1, source_target_pairs={{2,0},{7,1},{4,2},{1,3},{6,4},{3,5},{0,6},{5,7},{10,8},{15,9},{12,... | collective-permute-start | bytes 61448 | tf_op jit(solution)/shard_map/ppermute | solution.py:303
  75.8 11.0 %collective-permute-done.2 = bf16[2,40,128]{2,1,0:T(8,128)(2,1)S(1)} collective-permute-done((bf16[2,40,128]{2,1,0:T(8,128)(2,1)S(1)}, bf16[2,40,128]{2,1,0:T(8,128)(2,1)S(1)}, u32[]{:S(2)}, u32[]{:S(2)}) %collective-permute-start.2) | collective-permute-done | bytes 20512 | tf_op jit(solution)/shard_map/ppermute | solution.py:303
  86.8 7.6 %collective-permute-start.3 = (bf16[4,40,128]{2,1,0:T(8,128)(2,1)S(1)}, bf16[4,40,128]{2,1,0:T(8,128)(2,1)S(1)}, u32[]{:S(2)}, u32[]{:S(2)}) collective-permute-start(bf16[4,40,128]{2,1,0:T(8,128)(2,1)S(1)} %pad_maximum_fusion.3), channel_id=1, source_target_pairs={{4,0},{5,1},{6,2},{7,3},{0,4},{1,5},{2,6},{3,7},{12,8},{13,9},{14,... | collective-permute-start | bytes 122888 | tf_op jit(solution)/shard_map/ppermute | solution.py:303
  94.5 0.0 all-to-all-done.1.part_ref
  94.5 0.0 copy-done.1
  94.5 0.9 shard_map.72
  95.4 4.8 %all-to-all-start.2 = ((bf16[8,256,128]{2,1,0:T(8,128)(2,1)}), bf16[8,256,128]{2,1,0:T(8,128)(2,1)S(1)}, u32[]{:S(2)}, u32[]{:S(2)}) async-start(bf16[8,256,128]{2,1,0:T(8,128)(2,1)} %shard_map.72), calls=%async_computation.2 | async-start | bytes 1048576 | tf_op jit(solution)/shard_map/all_to_all | solution.py:19
  100.2 0.0 collective-permute-done.3
  100.3 3.4 %collective-permute-start.4 = (bf16[8,40,128]{2,1,0:T(8,128)(2,1)S(1)}, bf16[8,40,128]{2,1,0:T(8,128)(2,1)S(1)}, u32[]{:S(2)}, u32[]{:S(2)}) collective-permute-start(bf16[8,40,128]{2,1,0:T(8,128)(2,1)S(1)} %constant_dynamic-update-slice_fusion), channel_id=1, source_target_pairs={{0,512},{64,576},{128,640},{192,704},{256,768},{320,832},{384,896}... | collective-permute-start | bytes 245768 | tf_op jit(solution)/shard_map/ppermute | solution.py:287
  103.7 2.9 %collective-permute-done.4 = bf16[8,40,128]{2,1,0:T(8,128)(2,1)S(1)} collective-permute-done((bf16[8,40,128]{2,1,0:T(8,128)(2,1)S(1)}, bf16[8,40,128]{2,1,0:T(8,128)(2,1)S(1)}, u32[]{:S(2)}, u32[]{:S(2)}) %collective-permute-start.4) | collective-permute-done | bytes 81952 | tf_op jit(solution)/shard_map/ppermute | solution.py:287
  106.6 3.4 %collective-permute-start.5 = (bf16[2,8,40,128]{3,2,1,0:T(8,128)(2,1)S(1)}, bf16[2,8,40,128]{3,2,1,0:T(8,128)(2,1)S(1)}, u32[]{:S(2)}, u32[]{:S(2)}) collective-permute-start(bf16[2,8,40,128]{3,2,1,0:T(8,128)(2,1)S(1)} %pad_maximum_fusion.refs_0_), channel_id=1, source_target_pairs={{0,64},{64,128},{128,192},{192,256},{256,320},{320,384},{384,448},... | collective-permute-start | bytes 491528 | tf_op jit(solution)/shard_map/ppermute | solution.py:291
  110.0 3.6 %collective-permute-start.9 = (bf16[2,8,40,128]{3,2,1,0:T(8,128)(2,1)S(1)}, bf16[2,8,40,128]{3,2,1,0:T(8,128)(2,1)S(1)}, u32[]{:S(2)}, u32[]{:S(2)}) collective-permute-start(bf16[2,8,40,128]{3,2,1,0:T(8,128)(2,1)S(1)} %pad_maximum_fusion.refs_0_), channel_id=1, source_target_pairs={{0,448},{64,0},{128,64},{192,128},{256,192},{320,256},{384,320},{4... | collective-permute-start | bytes 491528 | tf_op jit(solution)/shard_map/ppermute | solution.py:291
  113.7 1.4 collective-permute-done.5.refs_1_
  115.0 2.9 %collective-permute-start.6 = (bf16[2,8,40,128]{3,2,1,0:T(8,128)(2,1)S(1)}, bf16[2,8,40,128]{3,2,1,0:T(8,128)(2,1)S(1)}, u32[]{:S(2)}, u32[]{:S(2)}) collective-permute-start(bf16[2,8,40,128]{3,2,1,0:T(8,128)(2,1)S(1)} %collective-permute-done.5.refs_1_), channel_id=1, source_target_pairs={{0,64},{64,128},{128,192},{192,256},{256,320},{320,384},{384,448},... | collective-permute-start | bytes 491528 | tf_op jit(solution)/shard_map/ppermute | solution.py:291
  118.0 0.3 collective-permute-done.9.refs_7_
  118.2 3.8 %collective-permute-start.10 = (bf16[2,8,40,128]{3,2,1,0:T(8,128)(2,1)S(1)}, bf16[2,8,40,128]{3,2,1,0:T(8,128)(2,1)S(1)}, u32[]{:S(2)}, u32[]{:S(2)}) collective-permute-start(bf16[2,8,40,128]{3,2,1,0:T(8,128)(2,1)S(1)} %collective-permute-done.9.refs_7_), channel_id=1, source_target_pairs={{0,448},{64,0},{128,64},{192,128},{256,192},{320,256},{384,320},{4... | collective-permute-start | bytes 491528 | tf_op jit(solution)/shard_map/ppermute | solution.py:291
  122.1 2.0 %collective-permute-done.6.refs_2_ = bf16[2,8,40,128]{3,2,1,0:T(8,128)(2,1)S(1)} collective-permute-done((bf16[2,8,40,128]{3,2,1,0:T(8,128)(2,1)S(1)}, bf16[2,8,40,128]{3,2,1,0:T(8,128)(2,1)S(1)}, u32[]{:S(2)}, u32[]{:S(2)}) %collective-permute-start.6) | collective-permute-done | bytes 163872 | tf_op jit(solution)/shard_map/ppermute | solution.py:291
  124.1 2.4 %collective-permute-start.7 = (bf16[2,8,40,128]{3,2,1,0:T(8,128)(2,1)S(1)}, bf16[2,8,40,128]{3,2,1,0:T(8,128)(2,1)S(1)}, u32[]{:S(2)}, u32[]{:S(2)}) collective-permute-start(bf16[2,8,40,128]{3,2,1,0:T(8,128)(2,1)S(1)} %collective-permute-done.6.refs_2_), channel_id=1, source_target_pairs={{0,64},{64,128},{128,192},{192,256},{256,320},{320,384},{384,448},... | collective-permute-start | bytes 491528 | tf_op jit(solution)/shard_map/ppermute | solution.py:291
  126.6 0.4 collective-permute-done.10.refs_6_
  127.0 4.5 %collective-permute-start.11 = (bf16[2,8,40,128]{3,2,1,0:T(8,128)(2,1)S(1)}, bf16[2,8,40,128]{3,2,1,0:T(8,128)(2,1)S(1)}, u32[]{:S(2)}, u32[]{:S(2)}) collective-permute-start(bf16[2,8,40,128]{3,2,1,0:T(8,128)(2,1)S(1)} %collective-permute-done.10.refs_6_), channel_id=1, source_target_pairs={{0,448},{64,0},{128,64},{192,128},{256,192},{320,256},{384,320},{4... | collective-permute-start | bytes 491528 | tf_op jit(solution)/shard_map/ppermute | solution.py:291
  131.5 2.7 %collective-permute-done.7.refs_3_ = bf16[2,8,40,128]{3,2,1,0:T(8,128)(2,1)S(1)} collective-permute-done((bf16[2,8,40,128]{3,2,1,0:T(8,128)(2,1)S(1)}, bf16[2,8,40,128]{3,2,1,0:T(8,128)(2,1)S(1)}, u32[]{:S(2)}, u32[]{:S(2)}) %collective-permute-start.7) | collective-permute-done | bytes 163872 | tf_op jit(solution)/shard_map/ppermute | solution.py:291
  134.2 1.9 %collective-permute-start.8 = (bf16[2,8,40,128]{3,2,1,0:T(8,128)(2,1)S(1)}, bf16[2,8,40,128]{3,2,1,0:T(8,128)(2,1)S(1)}, u32[]{:S(2)}, u32[]{:S(2)}) collective-permute-start(bf16[2,8,40,128]{3,2,1,0:T(8,128)(2,1)S(1)} %collective-permute-done.7.refs_3_), channel_id=1, source_target_pairs={{0,64},{64,128},{128,192},{192,256},{256,320},{320,384},{384,448},... | collective-permute-start | bytes 491528 | tf_op jit(solution)/shard_map/ppermute | solution.py:291
  136.1 0.1 copy.8.mine_ref
  136.3 0.1 pad_add_fusion.place_ref
  136.4 0.0 collective-permute-done.11.refs_5_
  136.4 6.3 %collective-permute-done.8.refs_4_ = bf16[2,8,40,128]{3,2,1,0:T(8,128)(2,1)S(1)} collective-permute-done((bf16[2,8,40,128]{3,2,1,0:T(8,128)(2,1)S(1)}, bf16[2,8,40,128]{3,2,1,0:T(8,128)(2,1)S(1)}, u32[]{:S(2)}, u32[]{:S(2)}) %collective-permute-start.8) | collective-permute-done | bytes 163872 | tf_op jit(solution)/shard_map/ppermute | solution.py:291
  142.6 1.6 %shard_map.74 = bf16[8,2,8,40,128]{4,3,2,1,0:T(8,128)(2,1)} custom-call(s32[3]{0:T(128)S(1)} %pad_add_fusion.place_ref, bf16[2,8,40,128]{3,2,1,0:T(8,128)(2,1)S(1)} %pad_maximum_fusion.refs_0_, bf16[2,8,40,128]{3,2,1,0:T(8,128)(2,1)S(1)} %collective-permute-done.5.refs_1_, bf16[2,8,40,128]{3,2,1,0:T(8,128)(2,1)S(1)} %collective-permute-done.6.refs_2_, ...), custom_call_target="tpu_custom_call" | custom-call | bytes 2621440 | tf_op jit(solution)/shard_map/pallas_call | solution.py:122
  144.3 0.3 shard_map.71
  144.5 0.0 all-to-all-done.2.kv_ref
  144.6 2.8 %shard_map.73 = bf16[128,640]{1,0:T(8,128)(2,1)} custom-call(s32[1]{0:T(128)} %bitcast.rank_ref, bf16[5,128,128]{2,1,0:T(8,128)(2,1)S(1)} %get-tuple-element.11.q_ref, f32[128,640]{1,0:T(8,128)S(1)} %get-tuple-element.12.mask_ref, bf16[8,256,128]{2,1,0:T(8,128)(2,1)S(1)} %all-to-all-done.2.kv_ref), custom_call_target="tpu_custom_call" | custom-call | flops 209715200 | bytes 1179652 | tf_op jit(solution)/shard_map/pallas_call | solution.py:34
  (8 shorter events, 0.1 us)
Async XLA Ops:
  0.6 17.5 %copy-start.2 = (bf16[1024,640]{1,0:T(8,128)(2,1)S(1)}, bf16[1024,640]{1,0:T(8,128)(2,1)}, u32[]{:S(2)}) copy-start(bf16[1024,640]{1,0:T(8,128)(2,1)} %own_hbm.1) | copy-start | bytes 3932164
  1.8 7.3 %collective-permute-start.1 = (bf16[40,576]{1,0:T(8,128)(2,1)S(1)}, bf16[40,576]{1,0:T(8,128)(2,1)S(1)}, u32[]{:S(2)}, u32[]{:S(2)}) collective-permute-start(bf16[40,576]{1,0:T(8,128)(2,1)S(1)} %get-tuple-element.9), channel_id=1, source_target_pairs={{0,1},{1,0},{2,3},{3,2},{4,5},{5,4},{6,7},{7,6},{8,9},{9,8},{10,11... | collective-permute-start | bytes 138248 | tf_op jit(solution)/shard_map/ppermute | solution.py:287
  10.2 39.4 %all-to-all-start = ((bf16[16,40,896]{2,1,0:T(8,128)(2,1)}), bf16[16,40,896]{2,1,0:T(8,128)(2,1)S(1)}, u32[]{:S(2)}, u32[]{:S(2)}) async-start(bf16[16,40,896]{2,1,0:T(8,128)(2,1)} %get-tuple-element.10), calls=%async_computation | async-start | bytes 2293760 | tf_op jit(solution)/shard_map/all_to_all | solution.py:19
  18.2 31.4 %collective-permute-start = (bf16[1024,640]{1,0:T(8,128)(2,1)S(1)}, bf16[1024,640]{1,0:T(8,128)(2,1)}, u32[]{:S(2)}, u32[]{:S(2)}) collective-permute-start(bf16[1024,640]{1,0:T(8,128)(2,1)S(1)} %copy-done.2), channel_id=1, source_target_pairs={{0,1},{1,0},{2,3},{3,2},{4,5},{5,4},{6,7},{7,6},{8,9},{9,8},{10,11... | collective-permute-start | bytes 3932168 | tf_op jit(solution)/shard_map/ppermute | solution.py:287
  53.9 15.2 %copy-start = (s32[1,1024]{1,0:T(1,128)S(1)}, s32[1,1024]{1,0:T(1,128)}, u32[]{:S(2)}) copy-start(s32[1,1024]{1,0:T(1,128)} %param.8) | copy-start | bytes 12292
  53.9 40.6 %copy-start.1 = (f32[896]{0:T(1024)S(1)}, f32[896]{0:T(1024)}, u32[]{:S(2)}) copy-start(f32[896]{0:T(1024)} %param.7) | copy-start | bytes 10756
  53.9 40.5 %all-to-all-start.1 = ((bf16[8,448,128]{2,1,0:T(8,128)(2,1)}), bf16[8,448,128]{2,1,0:T(8,128)(2,1)S(1)}, u32[]{:S(2)}, u32[]{:S(2)}) async-start(bf16[8,448,128]{2,1,0:T(8,128)(2,1)} %shard_map.70), calls=%async_computation.1 | async-start | bytes 1835008 | tf_op jit(solution)/shard_map/all_to_all | solution.py:19
  69.7 17.1 %collective-permute-start.2 = (bf16[2,40,128]{2,1,0:T(8,128)(2,1)S(1)}, bf16[2,40,128]{2,1,0:T(8,128)(2,1)S(1)}, u32[]{:S(2)}, u32[]{:S(2)}) collective-permute-start(bf16[2,40,128]{2,1,0:T(8,128)(2,1)S(1)} %get-tuple-element.13), channel_id=1, source_target_pairs={{2,0},{7,1},{4,2},{1,3},{6,4},{3,5},{0,6},{5,7},{10,8},{15,9},{12,... | collective-permute-start | bytes 61448 | tf_op jit(solution)/shard_map/ppermute | solution.py:303
  86.8 13.4 %collective-permute-start.3 = (bf16[4,40,128]{2,1,0:T(8,128)(2,1)S(1)}, bf16[4,40,128]{2,1,0:T(8,128)(2,1)S(1)}, u32[]{:S(2)}, u32[]{:S(2)}) collective-permute-start(bf16[4,40,128]{2,1,0:T(8,128)(2,1)S(1)} %pad_maximum_fusion.3), channel_id=1, source_target_pairs={{4,0},{5,1},{6,2},{7,3},{0,4},{1,5},{2,6},{3,7},{12,8},{13,9},{14,... | collective-permute-start | bytes 122888 | tf_op jit(solution)/shard_map/ppermute | solution.py:303
  95.4 49.1 %all-to-all-start.2 = ((bf16[8,256,128]{2,1,0:T(8,128)(2,1)}), bf16[8,256,128]{2,1,0:T(8,128)(2,1)S(1)}, u32[]{:S(2)}, u32[]{:S(2)}) async-start(bf16[8,256,128]{2,1,0:T(8,128)(2,1)} %shard_map.72), calls=%async_computation.2 | async-start | bytes 1048576 | tf_op jit(solution)/shard_map/all_to_all | solution.py:19
  100.3 6.3 %collective-permute-start.4 = (bf16[8,40,128]{2,1,0:T(8,128)(2,1)S(1)}, bf16[8,40,128]{2,1,0:T(8,128)(2,1)S(1)}, u32[]{:S(2)}, u32[]{:S(2)}) collective-permute-start(bf16[8,40,128]{2,1,0:T(8,128)(2,1)S(1)} %constant_dynamic-update-slice_fusion), channel_id=1, source_target_pairs={{0,512},{64,576},{128,640},{192,704},{256,768},{320,832},{384,896}... | collective-permute-start | bytes 245768 | tf_op jit(solution)/shard_map/ppermute | solution.py:287
  106.6 8.4 %collective-permute-start.5 = (bf16[2,8,40,128]{3,2,1,0:T(8,128)(2,1)S(1)}, bf16[2,8,40,128]{3,2,1,0:T(8,128)(2,1)S(1)}, u32[]{:S(2)}, u32[]{:S(2)}) collective-permute-start(bf16[2,8,40,128]{3,2,1,0:T(8,128)(2,1)S(1)} %pad_maximum_fusion.refs_0_), channel_id=1, source_target_pairs={{0,64},{64,128},{128,192},{192,256},{256,320},{320,384},{384,448},... | collective-permute-start | bytes 491528 | tf_op jit(solution)/shard_map/ppermute | solution.py:291
  110.0 8.2 %collective-permute-start.9 = (bf16[2,8,40,128]{3,2,1,0:T(8,128)(2,1)S(1)}, bf16[2,8,40,128]{3,2,1,0:T(8,128)(2,1)S(1)}, u32[]{:S(2)}, u32[]{:S(2)}) collective-permute-start(bf16[2,8,40,128]{3,2,1,0:T(8,128)(2,1)S(1)} %pad_maximum_fusion.refs_0_), channel_id=1, source_target_pairs={{0,448},{64,0},{128,64},{192,128},{256,192},{320,256},{384,320},{4... | collective-permute-start | bytes 491528 | tf_op jit(solution)/shard_map/ppermute | solution.py:291
  115.0 9.1 %collective-permute-start.6 = (bf16[2,8,40,128]{3,2,1,0:T(8,128)(2,1)S(1)}, bf16[2,8,40,128]{3,2,1,0:T(8,128)(2,1)S(1)}, u32[]{:S(2)}, u32[]{:S(2)}) collective-permute-start(bf16[2,8,40,128]{3,2,1,0:T(8,128)(2,1)S(1)} %collective-permute-done.5.refs_1_), channel_id=1, source_target_pairs={{0,64},{64,128},{128,192},{192,256},{256,320},{320,384},{384,448},... | collective-permute-start | bytes 491528 | tf_op jit(solution)/shard_map/ppermute | solution.py:291
  118.2 8.8 %collective-permute-start.10 = (bf16[2,8,40,128]{3,2,1,0:T(8,128)(2,1)S(1)}, bf16[2,8,40,128]{3,2,1,0:T(8,128)(2,1)S(1)}, u32[]{:S(2)}, u32[]{:S(2)}) collective-permute-start(bf16[2,8,40,128]{3,2,1,0:T(8,128)(2,1)S(1)} %collective-permute-done.9.refs_7_), channel_id=1, source_target_pairs={{0,448},{64,0},{128,64},{192,128},{256,192},{320,256},{384,320},{4... | collective-permute-start | bytes 491528 | tf_op jit(solution)/shard_map/ppermute | solution.py:291
  124.1 10.1 %collective-permute-start.7 = (bf16[2,8,40,128]{3,2,1,0:T(8,128)(2,1)S(1)}, bf16[2,8,40,128]{3,2,1,0:T(8,128)(2,1)S(1)}, u32[]{:S(2)}, u32[]{:S(2)}) collective-permute-start(bf16[2,8,40,128]{3,2,1,0:T(8,128)(2,1)S(1)} %collective-permute-done.6.refs_2_), channel_id=1, source_target_pairs={{0,64},{64,128},{128,192},{192,256},{256,320},{320,384},{384,448},... | collective-permute-start | bytes 491528 | tf_op jit(solution)/shard_map/ppermute | solution.py:291
  127.0 9.4 %collective-permute-start.11 = (bf16[2,8,40,128]{3,2,1,0:T(8,128)(2,1)S(1)}, bf16[2,8,40,128]{3,2,1,0:T(8,128)(2,1)S(1)}, u32[]{:S(2)}, u32[]{:S(2)}) collective-permute-start(bf16[2,8,40,128]{3,2,1,0:T(8,128)(2,1)S(1)} %collective-permute-done.10.refs_6_), channel_id=1, source_target_pairs={{0,448},{64,0},{128,64},{192,128},{256,192},{320,256},{384,320},{4... | collective-permute-start | bytes 491528 | tf_op jit(solution)/shard_map/ppermute | solution.py:291
  134.2 8.4 %collective-permute-start.8 = (bf16[2,8,40,128]{3,2,1,0:T(8,128)(2,1)S(1)}, bf16[2,8,40,128]{3,2,1,0:T(8,128)(2,1)S(1)}, u32[]{:S(2)}, u32[]{:S(2)}) collective-permute-start(bf16[2,8,40,128]{3,2,1,0:T(8,128)(2,1)S(1)} %collective-permute-done.7.refs_3_), channel_id=1, source_target_pairs={{0,64},{64,128},{128,192},{192,256},{256,320},{320,384},{384,448},... | collective-permute-start | bytes 491528 | tf_op jit(solution)/shard_map/ppermute | solution.py:291

commit v9 on v8

--- a/solution.py
+++ b/solution.py
@@ -130,17 +130,18 @@
     )(place, *parts)
 
 
-def project(own_hbm, other_hbm, w_ref, out_ref, own_ref, other_ref, sems):
+def project(core_ref, own_hbm, far_hbm, near_hbm, w_ref, out_ref, own_ref, other_ref, sems):
     blocks = out_ref.shape[0]
     rows = own_hbm.shape[0]
     step = rows // 2
+    core = core_ref[0]
     loads = []
     for part in range(2):
         span = pl.ds(part * step, step)
-        for side, (source, target) in enumerate([(own_hbm, own_ref), (other_hbm, other_ref)]):
-            loads.append(
-                pltpu.make_async_copy(source.at[span], target.at[span], sems.at[2 * part + side])
-            )
+        loads.append(pltpu.make_async_copy(own_hbm.at[span], own_ref.at[span], sems.at[part]))
+    for source, index in ((far_hbm, core), (near_hbm, 1 - core)):
+        span = pl.ds(pl.multiple_of(index * step, step), step)
+        loads.append(pltpu.make_async_copy(source, other_ref.at[span], sems.at[len(loads)]))
     for load in loads:
         load.start()
     shared = w_ref[:, 3 * HD : 4 * HD]
@@ -151,8 +152,10 @@
     low = lanes_below_half((size // 2, HD))
     for part in range(2):
         at = part * step
-        loads[2 * part].wait()
-        loads[2 * part + 1].wait()
+        loads[part].wait()
+        if part == 0:
+            loads[2].wait()
+            loads[3].wait()
         value = jnp.dot(own_ref[at : at + step, :], w_own, preferred_element_type=jnp.float32)
         value = value + jnp.dot(
             other_ref[at : at + step, :], w_other, preferred_element_type=jnp.float32
@@ -169,14 +172,14 @@
             out_ref[j, 3 * size :] = packed.astype(jnp.bfloat16)
 
 
-def projected(own, other, gathered, blocks):
+def projected(core, own, far, near, gathered, blocks):
     rows, features = own.shape
     vmem = pl.BlockSpec(memory_space=pltpu.VMEM)
     hbm = pl.BlockSpec(memory_space=pltpu.HBM)
     return pl.pallas_call(
         project,
         out_shape=jax.ShapeDtypeStruct((blocks, 7 * rows // blocks // 2, HD), jnp.bfloat16),
-        in_specs=[hbm, hbm, vmem],
+        in_specs=[pl.BlockSpec(memory_space=pltpu.SMEM), hbm, hbm, hbm, vmem],
         out_specs=vmem,
         scratch_shapes=[
             pltpu.VMEM(own.shape, own.dtype),
@@ -185,7 +188,7 @@
         ],
         compiler_params=pltpu.CompilerParams(vmem_limit_bytes=24 * 1024 * 1024),
         cost_estimate=cost(4 * rows * features * 4 * HD, 4 * own.size + 2 * gathered.size),
-    )(in_hbm(own), in_hbm(other), gathered)
+    )(core.reshape(1), in_hbm(own), in_hbm(far), in_hbm(near), gathered)
 
 
 def turned(value, cosine, sine):
@@ -293,7 +296,10 @@
     own_features, width = policy_key.shape
     keep, give = split_columns(rank, in_hbm(ref_qkv), in_hbm(policy_key))
     got = swapped(give, "rep", 1)
-    other = swapped(tokens, "rep", 1)
+    core = lax.axis_index("tp") & 1
+    fetched = lax.dynamic_slice_in_dim(tokens, core * (rows // 2), rows // 2, 0)
+    far = swapped(fetched, "rep", 1)
+    near = swapped(far, "tp", 1)
     copies = jax.ShapeDtypeStruct((shards, own_features, 7 * HD), bf16)
     pair = jax.ShapeDtypeStruct((2, own_features, width), bf16)
     copies, pair = call(pack, (copies, pair), 0, keep, got)
@@ -323,7 +329,7 @@
     sine = jnp.concatenate([-sine, sine], axis=1)
     bias = ref_bias.reshape(SHARE + 2, HD)
 
-    part = projected(tokens, other, gathered, replicas)
+    part = projected(core, tokens, far, near, gathered, replicas)
     part = exchanged(part, "rep")
     my_kv = call(
         keys_and_values,

time: 148 us -> 145 us (0.980)
  waiting for transfers between devices: 56.5 us -> 50.8 us
  starting transfers between devices: 76.8 us -> 78.8 us
    ppermute x3 -> x4, waiting for transfers between devices: 32.4 us -> 20.9 us  [swapped(): return lax.ppermute(value, axis, pairs)]
    all_to_all x3, waiting for transfers between devices: 0.01 us -> 5.97 us  [exchanged(): return lax.all_to_all(blocks, axis, split_axis=0, concat_axis=0, tiled=True)]
    ppermute x3 -> x4, starting transfers between devices: 12.5 us -> 13.8 us  [swapped(): return lax.ppermute(value, axis, pairs)]
  transfers between devices with their start and end apart: 15 -> 16, of which waited for: 10 -> 11; matrix products, arithmetic and copies ran while one was open for 1% -> 1% of each run, Pallas kernels for 2% -> 2%
where the time goes in v9:
time: 145 us; the launch traced here: 144 us
  starting transfers between devices  78.8 us (54%)
  waiting for transfers between devices  50.8 us (35%)
  Pallas kernels  12.6 us (9%)
    all_to_all x3, starting transfers between devices, exchanged(): return lax.all_to_all(blocks, axis, split_axis=0, concat_axis=0, tiled=True)  28.2 us
    ppermute x7, starting transfers between devices, passed(): return lax.ppermute(value, 'fsdp', pairs)  23.1 us
    ppermute x4, waiting for transfers between devices, swapped(): return lax.ppermute(value, axis, pairs)  20.9 us
    ppermute x4, starting transfers between devices, swapped(): return lax.ppermute(value, axis, pairs)  13.8 us
    ppermute x2, starting transfers between devices, body(): column = jnp.concatenate([column, lax.ppermute(column, 'rep', pairs)])  13.6 us
    ppermute x7, waiting for transfers between devices, passed(): return lax.ppermute(value, 'fsdp', pairs)  12.6 us
    ppermute x2, waiting for transfers between devices, body(): column = jnp.concatenate([column, lax.ppermute(column, 'rep', pairs)])  11.3 us
    all_to_all x3, waiting for transfers between devices, exchanged(): return lax.all_to_all(blocks, axis, split_axis=0, concat_axis=0, tiled=True)  5.97 us
  transfers between devices with their start and end apart: 16, of which 11 were waited for; matrix products, arithmetic and copies ran while one was open for 1% of the time, Pallas kernels for 2%

profile of v9, /device:TPU:32, one launch (start us, length us, event | category | flops | bytes accessed | tf_op | source)
XLA Modules:
  0.0 144.1 jit_solution(4977561812921162305)
XLA Ops:
  0.6 0.0 copy-start.2
  0.6 1.1 shard_map.68
  1.8 5.2 %collective-permute-start.2 = (bf16[40,576]{1,0:T(8,128)(2,1)S(1)}, bf16[40,576]{1,0:T(8,128)(2,1)S(1)}, u32[]{:S(2)}, u32[]{:S(2)}) collective-permute-start(bf16[40,576]{1,0:T(8,128)(2,1)S(1)} %get-tuple-element.9), channel_id=1, source_target_pairs={{0,1},{1,0},{2,3},{3,2},{4,5},{5,4},{6,7},{7,6},{8,9},{9,8},{10,11... | collective-permute-start | bytes 138248 | tf_op jit(solution)/shard_map/ppermute | solution.py:290
  7.0 2.1 %collective-permute-done.2.got_ref = bf16[40,576]{1,0:T(8,128)(2,1)S(1)} collective-permute-done((bf16[40,576]{1,0:T(8,128)(2,1)S(1)}, bf16[40,576]{1,0:T(8,128)(2,1)S(1)}, u32[]{:S(2)}, u32[]{:S(2)}) %collective-permute-start.2) | collective-permute-done | bytes 46112 | tf_op jit(solution)/shard_map/ppermute | solution.py:290
  9.0 1.1 shard_map.69
  10.2 8.0 %all-to-all-start = ((bf16[16,40,896]{2,1,0:T(8,128)(2,1)}), bf16[16,40,896]{2,1,0:T(8,128)(2,1)S(1)}, u32[]{:S(2)}, u32[]{:S(2)}) async-start(bf16[16,40,896]{2,1,0:T(8,128)(2,1)} %get-tuple-element.10), calls=%async_computation | async-start | bytes 2293760 | tf_op jit(solution)/shard_map/all_to_all | solution.py:19
  18.2 0.0 copy-done.2
  18.2 0.1 constant_dynamic-slice_fusion.1
  18.2 3.9 %collective-permute-start = (bf16[512,640]{1,0:T(8,128)(2,1)S(1)}, bf16[512,640]{1,0:T(8,128)(2,1)S(1)}, u32[]{:S(2)}, u32[]{:S(2)}) collective-permute-start(bf16[512,640]{1,0:T(8,128)(2,1)S(1)} %constant_dynamic-slice_fusion.1), channel_id=1, source_target_pairs={{0,1},{1,0},{2,3},{3,2},{4,5},{5,4},{6,7},{7,6},{8,9},{9,8},{10,11... | collective-permute-start | bytes 1966088 | tf_op jit(solution)/shard_map/ppermute | solution.py:290
  22.2 13.3 %collective-permute-done.far_hbm = bf16[512,640]{1,0:T(8,128)(2,1)S(1)} collective-permute-done((bf16[512,640]{1,0:T(8,128)(2,1)S(1)}, bf16[512,640]{1,0:T(8,128)(2,1)S(1)}, u32[]{:S(2)}, u32[]{:S(2)}) %collective-permute-start) | collective-permute-done | bytes 655392 | tf_op jit(solution)/shard_map/ppermute | solution.py:290
  35.5 0.0 copy-start.3
  35.5 1.9 %collective-permute-start.1 = (bf16[512,640]{1,0:T(8,128)(2,1)S(1)}, bf16[512,640]{1,0:T(8,128)(2,1)S(1)}, u32[]{:S(2)}, u32[]{:S(2)}) collective-permute-start(bf16[512,640]{1,0:T(8,128)(2,1)S(1)} %collective-permute-done.far_hbm), channel_id=1, source_target_pairs={{0,8},{8,0},{16,24},{24,16},{32,40},{40,32},{48,56},{56,48},{1,9},... | collective-permute-start | bytes 1966088 | tf_op jit(solution)/shard_map/ppermute | solution.py:290
  37.4 2.1 %collective-permute-done.1.near_hbm = bf16[512,640]{1,0:T(8,128)(2,1)S(1)} collective-permute-done((bf16[512,640]{1,0:T(8,128)(2,1)S(1)}, bf16[512,640]{1,0:T(8,128)(2,1)S(1)}, u32[]{:S(2)}, u32[]{:S(2)}) %collective-permute-start.1) | collective-permute-done | bytes 655392 | tf_op jit(solution)/shard_map/ppermute | solution.py:290
  39.4 0.0 copy-start.4
  39.5 6.0 %all-to-all-done = bf16[16,40,896]{2,1,0:T(8,128)(2,1)S(1)} async-done(((bf16[16,40,896]{2,1,0:T(8,128)(2,1)}), bf16[16,40,896]{2,1,0:T(8,128)(2,1)S(1)}, u32[]{:S(2)}, u32[]{:S(2)}) %all-to-all-start) | async-done | bytes 1146912 | tf_op jit(solution)/shard_map/all_to_all | solution.py:19
  45.4 0.0 copy-done.3
  45.4 0.0 copy-done.4
  45.4 4.7 %shard_map.70 = bf16[8,448,128]{2,1,0:T(8,128)(2,1)} custom-call(s32[1]{0:T(128)} %bitcast.1.core_ref, bf16[1024,640]{1,0:T(8,128)(2,1)} %own_hbm.1, bf16[512,640]{1,0:T(8,128)(2,1)} %copy-done.3, bf16[512,640]{1,0:T(8,128)(2,1)} %copy-done.4, bf16[640,896]{1,0:T(8,128)(2,1)S(1)} %bitcast.15), custom_call_target="tpu_custom_call" | custom-call | flops 1342177280 | bytes 3768320 | tf_op jit(solution)/shard_map/pallas_call | solution.py:179
  50.2 0.0 copy-start
  50.2 0.0 copy-start.1
  50.2 15.3 %all-to-all-start.1 = ((bf16[8,448,128]{2,1,0:T(8,128)(2,1)}), bf16[8,448,128]{2,1,0:T(8,128)(2,1)S(1)}, u32[]{:S(2)}, u32[]{:S(2)}) async-start(bf16[8,448,128]{2,1,0:T(8,128)(2,1)} %shard_map.70), calls=%async_computation.1 | async-start | bytes 1835008 | tf_op jit(solution)/shard_map/all_to_all | solution.py:19
  65.6 0.0 copy-done
  65.6 0.2 convert_reduce_fusion
  65.8 0.3 fusion
  66.1 0.1 pad_maximum_fusion.1
  66.2 6.0 %collective-permute-start.3 = (bf16[2,40,128]{2,1,0:T(8,128)(2,1)S(1)}, bf16[2,40,128]{2,1,0:T(8,128)(2,1)S(1)}, u32[]{:S(2)}, u32[]{:S(2)}) collective-permute-start(bf16[2,40,128]{2,1,0:T(8,128)(2,1)S(1)} %get-tuple-element.13), channel_id=1, source_target_pairs={{2,0},{7,1},{4,2},{1,3},{6,4},{3,5},{0,6},{5,7},{10,8},{15,9},{12,... | collective-permute-start | bytes 61448 | tf_op jit(solution)/shard_map/ppermute | solution.py:309
  72.3 11.3 %collective-permute-done.3 = bf16[2,40,128]{2,1,0:T(8,128)(2,1)S(1)} collective-permute-done((bf16[2,40,128]{2,1,0:T(8,128)(2,1)S(1)}, bf16[2,40,128]{2,1,0:T(8,128)(2,1)S(1)}, u32[]{:S(2)}, u32[]{:S(2)}) %collective-permute-start.3) | collective-permute-done | bytes 20512 | tf_op jit(solution)/shard_map/ppermute | solution.py:309
  83.6 7.6 %collective-permute-start.4 = (bf16[4,40,128]{2,1,0:T(8,128)(2,1)S(1)}, bf16[4,40,128]{2,1,0:T(8,128)(2,1)S(1)}, u32[]{:S(2)}, u32[]{:S(2)}) collective-permute-start(bf16[4,40,128]{2,1,0:T(8,128)(2,1)S(1)} %pad_maximum_fusion.3), channel_id=1, source_target_pairs={{4,0},{5,1},{6,2},{7,3},{0,4},{1,5},{2,6},{3,7},{12,8},{13,9},{14,... | collective-permute-start | bytes 122888 | tf_op jit(solution)/shard_map/ppermute | solution.py:309
  91.2 0.0 all-to-all-done.1.part_ref
  91.2 0.0 copy-done.1
  91.2 0.9 shard_map.72
  92.1 4.8 %all-to-all-start.2 = ((bf16[8,256,128]{2,1,0:T(8,128)(2,1)}), bf16[8,256,128]{2,1,0:T(8,128)(2,1)S(1)}, u32[]{:S(2)}, u32[]{:S(2)}) async-start(bf16[8,256,128]{2,1,0:T(8,128)(2,1)} %shard_map.72), calls=%async_computation.2 | async-start | bytes 1048576 | tf_op jit(solution)/shard_map/all_to_all | solution.py:19
  96.9 0.0 collective-permute-done.4
  97.0 2.8 %collective-permute-start.5 = (bf16[8,40,128]{2,1,0:T(8,128)(2,1)S(1)}, bf16[8,40,128]{2,1,0:T(8,128)(2,1)S(1)}, u32[]{:S(2)}, u32[]{:S(2)}) collective-permute-start(bf16[8,40,128]{2,1,0:T(8,128)(2,1)S(1)} %constant_dynamic-update-slice_fusion), channel_id=1, source_target_pairs={{0,512},{64,576},{128,640},{192,704},{256,768},{320,832},{384,896}... | collective-permute-start | bytes 245768 | tf_op jit(solution)/shard_map/ppermute | solution.py:290
  99.8 3.5 %collective-permute-done.5 = bf16[8,40,128]{2,1,0:T(8,128)(2,1)S(1)} collective-permute-done((bf16[8,40,128]{2,1,0:T(8,128)(2,1)S(1)}, bf16[8,40,128]{2,1,0:T(8,128)(2,1)S(1)}, u32[]{:S(2)}, u32[]{:S(2)}) %collective-permute-start.5) | collective-permute-done | bytes 81952 | tf_op jit(solution)/shard_map/ppermute | solution.py:290
  103.3 2.4 %collective-permute-start.6 = (bf16[2,8,40,128]{3,2,1,0:T(8,128)(2,1)S(1)}, bf16[2,8,40,128]{3,2,1,0:T(8,128)(2,1)S(1)}, u32[]{:S(2)}, u32[]{:S(2)}) collective-permute-start(bf16[2,8,40,128]{3,2,1,0:T(8,128)(2,1)S(1)} %pad_maximum_fusion.refs_0_), channel_id=1, source_target_pairs={{0,64},{64,128},{128,192},{192,256},{256,320},{320,384},{384,448},... | collective-permute-start | bytes 491528 | tf_op jit(solution)/shard_map/ppermute | solution.py:294
  105.7 4.7 %collective-permute-start.10 = (bf16[2,8,40,128]{3,2,1,0:T(8,128)(2,1)S(1)}, bf16[2,8,40,128]{3,2,1,0:T(8,128)(2,1)S(1)}, u32[]{:S(2)}, u32[]{:S(2)}) collective-permute-start(bf16[2,8,40,128]{3,2,1,0:T(8,128)(2,1)S(1)} %pad_maximum_fusion.refs_0_), channel_id=1, source_target_pairs={{0,448},{64,0},{128,64},{192,128},{256,192},{320,256},{384,320},{4... | collective-permute-start | bytes 491528 | tf_op jit(solution)/shard_map/ppermute | solution.py:294
  110.4 1.4 collective-permute-done.6.refs_1_
  111.7 3.0 %collective-permute-start.7 = (bf16[2,8,40,128]{3,2,1,0:T(8,128)(2,1)S(1)}, bf16[2,8,40,128]{3,2,1,0:T(8,128)(2,1)S(1)}, u32[]{:S(2)}, u32[]{:S(2)}) collective-permute-start(bf16[2,8,40,128]{3,2,1,0:T(8,128)(2,1)S(1)} %collective-permute-done.6.refs_1_), channel_id=1, source_target_pairs={{0,64},{64,128},{128,192},{192,256},{256,320},{320,384},{384,448},... | collective-permute-start | bytes 491528 | tf_op jit(solution)/shard_map/ppermute | solution.py:294
  114.8 0.0 collective-permute-done.10.refs_7_
  114.8 4.0 %collective-permute-start.11 = (bf16[2,8,40,128]{3,2,1,0:T(8,128)(2,1)S(1)}, bf16[2,8,40,128]{3,2,1,0:T(8,128)(2,1)S(1)}, u32[]{:S(2)}, u32[]{:S(2)}) collective-permute-start(bf16[2,8,40,128]{3,2,1,0:T(8,128)(2,1)S(1)} %collective-permute-done.10.refs_7_), channel_id=1, source_target_pairs={{0,448},{64,0},{128,64},{192,128},{256,192},{320,256},{384,320},{4... | collective-permute-start | bytes 491528 | tf_op jit(solution)/shard_map/ppermute | solution.py:294
  118.8 2.0 %collective-permute-done.7.refs_2_ = bf16[2,8,40,128]{3,2,1,0:T(8,128)(2,1)S(1)} collective-permute-done((bf16[2,8,40,128]{3,2,1,0:T(8,128)(2,1)S(1)}, bf16[2,8,40,128]{3,2,1,0:T(8,128)(2,1)S(1)}, u32[]{:S(2)}, u32[]{:S(2)}) %collective-permute-start.7) | collective-permute-done | bytes 163872 | tf_op jit(solution)/shard_map/ppermute | solution.py:294
  120.8 2.6 %collective-permute-start.8 = (bf16[2,8,40,128]{3,2,1,0:T(8,128)(2,1)S(1)}, bf16[2,8,40,128]{3,2,1,0:T(8,128)(2,1)S(1)}, u32[]{:S(2)}, u32[]{:S(2)}) collective-permute-start(bf16[2,8,40,128]{3,2,1,0:T(8,128)(2,1)S(1)} %collective-permute-done.7.refs_2_), channel_id=1, source_target_pairs={{0,64},{64,128},{128,192},{192,256},{256,320},{320,384},{384,448},... | collective-permute-start | bytes 491528 | tf_op jit(solution)/shard_map/ppermute | solution.py:294
  123.5 0.2 collective-permute-done.11.refs_6_
  123.7 4.5 %collective-permute-start.12 = (bf16[2,8,40,128]{3,2,1,0:T(8,128)(2,1)S(1)}, bf16[2,8,40,128]{3,2,1,0:T(8,128)(2,1)S(1)}, u32[]{:S(2)}, u32[]{:S(2)}) collective-permute-start(bf16[2,8,40,128]{3,2,1,0:T(8,128)(2,1)S(1)} %collective-permute-done.11.refs_6_), channel_id=1, source_target_pairs={{0,448},{64,0},{128,64},{192,128},{256,192},{320,256},{384,320},{4... | collective-permute-start | bytes 491528 | tf_op jit(solution)/shard_map/ppermute | solution.py:294
  128.2 2.7 %collective-permute-done.8.refs_3_ = bf16[2,8,40,128]{3,2,1,0:T(8,128)(2,1)S(1)} collective-permute-done((bf16[2,8,40,128]{3,2,1,0:T(8,128)(2,1)S(1)}, bf16[2,8,40,128]{3,2,1,0:T(8,128)(2,1)S(1)}, u32[]{:S(2)}, u32[]{:S(2)}) %collective-permute-start.8) | collective-permute-done | bytes 163872 | tf_op jit(solution)/shard_map/ppermute | solution.py:294
  130.9 1.9 %collective-permute-start.9 = (bf16[2,8,40,128]{3,2,1,0:T(8,128)(2,1)S(1)}, bf16[2,8,40,128]{3,2,1,0:T(8,128)(2,1)S(1)}, u32[]{:S(2)}, u32[]{:S(2)}) collective-permute-start(bf16[2,8,40,128]{3,2,1,0:T(8,128)(2,1)S(1)} %collective-permute-done.8.refs_3_), channel_id=1, source_target_pairs={{0,64},{64,128},{128,192},{192,256},{256,320},{320,384},{384,448},... | collective-permute-start | bytes 491528 | tf_op jit(solution)/shard_map/ppermute | solution.py:294
  132.9 0.1 copy.8.mine_ref
  133.0 0.1 pad_add_fusion.place_ref
  133.1 0.0 collective-permute-done.12.refs_5_
  133.1 6.3 %collective-permute-done.9.refs_4_ = bf16[2,8,40,128]{3,2,1,0:T(8,128)(2,1)S(1)} collective-permute-done((bf16[2,8,40,128]{3,2,1,0:T(8,128)(2,1)S(1)}, bf16[2,8,40,128]{3,2,1,0:T(8,128)(2,1)S(1)}, u32[]{:S(2)}, u32[]{:S(2)}) %collective-permute-start.9) | collective-permute-done | bytes 163872 | tf_op jit(solution)/shard_map/ppermute | solution.py:294
  139.3 1.6 %shard_map.74 = bf16[8,2,8,40,128]{4,3,2,1,0:T(8,128)(2,1)} custom-call(s32[3]{0:T(128)S(1)} %pad_add_fusion.place_ref, bf16[2,8,40,128]{3,2,1,0:T(8,128)(2,1)S(1)} %pad_maximum_fusion.refs_0_, bf16[2,8,40,128]{3,2,1,0:T(8,128)(2,1)S(1)} %collective-permute-done.6.refs_1_, bf16[2,8,40,128]{3,2,1,0:T(8,128)(2,1)S(1)} %collective-permute-done.7.refs_2_, ...), custom_call_target="tpu_custom_call" | custom-call | bytes 2621440 | tf_op jit(solution)/shard_map/pallas_call | solution.py:122
  141.0 0.3 shard_map.71
  141.2 0.0 all-to-all-done.2.kv_ref
  141.3 2.8 %shard_map.73 = bf16[128,640]{1,0:T(8,128)(2,1)} custom-call(s32[1]{0:T(128)} %bitcast.rank_ref, bf16[5,128,128]{2,1,0:T(8,128)(2,1)S(1)} %get-tuple-element.11.q_ref, f32[128,640]{1,0:T(8,128)S(1)} %get-tuple-element.12.mask_ref, bf16[8,256,128]{2,1,0:T(8,128)(2,1)S(1)} %all-to-all-done.2.kv_ref), custom_call_target="tpu_custom_call" | custom-call | flops 209715200 | bytes 1179652 | tf_op jit(solution)/shard_map/pallas_call | solution.py:34
  (8 shorter events, 0.1 us)
Async XLA Ops:
  0.6 17.5 %copy-start.2 = (bf16[1024,640]{1,0:T(8,128)(2,1)S(1)}, bf16[1024,640]{1,0:T(8,128)(2,1)}, u32[]{:S(2)}) copy-start(bf16[1024,640]{1,0:T(8,128)(2,1)} %own_hbm.1) | copy-start | bytes 3932164
  1.8 7.3 %collective-permute-start.2 = (bf16[40,576]{1,0:T(8,128)(2,1)S(1)}, bf16[40,576]{1,0:T(8,128)(2,1)S(1)}, u32[]{:S(2)}, u32[]{:S(2)}) collective-permute-start(bf16[40,576]{1,0:T(8,128)(2,1)S(1)} %get-tuple-element.9), channel_id=1, source_target_pairs={{0,1},{1,0},{2,3},{3,2},{4,5},{5,4},{6,7},{7,6},{8,9},{9,8},{10,11... | collective-permute-start | bytes 138248 | tf_op jit(solution)/shard_map/ppermute | solution.py:290
  10.2 35.3 %all-to-all-start = ((bf16[16,40,896]{2,1,0:T(8,128)(2,1)}), bf16[16,40,896]{2,1,0:T(8,128)(2,1)S(1)}, u32[]{:S(2)}, u32[]{:S(2)}) async-start(bf16[16,40,896]{2,1,0:T(8,128)(2,1)} %get-tuple-element.10), calls=%async_computation | async-start | bytes 2293760 | tf_op jit(solution)/shard_map/all_to_all | solution.py:19
  18.2 17.2 %collective-permute-start = (bf16[512,640]{1,0:T(8,128)(2,1)S(1)}, bf16[512,640]{1,0:T(8,128)(2,1)S(1)}, u32[]{:S(2)}, u32[]{:S(2)}) collective-permute-start(bf16[512,640]{1,0:T(8,128)(2,1)S(1)} %constant_dynamic-slice_fusion.1), channel_id=1, source_target_pairs={{0,1},{1,0},{2,3},{3,2},{4,5},{5,4},{6,7},{7,6},{8,9},{9,8},{10,11... | collective-permute-start | bytes 1966088 | tf_op jit(solution)/shard_map/ppermute | solution.py:290
  35.5 10.0 %copy-start.3 = (bf16[512,640]{1,0:T(8,128)(2,1)}, bf16[512,640]{1,0:T(8,128)(2,1)S(1)}, u32[]{:S(2)}) copy-start(bf16[512,640]{1,0:T(8,128)(2,1)S(1)} %collective-permute-done.far_hbm) | copy-start | bytes 1966084
  35.5 4.0 %collective-permute-start.1 = (bf16[512,640]{1,0:T(8,128)(2,1)S(1)}, bf16[512,640]{1,0:T(8,128)(2,1)S(1)}, u32[]{:S(2)}, u32[]{:S(2)}) collective-permute-start(bf16[512,640]{1,0:T(8,128)(2,1)S(1)} %collective-permute-done.far_hbm), channel_id=1, source_target_pairs={{0,8},{8,0},{16,24},{24,16},{32,40},{40,32},{48,56},{56,48},{1,9},... | collective-permute-start | bytes 1966088 | tf_op jit(solution)/shard_map/ppermute | solution.py:290
  39.4 6.0 %copy-start.4 = (bf16[512,640]{1,0:T(8,128)(2,1)}, bf16[512,640]{1,0:T(8,128)(2,1)S(1)}, u32[]{:S(2)}) copy-start(bf16[512,640]{1,0:T(8,128)(2,1)S(1)} %collective-permute-done.1.near_hbm) | copy-start | bytes 1966084
  50.2 15.4 %copy-start = (s32[1,1024]{1,0:T(1,128)S(1)}, s32[1,1024]{1,0:T(1,128)}, u32[]{:S(2)}) copy-start(s32[1,1024]{1,0:T(1,128)} %param.8) | copy-start | bytes 12292
  50.2 41.0 %copy-start.1 = (f32[896]{0:T(1024)S(1)}, f32[896]{0:T(1024)}, u32[]{:S(2)}) copy-start(f32[896]{0:T(1024)} %param.7) | copy-start | bytes 10756
  50.2 41.0 %all-to-all-start.1 = ((bf16[8,448,128]{2,1,0:T(8,128)(2,1)}), bf16[8,448,128]{2,1,0:T(8,128)(2,1)S(1)}, u32[]{:S(2)}, u32[]{:S(2)}) async-start(bf16[8,448,128]{2,1,0:T(8,128)(2,1)} %shard_map.70), calls=%async_computation.1 | async-start | bytes 1835008 | tf_op jit(solution)/shard_map/all_to_all | solution.py:19
  66.2 17.3 %collective-permute-start.3 = (bf16[2,40,128]{2,1,0:T(8,128)(2,1)S(1)}, bf16[2,40,128]{2,1,0:T(8,128)(2,1)S(1)}, u32[]{:S(2)}, u32[]{:S(2)}) collective-permute-start(bf16[2,40,128]{2,1,0:T(8,128)(2,1)S(1)} %get-tuple-element.13), channel_id=1, source_target_pairs={{2,0},{7,1},{4,2},{1,3},{6,4},{3,5},{0,6},{5,7},{10,8},{15,9},{12,... | collective-permute-start | bytes 61448 | tf_op jit(solution)/shard_map/ppermute | solution.py:309
  83.6 13.4 %collective-permute-start.4 = (bf16[4,40,128]{2,1,0:T(8,128)(2,1)S(1)}, bf16[4,40,128]{2,1,0:T(8,128)(2,1)S(1)}, u32[]{:S(2)}, u32[]{:S(2)}) collective-permute-start(bf16[4,40,128]{2,1,0:T(8,128)(2,1)S(1)} %pad_maximum_fusion.3), channel_id=1, source_target_pairs={{4,0},{5,1},{6,2},{7,3},{0,4},{1,5},{2,6},{3,7},{12,8},{13,9},{14,... | collective-permute-start | bytes 122888 | tf_op jit(solution)/shard_map/ppermute | solution.py:309
  92.1 49.1 %all-to-all-start.2 = ((bf16[8,256,128]{2,1,0:T(8,128)(2,1)}), bf16[8,256,128]{2,1,0:T(8,128)(2,1)S(1)}, u32[]{:S(2)}, u32[]{:S(2)}) async-start(bf16[8,256,128]{2,1,0:T(8,128)(2,1)} %shard_map.72), calls=%async_computation.2 | async-start | bytes 1048576 | tf_op jit(solution)/shard_map/all_to_all | solution.py:19
  97.0 6.3 %collective-permute-start.5 = (bf16[8,40,128]{2,1,0:T(8,128)(2,1)S(1)}, bf16[8,40,128]{2,1,0:T(8,128)(2,1)S(1)}, u32[]{:S(2)}, u32[]{:S(2)}) collective-permute-start(bf16[8,40,128]{2,1,0:T(8,128)(2,1)S(1)} %constant_dynamic-update-slice_fusion), channel_id=1, source_target_pairs={{0,512},{64,576},{128,640},{192,704},{256,768},{320,832},{384,896}... | collective-permute-start | bytes 245768 | tf_op jit(solution)/shard_map/ppermute | solution.py:290
  103.3 8.4 %collective-permute-start.6 = (bf16[2,8,40,128]{3,2,1,0:T(8,128)(2,1)S(1)}, bf16[2,8,40,128]{3,2,1,0:T(8,128)(2,1)S(1)}, u32[]{:S(2)}, u32[]{:S(2)}) collective-permute-start(bf16[2,8,40,128]{3,2,1,0:T(8,128)(2,1)S(1)} %pad_maximum_fusion.refs_0_), channel_id=1, source_target_pairs={{0,64},{64,128},{128,192},{192,256},{256,320},{320,384},{384,448},... | collective-permute-start | bytes 491528 | tf_op jit(solution)/shard_map/ppermute | solution.py:294
  105.7 9.0 %collective-permute-start.10 = (bf16[2,8,40,128]{3,2,1,0:T(8,128)(2,1)S(1)}, bf16[2,8,40,128]{3,2,1,0:T(8,128)(2,1)S(1)}, u32[]{:S(2)}, u32[]{:S(2)}) collective-permute-start(bf16[2,8,40,128]{3,2,1,0:T(8,128)(2,1)S(1)} %pad_maximum_fusion.refs_0_), channel_id=1, source_target_pairs={{0,448},{64,0},{128,64},{192,128},{256,192},{320,256},{384,320},{4... | collective-permute-start | bytes 491528 | tf_op jit(solution)/shard_map/ppermute | solution.py:294
  111.7 9.1 %collective-permute-start.7 = (bf16[2,8,40,128]{3,2,1,0:T(8,128)(2,1)S(1)}, bf16[2,8,40,128]{3,2,1,0:T(8,128)(2,1)S(1)}, u32[]{:S(2)}, u32[]{:S(2)}) collective-permute-start(bf16[2,8,40,128]{3,2,1,0:T(8,128)(2,1)S(1)} %collective-permute-done.6.refs_1_), channel_id=1, source_target_pairs={{0,64},{64,128},{128,192},{192,256},{256,320},{320,384},{384,448},... | collective-permute-start | bytes 491528 | tf_op jit(solution)/shard_map/ppermute | solution.py:294
  114.8 8.9 %collective-permute-start.11 = (bf16[2,8,40,128]{3,2,1,0:T(8,128)(2,1)S(1)}, bf16[2,8,40,128]{3,2,1,0:T(8,128)(2,1)S(1)}, u32[]{:S(2)}, u32[]{:S(2)}) collective-permute-start(bf16[2,8,40,128]{3,2,1,0:T(8,128)(2,1)S(1)} %collective-permute-done.10.refs_7_), channel_id=1, source_target_pairs={{0,448},{64,0},{128,64},{192,128},{256,192},{320,256},{384,320},{4... | collective-permute-start | bytes 491528 | tf_op jit(solution)/shard_map/ppermute | solution.py:294
  120.8 10.1 %collective-permute-start.8 = (bf16[2,8,40,128]{3,2,1,0:T(8,128)(2,1)S(1)}, bf16[2,8,40,128]{3,2,1,0:T(8,128)(2,1)S(1)}, u32[]{:S(2)}, u32[]{:S(2)}) collective-permute-start(bf16[2,8,40,128]{3,2,1,0:T(8,128)(2,1)S(1)} %collective-permute-done.7.refs_2_), channel_id=1, source_target_pairs={{0,64},{64,128},{128,192},{192,256},{256,320},{320,384},{384,448},... | collective-permute-start | bytes 491528 | tf_op jit(solution)/shard_map/ppermute | solution.py:294
  123.7 9.4 %collective-permute-start.12 = (bf16[2,8,40,128]{3,2,1,0:T(8,128)(2,1)S(1)}, bf16[2,8,40,128]{3,2,1,0:T(8,128)(2,1)S(1)}, u32[]{:S(2)}, u32[]{:S(2)}) collective-permute-start(bf16[2,8,40,128]{3,2,1,0:T(8,128)(2,1)S(1)} %collective-permute-done.11.refs_6_), channel_id=1, source_target_pairs={{0,448},{64,0},{128,64},{192,128},{256,192},{320,256},{384,320},{4... | collective-permute-start | bytes 491528 | tf_op jit(solution)/shard_map/ppermute | solution.py:294
  130.9 8.4 %collective-permute-start.9 = (bf16[2,8,40,128]{3,2,1,0:T(8,128)(2,1)S(1)}, bf16[2,8,40,128]{3,2,1,0:T(8,128)(2,1)S(1)}, u32[]{:S(2)}, u32[]{:S(2)}) collective-permute-start(bf16[2,8,40,128]{3,2,1,0:T(8,128)(2,1)S(1)} %collective-permute-done.8.refs_3_), channel_id=1, source_target_pairs={{0,64},{64,128},{128,192},{192,256},{256,320},{320,384},{384,448},... | collective-permute-start | bytes 491528 | tf_op jit(solution)/shard_map/ppermute | solution.py:294

commit v10 on v9

--- a/solution.py
+++ b/solution.py
@@ -100,7 +100,6 @@
 def arrange(place_ref, *refs):
     *parts, out_ref, sem = refs
     x, y, z = place_ref[0], place_ref[1], place_ref[2]
-    way = 1 - 2 * jnp.bitwise_and(z, 1)
     length, sides, replicas = len(parts), out_ref.shape[1], out_ref.shape[0]
     copies = []
     for k, part in enumerate(parts):
@@ -108,8 +107,7 @@
         column = jnp.bitwise_and(x - distance, length - 1)
         for side in range(sides):
             for b in range(replicas):
-                source = jnp.bitwise_and(z + way * (b - b % 2), replicas - 1) ^ (b % 2)
-                place = out_ref.at[source, y ^ side, column]
+                place = out_ref.at[z ^ b, y ^ side, column]
                 copies.append(pltpu.make_async_copy(part.at[side, b], place, sem))
     for copy in copies:
         copy.start()
@@ -303,10 +301,8 @@
     copies = jax.ShapeDtypeStruct((shards, own_features, 7 * HD), bf16)
     pair = jax.ShapeDtypeStruct((2, own_features, width), bf16)
     copies, pair = call(pack, (copies, pair), 0, keep, got)
-    column = pair
-    for step in (1 << bit for bit in range(1, replicas.bit_length() - 1)):
-        pairs = [((i - step if i % 2 else i + step) % replicas, i) for i in range(replicas)]
-        column = jnp.concatenate([column, lax.ppermute(column, "rep", pairs)])
+    pairs = [pair] + [swapped(pair, "rep", bit) for bit in range(2, replicas, 2)]
+    column = jnp.concatenate(pairs)
     gathered = exchanged(copies, "fsdp").reshape(features, -1)
     both = jnp.stack([column, swapped(column, "fsdp", length)])
     up, down = [both], [both]

time: 145 us -> 142 us (0.979)
  starting transfers between devices: 78.8 us -> 76.2 us
    ppermute x2 -> x0, starting transfers between devices: 13.6 us -> none  [body(): column = jnp.concatenate([column, lax.ppermute(column, 'rep', pairs)])]
    ppermute x4 -> x7, waiting for transfers between devices: 20.9 us -> 33.6 us  [swapped(): return lax.ppermute(value, axis, pairs)]
    ppermute x4 -> x7, starting transfers between devices: 13.8 us -> 26.1 us  [swapped(): return lax.ppermute(value, axis, pairs)]
    ppermute x2 -> x0, waiting for transfers between devices: 11.3 us -> none  [body(): column = jnp.concatenate([column, lax.ppermute(column, 'rep', pairs)])]
  transfers between devices with their start and end apart: 16 -> 17, of which waited for: 11 -> 11; matrix products, arithmetic and copies ran while one was open for 1% -> 1% of each run, Pallas kernels for 2% -> 2%
where the time goes in v10:
time: 142 us
  starting transfers between devices  76.2 us (54%)
  waiting for transfers between devices  50.8 us (36%)
  Pallas kernels  12.6 us (9%)
    ppermute x7, waiting for transfers between devices, swapped(): return lax.ppermute(value, axis, pairs)  33.6 us
    all_to_all x3, starting transfers between devices, exchanged(): return lax.all_to_all(blocks, axis, split_axis=0, concat_axis=0, tiled=True)  26.8 us
    ppermute x7, starting transfers between devices, swapped(): return lax.ppermute(value, axis, pairs)  26.1 us
    ppermute x7, starting transfers between devices, passed(): return lax.ppermute(value, 'fsdp', pairs)  23.3 us
    ppermute x7, waiting for transfers between devices, passed(): return lax.ppermute(value, 'fsdp', pairs)  11.2 us
    all_to_all x3, waiting for transfers between devices, exchanged(): return lax.all_to_all(blocks, axis, split_axis=0, concat_axis=0, tiled=True)  5.97 us
    pallas_call x4, Pallas kernels, call(): pl.pallas_call(kernel, out_shape=outs if len(outs) > 1 else outs[0], in_s...  5.13 us
    pallas_call x1, Pallas kernels, projected(): pl.pallas_call(project, out_shape=jax.ShapeDtypeStruct((blocks, 7 * rows...  4.74 us
  transfers between devices with their start and end apart: 17, of which 11 were waited for; matrix products, arithmetic and copies ran while one was open for 1% of the time, Pallas kernels for 2%

profile of v10, /device:TPU:32, one launch (start us, length us, event | category | flops | bytes accessed | tf_op | source)
XLA Modules:
  0.0 141.6 jit_solution(11209870606550295741)
XLA Ops:
  0.6 0.0 copy-start.2
  0.6 1.1 shard_map.68
  1.8 5.2 %collective-permute-start.2 = (bf16[40,576]{1,0:T(8,128)(2,1)S(1)}, bf16[40,576]{1,0:T(8,128)(2,1)S(1)}, u32[]{:S(2)}, u32[]{:S(2)}) collective-permute-start(bf16[40,576]{1,0:T(8,128)(2,1)S(1)} %get-tuple-element.9), channel_id=1, source_target_pairs={{0,1},{1,0},{2,3},{3,2},{4,5},{5,4},{6,7},{7,6},{8,9},{9,8},{10,11... | collective-permute-start | bytes 138248 | tf_op jit(solution)/shard_map/ppermute | solution.py:288
  7.0 2.1 %collective-permute-done.2.got_ref = bf16[40,576]{1,0:T(8,128)(2,1)S(1)} collective-permute-done((bf16[40,576]{1,0:T(8,128)(2,1)S(1)}, bf16[40,576]{1,0:T(8,128)(2,1)S(1)}, u32[]{:S(2)}, u32[]{:S(2)}) %collective-permute-start.2) | collective-permute-done | bytes 46112 | tf_op jit(solution)/shard_map/ppermute | solution.py:288
  9.0 1.1 shard_map.69
  10.2 8.0 %all-to-all-start = ((bf16[16,40,896]{2,1,0:T(8,128)(2,1)}), bf16[16,40,896]{2,1,0:T(8,128)(2,1)S(1)}, u32[]{:S(2)}, u32[]{:S(2)}) async-start(bf16[16,40,896]{2,1,0:T(8,128)(2,1)} %get-tuple-element.10), calls=%async_computation | async-start | bytes 2293760 | tf_op jit(solution)/shard_map/all_to_all | solution.py:19
  18.2 0.0 copy-done.2
  18.2 0.1 constant_dynamic-slice_fusion.1
  18.2 3.9 %collective-permute-start = (bf16[512,640]{1,0:T(8,128)(2,1)S(1)}, bf16[512,640]{1,0:T(8,128)(2,1)S(1)}, u32[]{:S(2)}, u32[]{:S(2)}) collective-permute-start(bf16[512,640]{1,0:T(8,128)(2,1)S(1)} %constant_dynamic-slice_fusion.1), channel_id=1, source_target_pairs={{0,1},{1,0},{2,3},{3,2},{4,5},{5,4},{6,7},{7,6},{8,9},{9,8},{10,11... | collective-permute-start | bytes 1966088 | tf_op jit(solution)/shard_map/ppermute | solution.py:288
  22.2 13.3 %collective-permute-done.far_hbm = bf16[512,640]{1,0:T(8,128)(2,1)S(1)} collective-permute-done((bf16[512,640]{1,0:T(8,128)(2,1)S(1)}, bf16[512,640]{1,0:T(8,128)(2,1)S(1)}, u32[]{:S(2)}, u32[]{:S(2)}) %collective-permute-start) | collective-permute-done | bytes 655392 | tf_op jit(solution)/shard_map/ppermute | solution.py:288
  35.5 0.0 copy-start.3
  35.5 1.9 %collective-permute-start.1 = (bf16[512,640]{1,0:T(8,128)(2,1)S(1)}, bf16[512,640]{1,0:T(8,128)(2,1)S(1)}, u32[]{:S(2)}, u32[]{:S(2)}) collective-permute-start(bf16[512,640]{1,0:T(8,128)(2,1)S(1)} %collective-permute-done.far_hbm), channel_id=1, source_target_pairs={{0,8},{8,0},{16,24},{24,16},{32,40},{40,32},{48,56},{56,48},{1,9},... | collective-permute-start | bytes 1966088 | tf_op jit(solution)/shard_map/ppermute | solution.py:288
  37.4 2.1 %collective-permute-done.1.near_hbm = bf16[512,640]{1,0:T(8,128)(2,1)S(1)} collective-permute-done((bf16[512,640]{1,0:T(8,128)(2,1)S(1)}, bf16[512,640]{1,0:T(8,128)(2,1)S(1)}, u32[]{:S(2)}, u32[]{:S(2)}) %collective-permute-start.1) | collective-permute-done | bytes 655392 | tf_op jit(solution)/shard_map/ppermute | solution.py:288
  39.4 0.0 copy-start.4
  39.5 6.0 %all-to-all-done = bf16[16,40,896]{2,1,0:T(8,128)(2,1)S(1)} async-done(((bf16[16,40,896]{2,1,0:T(8,128)(2,1)}), bf16[16,40,896]{2,1,0:T(8,128)(2,1)S(1)}, u32[]{:S(2)}, u32[]{:S(2)}) %all-to-all-start) | async-done | bytes 1146912 | tf_op jit(solution)/shard_map/all_to_all | solution.py:19
  45.4 0.0 copy-done.3
  45.4 0.0 copy-done.4
  45.4 4.7 %shard_map.70 = bf16[8,448,128]{2,1,0:T(8,128)(2,1)} custom-call(s32[1]{0:T(128)} %bitcast.1.core_ref, bf16[1024,640]{1,0:T(8,128)(2,1)} %own_hbm.1, bf16[512,640]{1,0:T(8,128)(2,1)} %copy-done.3, bf16[512,640]{1,0:T(8,128)(2,1)} %copy-done.4, bf16[640,896]{1,0:T(8,128)(2,1)S(1)} %bitcast.15), custom_call_target="tpu_custom_call" | custom-call | flops 1342177280 | bytes 3768320 | tf_op jit(solution)/shard_map/pallas_call | solution.py:177
  50.2 0.0 copy-start
  50.2 0.0 copy-start.1
  50.2 15.3 %all-to-all-start.1 = ((bf16[8,448,128]{2,1,0:T(8,128)(2,1)}), bf16[8,448,128]{2,1,0:T(8,128)(2,1)S(1)}, u32[]{:S(2)}, u32[]{:S(2)}) async-start(bf16[8,448,128]{2,1,0:T(8,128)(2,1)} %shard_map.70), calls=%async_computation.1 | async-start | bytes 1835008 | tf_op jit(solution)/shard_map/all_to_all | solution.py:19
  65.6 0.0 copy-done
  65.6 0.2 convert_reduce_fusion
  65.8 0.3 fusion
  66.1 0.1 pad_maximum_fusion.1
  66.2 4.8 %collective-permute-start.3 = (bf16[2,40,128]{2,1,0:T(8,128)(2,1)S(1)}, bf16[2,40,128]{2,1,0:T(8,128)(2,1)S(1)}, u32[]{:S(2)}, u32[]{:S(2)}) collective-permute-start(bf16[2,40,128]{2,1,0:T(8,128)(2,1)S(1)} %get-tuple-element.13), channel_id=1, source_target_pairs={{0,2},{1,3},{2,0},{3,1},{4,6},{5,7},{6,4},{7,5},{8,10},{9,11},{10,... | collective-permute-start | bytes 61448 | tf_op jit(solution)/shard_map/ppermute | solution.py:288
  71.1 5.5 %collective-permute-start.4 = (bf16[2,40,128]{2,1,0:T(8,128)(2,1)S(1)}, bf16[2,40,128]{2,1,0:T(8,128)(2,1)S(1)}, u32[]{:S(2)}, u32[]{:S(2)}) collective-permute-start(bf16[2,40,128]{2,1,0:T(8,128)(2,1)S(1)} %get-tuple-element.13), channel_id=1, source_target_pairs={{0,4},{1,5},{2,6},{3,7},{4,0},{5,1},{6,2},{7,3},{8,12},{9,13},{10,... | collective-permute-start | bytes 61448 | tf_op jit(solution)/shard_map/ppermute | solution.py:288
  76.6 1.9 %collective-permute-start.5 = (bf16[2,40,128]{2,1,0:T(8,128)(2,1)S(1)}, bf16[2,40,128]{2,1,0:T(8,128)(2,1)S(1)}, u32[]{:S(2)}, u32[]{:S(2)}) collective-permute-start(bf16[2,40,128]{2,1,0:T(8,128)(2,1)S(1)} %get-tuple-element.13), channel_id=1, source_target_pairs={{0,6},{1,7},{2,4},{3,5},{4,2},{5,3},{6,0},{7,1},{8,14},{9,15},{10,... | collective-permute-start | bytes 61448 | tf_op jit(solution)/shard_map/ppermute | solution.py:288
  78.5 5.9 %collective-permute-done.3 = bf16[2,40,128]{2,1,0:T(8,128)(2,1)S(1)} collective-permute-done((bf16[2,40,128]{2,1,0:T(8,128)(2,1)S(1)}, bf16[2,40,128]{2,1,0:T(8,128)(2,1)S(1)}, u32[]{:S(2)}, u32[]{:S(2)}) %collective-permute-start.3) | collective-permute-done | bytes 20512 | tf_op jit(solution)/shard_map/ppermute | solution.py:288
  84.4 6.8 %collective-permute-done.4 = bf16[2,40,128]{2,1,0:T(8,128)(2,1)S(1)} collective-permute-done((bf16[2,40,128]{2,1,0:T(8,128)(2,1)S(1)}, bf16[2,40,128]{2,1,0:T(8,128)(2,1)S(1)}, u32[]{:S(2)}, u32[]{:S(2)}) %collective-permute-start.4) | collective-permute-done | bytes 20512 | tf_op jit(solution)/shard_map/ppermute | solution.py:288
  91.2 0.0 all-to-all-done.1.part_ref
  91.2 0.0 copy-done.1
  91.2 0.9 shard_map.72
  92.1 3.5 %all-to-all-start.2 = ((bf16[8,256,128]{2,1,0:T(8,128)(2,1)}), bf16[8,256,128]{2,1,0:T(8,128)(2,1)S(1)}, u32[]{:S(2)}, u32[]{:S(2)}) async-start(bf16[8,256,128]{2,1,0:T(8,128)(2,1)} %shard_map.72), calls=%async_computation.2 | async-start | bytes 1048576 | tf_op jit(solution)/shard_map/all_to_all | solution.py:19
  95.6 0.0 collective-permute-done.5
  95.7 2.8 %collective-permute-start.6 = (bf16[8,40,128]{2,1,0:T(8,128)(2,1)S(1)}, bf16[8,40,128]{2,1,0:T(8,128)(2,1)S(1)}, u32[]{:S(2)}, u32[]{:S(2)}) collective-permute-start(bf16[8,40,128]{2,1,0:T(8,128)(2,1)S(1)} %constant_dynamic-update-slice_fusion), channel_id=1, source_target_pairs={{0,512},{64,576},{128,640},{192,704},{256,768},{320,832},{384,896}... | collective-permute-start | bytes 245768 | tf_op jit(solution)/shard_map/ppermute | solution.py:288
  98.5 3.5 %collective-permute-done.6 = bf16[8,40,128]{2,1,0:T(8,128)(2,1)S(1)} collective-permute-done((bf16[8,40,128]{2,1,0:T(8,128)(2,1)S(1)}, bf16[8,40,128]{2,1,0:T(8,128)(2,1)S(1)}, u32[]{:S(2)}, u32[]{:S(2)}) %collective-permute-start.6) | collective-permute-done | bytes 81952 | tf_op jit(solution)/shard_map/ppermute | solution.py:288
  102.0 2.4 %collective-permute-start.7 = (bf16[2,8,40,128]{3,2,1,0:T(8,128)(2,1)S(1)}, bf16[2,8,40,128]{3,2,1,0:T(8,128)(2,1)S(1)}, u32[]{:S(2)}, u32[]{:S(2)}) collective-permute-start(bf16[2,8,40,128]{3,2,1,0:T(8,128)(2,1)S(1)} %pad_maximum_fusion.refs_0_), channel_id=1, source_target_pairs={{0,64},{64,128},{128,192},{192,256},{256,320},{320,384},{384,448},... | collective-permute-start | bytes 491528 | tf_op jit(solution)/shard_map/ppermute | solution.py:292
  104.4 4.7 %collective-permute-start.11 = (bf16[2,8,40,128]{3,2,1,0:T(8,128)(2,1)S(1)}, bf16[2,8,40,128]{3,2,1,0:T(8,128)(2,1)S(1)}, u32[]{:S(2)}, u32[]{:S(2)}) collective-permute-start(bf16[2,8,40,128]{3,2,1,0:T(8,128)(2,1)S(1)} %pad_maximum_fusion.refs_0_), channel_id=1, source_target_pairs={{0,448},{64,0},{128,64},{192,128},{256,192},{320,256},{384,320},{4... | collective-permute-start | bytes 491528 | tf_op jit(solution)/shard_map/ppermute | solution.py:292
  109.1 1.4 collective-permute-done.7.refs_1_
  110.4 1.9 %collective-permute-start.8 = (bf16[2,8,40,128]{3,2,1,0:T(8,128)(2,1)S(1)}, bf16[2,8,40,128]{3,2,1,0:T(8,128)(2,1)S(1)}, u32[]{:S(2)}, u32[]{:S(2)}) collective-permute-start(bf16[2,8,40,128]{3,2,1,0:T(8,128)(2,1)S(1)} %collective-permute-done.7.refs_1_), channel_id=1, source_target_pairs={{0,64},{64,128},{128,192},{192,256},{256,320},{320,384},{384,448},... | collective-permute-start | bytes 491528 | tf_op jit(solution)/shard_map/ppermute | solution.py:292
  112.4 0.0 collective-permute-done.11.refs_7_
  112.4 5.1 %collective-permute-start.12 = (bf16[2,8,40,128]{3,2,1,0:T(8,128)(2,1)S(1)}, bf16[2,8,40,128]{3,2,1,0:T(8,128)(2,1)S(1)}, u32[]{:S(2)}, u32[]{:S(2)}) collective-permute-start(bf16[2,8,40,128]{3,2,1,0:T(8,128)(2,1)S(1)} %collective-permute-done.11.refs_7_), channel_id=1, source_target_pairs={{0,448},{64,0},{128,64},{192,128},{256,192},{320,256},{384,320},{4... | collective-permute-start | bytes 491528 | tf_op jit(solution)/shard_map/ppermute | solution.py:292
  117.5 1.3 collective-permute-done.8.refs_2_
  118.9 1.9 %collective-permute-start.9 = (bf16[2,8,40,128]{3,2,1,0:T(8,128)(2,1)S(1)}, bf16[2,8,40,128]{3,2,1,0:T(8,128)(2,1)S(1)}, u32[]{:S(2)}, u32[]{:S(2)}) collective-permute-start(bf16[2,8,40,128]{3,2,1,0:T(8,128)(2,1)S(1)} %collective-permute-done.8.refs_2_), channel_id=1, source_target_pairs={{0,64},{64,128},{128,192},{192,256},{256,320},{320,384},{384,448},... | collective-permute-start | bytes 491528 | tf_op jit(solution)/shard_map/ppermute | solution.py:292
  120.8 0.0 collective-permute-done.12.refs_6_
  120.8 5.4 %collective-permute-start.13 = (bf16[2,8,40,128]{3,2,1,0:T(8,128)(2,1)S(1)}, bf16[2,8,40,128]{3,2,1,0:T(8,128)(2,1)S(1)}, u32[]{:S(2)}, u32[]{:S(2)}) collective-permute-start(bf16[2,8,40,128]{3,2,1,0:T(8,128)(2,1)S(1)} %collective-permute-done.12.refs_6_), channel_id=1, source_target_pairs={{0,448},{64,0},{128,64},{192,128},{256,192},{320,256},{384,320},{4... | collective-permute-start | bytes 491528 | tf_op jit(solution)/shard_map/ppermute | solution.py:292
  126.2 2.2 %collective-permute-done.9.refs_3_ = bf16[2,8,40,128]{3,2,1,0:T(8,128)(2,1)S(1)} collective-permute-done((bf16[2,8,40,128]{3,2,1,0:T(8,128)(2,1)S(1)}, bf16[2,8,40,128]{3,2,1,0:T(8,128)(2,1)S(1)}, u32[]{:S(2)}, u32[]{:S(2)}) %collective-permute-start.9) | collective-permute-done | bytes 163872 | tf_op jit(solution)/shard_map/ppermute | solution.py:292
  128.4 1.9 %collective-permute-start.10 = (bf16[2,8,40,128]{3,2,1,0:T(8,128)(2,1)S(1)}, bf16[2,8,40,128]{3,2,1,0:T(8,128)(2,1)S(1)}, u32[]{:S(2)}, u32[]{:S(2)}) collective-permute-start(bf16[2,8,40,128]{3,2,1,0:T(8,128)(2,1)S(1)} %collective-permute-done.9.refs_3_), channel_id=1, source_target_pairs={{0,64},{64,128},{128,192},{192,256},{256,320},{320,384},{384,448},... | collective-permute-start | bytes 491528 | tf_op jit(solution)/shard_map/ppermute | solution.py:292
  130.3 0.1 copy.8.mine_ref
  130.5 0.1 pad_add_fusion.place_ref
  130.6 0.0 collective-permute-done.13.refs_5_
  130.6 6.3 %collective-permute-done.10.refs_4_ = bf16[2,8,40,128]{3,2,1,0:T(8,128)(2,1)S(1)} collective-permute-done((bf16[2,8,40,128]{3,2,1,0:T(8,128)(2,1)S(1)}, bf16[2,8,40,128]{3,2,1,0:T(8,128)(2,1)S(1)}, u32[]{:S(2)}, u32[]{:S(2)}) %collective-permute-start.10) | collective-permute-done | bytes 163872 | tf_op jit(solution)/shard_map/ppermute | solution.py:292
  136.8 1.6 %shard_map.74 = bf16[8,2,8,40,128]{4,3,2,1,0:T(8,128)(2,1)} custom-call(s32[3]{0:T(128)S(1)} %pad_add_fusion.place_ref, bf16[2,8,40,128]{3,2,1,0:T(8,128)(2,1)S(1)} %pad_maximum_fusion.refs_0_, bf16[2,8,40,128]{3,2,1,0:T(8,128)(2,1)S(1)} %collective-permute-done.7.refs_1_, bf16[2,8,40,128]{3,2,1,0:T(8,128)(2,1)S(1)} %collective-permute-done.8.refs_2_, ...), custom_call_target="tpu_custom_call" | custom-call | bytes 2621440 | tf_op jit(solution)/shard_map/pallas_call | solution.py:120
  138.5 0.3 shard_map.71
  138.7 0.0 all-to-all-done.2.kv_ref
  138.7 2.8 %shard_map.73 = bf16[128,640]{1,0:T(8,128)(2,1)} custom-call(s32[1]{0:T(128)} %bitcast.rank_ref, bf16[5,128,128]{2,1,0:T(8,128)(2,1)S(1)} %get-tuple-element.11.q_ref, f32[128,640]{1,0:T(8,128)S(1)} %get-tuple-element.12.mask_ref, bf16[8,256,128]{2,1,0:T(8,128)(2,1)S(1)} %all-to-all-done.2.kv_ref), custom_call_target="tpu_custom_call" | custom-call | flops 209715200 | bytes 1179652 | tf_op jit(solution)/shard_map/pallas_call | solution.py:34
  (8 shorter events, 0.1 us)
Async XLA Ops:
  0.6 17.5 %copy-start.2 = (bf16[1024,640]{1,0:T(8,128)(2,1)S(1)}, bf16[1024,640]{1,0:T(8,128)(2,1)}, u32[]{:S(2)}) copy-start(bf16[1024,640]{1,0:T(8,128)(2,1)} %own_hbm.1) | copy-start | bytes 3932164
  1.8 7.3 %collective-permute-start.2 = (bf16[40,576]{1,0:T(8,128)(2,1)S(1)}, bf16[40,576]{1,0:T(8,128)(2,1)S(1)}, u32[]{:S(2)}, u32[]{:S(2)}) collective-permute-start(bf16[40,576]{1,0:T(8,128)(2,1)S(1)} %get-tuple-element.9), channel_id=1, source_target_pairs={{0,1},{1,0},{2,3},{3,2},{4,5},{5,4},{6,7},{7,6},{8,9},{9,8},{10,11... | collective-permute-start | bytes 138248 | tf_op jit(solution)/shard_map/ppermute | solution.py:288
  10.2 35.3 %all-to-all-start = ((bf16[16,40,896]{2,1,0:T(8,128)(2,1)}), bf16[16,40,896]{2,1,0:T(8,128)(2,1)S(1)}, u32[]{:S(2)}, u32[]{:S(2)}) async-start(bf16[16,40,896]{2,1,0:T(8,128)(2,1)} %get-tuple-element.10), calls=%async_computation | async-start | bytes 2293760 | tf_op jit(solution)/shard_map/all_to_all | solution.py:19
  18.2 17.2 %collective-permute-start = (bf16[512,640]{1,0:T(8,128)(2,1)S(1)}, bf16[512,640]{1,0:T(8,128)(2,1)S(1)}, u32[]{:S(2)}, u32[]{:S(2)}) collective-permute-start(bf16[512,640]{1,0:T(8,128)(2,1)S(1)} %constant_dynamic-slice_fusion.1), channel_id=1, source_target_pairs={{0,1},{1,0},{2,3},{3,2},{4,5},{5,4},{6,7},{7,6},{8,9},{9,8},{10,11... | collective-permute-start | bytes 1966088 | tf_op jit(solution)/shard_map/ppermute | solution.py:288
  35.5 10.0 %copy-start.3 = (bf16[512,640]{1,0:T(8,128)(2,1)}, bf16[512,640]{1,0:T(8,128)(2,1)S(1)}, u32[]{:S(2)}) copy-start(bf16[512,640]{1,0:T(8,128)(2,1)S(1)} %collective-permute-done.far_hbm) | copy-start | bytes 1966084
  35.5 4.0 %collective-permute-start.1 = (bf16[512,640]{1,0:T(8,128)(2,1)S(1)}, bf16[512,640]{1,0:T(8,128)(2,1)S(1)}, u32[]{:S(2)}, u32[]{:S(2)}) collective-permute-start(bf16[512,640]{1,0:T(8,128)(2,1)S(1)} %collective-permute-done.far_hbm), channel_id=1, source_target_pairs={{0,8},{8,0},{16,24},{24,16},{32,40},{40,32},{48,56},{56,48},{1,9},... | collective-permute-start | bytes 1966088 | tf_op jit(solution)/shard_map/ppermute | solution.py:288
  39.4 6.0 %copy-start.4 = (bf16[512,640]{1,0:T(8,128)(2,1)}, bf16[512,640]{1,0:T(8,128)(2,1)S(1)}, u32[]{:S(2)}) copy-start(bf16[512,640]{1,0:T(8,128)(2,1)S(1)} %collective-permute-done.1.near_hbm) | copy-start | bytes 1966084
  50.2 15.4 %copy-start = (s32[1,1024]{1,0:T(1,128)S(1)}, s32[1,1024]{1,0:T(1,128)}, u32[]{:S(2)}) copy-start(s32[1,1024]{1,0:T(1,128)} %param.8) | copy-start | bytes 12292
  50.2 41.0 %copy-start.1 = (f32[896]{0:T(1024)S(1)}, f32[896]{0:T(1024)}, u32[]{:S(2)}) copy-start(f32[896]{0:T(1024)} %param.7) | copy-start | bytes 10756
  50.2 41.0 %all-to-all-start.1 = ((bf16[8,448,128]{2,1,0:T(8,128)(2,1)}), bf16[8,448,128]{2,1,0:T(8,128)(2,1)S(1)}, u32[]{:S(2)}, u32[]{:S(2)}) async-start(bf16[8,448,128]{2,1,0:T(8,128)(2,1)} %shard_map.70), calls=%async_computation.1 | async-start | bytes 1835008 | tf_op jit(solution)/shard_map/all_to_all | solution.py:19
  66.2 18.2 %collective-permute-start.3 = (bf16[2,40,128]{2,1,0:T(8,128)(2,1)S(1)}, bf16[2,40,128]{2,1,0:T(8,128)(2,1)S(1)}, u32[]{:S(2)}, u32[]{:S(2)}) collective-permute-start(bf16[2,40,128]{2,1,0:T(8,128)(2,1)S(1)} %get-tuple-element.13), channel_id=1, source_target_pairs={{0,2},{1,3},{2,0},{3,1},{4,6},{5,7},{6,4},{7,5},{8,10},{9,11},{10,... | collective-permute-start | bytes 61448 | tf_op jit(solution)/shard_map/ppermute | solution.py:288
  71.1 20.1 %collective-permute-start.4 = (bf16[2,40,128]{2,1,0:T(8,128)(2,1)S(1)}, bf16[2,40,128]{2,1,0:T(8,128)(2,1)S(1)}, u32[]{:S(2)}, u32[]{:S(2)}) collective-permute-start(bf16[2,40,128]{2,1,0:T(8,128)(2,1)S(1)} %get-tuple-element.13), channel_id=1, source_target_pairs={{0,4},{1,5},{2,6},{3,7},{4,0},{5,1},{6,2},{7,3},{8,12},{9,13},{10,... | collective-permute-start | bytes 61448 | tf_op jit(solution)/shard_map/ppermute | solution.py:288
  76.6 19.1 %collective-permute-start.5 = (bf16[2,40,128]{2,1,0:T(8,128)(2,1)S(1)}, bf16[2,40,128]{2,1,0:T(8,128)(2,1)S(1)}, u32[]{:S(2)}, u32[]{:S(2)}) collective-permute-start(bf16[2,40,128]{2,1,0:T(8,128)(2,1)S(1)} %get-tuple-element.13), channel_id=1, source_target_pairs={{0,6},{1,7},{2,4},{3,5},{4,2},{5,3},{6,0},{7,1},{8,14},{9,15},{10,... | collective-permute-start | bytes 61448 | tf_op jit(solution)/shard_map/ppermute | solution.py:288
  92.1 46.6 %all-to-all-start.2 = ((bf16[8,256,128]{2,1,0:T(8,128)(2,1)}), bf16[8,256,128]{2,1,0:T(8,128)(2,1)S(1)}, u32[]{:S(2)}, u32[]{:S(2)}) async-start(bf16[8,256,128]{2,1,0:T(8,128)(2,1)} %shard_map.72), calls=%async_computation.2 | async-start | bytes 1048576 | tf_op jit(solution)/shard_map/all_to_all | solution.py:19
  95.7 6.3 %collective-permute-start.6 = (bf16[8,40,128]{2,1,0:T(8,128)(2,1)S(1)}, bf16[8,40,128]{2,1,0:T(8,128)(2,1)S(1)}, u32[]{:S(2)}, u32[]{:S(2)}) collective-permute-start(bf16[8,40,128]{2,1,0:T(8,128)(2,1)S(1)} %constant_dynamic-update-slice_fusion), channel_id=1, source_target_pairs={{0,512},{64,576},{128,640},{192,704},{256,768},{320,832},{384,896}... | collective-permute-start | bytes 245768 | tf_op jit(solution)/shard_map/ppermute | solution.py:288
  102.0 8.4 %collective-permute-start.7 = (bf16[2,8,40,128]{3,2,1,0:T(8,128)(2,1)S(1)}, bf16[2,8,40,128]{3,2,1,0:T(8,128)(2,1)S(1)}, u32[]{:S(2)}, u32[]{:S(2)}) collective-permute-start(bf16[2,8,40,128]{3,2,1,0:T(8,128)(2,1)S(1)} %pad_maximum_fusion.refs_0_), channel_id=1, source_target_pairs={{0,64},{64,128},{128,192},{192,256},{256,320},{320,384},{384,448},... | collective-permute-start | bytes 491528 | tf_op jit(solution)/shard_map/ppermute | solution.py:292
  104.4 7.9 %collective-permute-start.11 = (bf16[2,8,40,128]{3,2,1,0:T(8,128)(2,1)S(1)}, bf16[2,8,40,128]{3,2,1,0:T(8,128)(2,1)S(1)}, u32[]{:S(2)}, u32[]{:S(2)}) collective-permute-start(bf16[2,8,40,128]{3,2,1,0:T(8,128)(2,1)S(1)} %pad_maximum_fusion.refs_0_), channel_id=1, source_target_pairs={{0,448},{64,0},{128,64},{192,128},{256,192},{320,256},{384,320},{4... | collective-permute-start | bytes 491528 | tf_op jit(solution)/shard_map/ppermute | solution.py:292
  110.4 8.4 %collective-permute-start.8 = (bf16[2,8,40,128]{3,2,1,0:T(8,128)(2,1)S(1)}, bf16[2,8,40,128]{3,2,1,0:T(8,128)(2,1)S(1)}, u32[]{:S(2)}, u32[]{:S(2)}) collective-permute-start(bf16[2,8,40,128]{3,2,1,0:T(8,128)(2,1)S(1)} %collective-permute-done.7.refs_1_), channel_id=1, source_target_pairs={{0,64},{64,128},{128,192},{192,256},{256,320},{320,384},{384,448},... | collective-permute-start | bytes 491528 | tf_op jit(solution)/shard_map/ppermute | solution.py:292
  112.4 8.4 %collective-permute-start.12 = (bf16[2,8,40,128]{3,2,1,0:T(8,128)(2,1)S(1)}, bf16[2,8,40,128]{3,2,1,0:T(8,128)(2,1)S(1)}, u32[]{:S(2)}, u32[]{:S(2)}) collective-permute-start(bf16[2,8,40,128]{3,2,1,0:T(8,128)(2,1)S(1)} %collective-permute-done.11.refs_7_), channel_id=1, source_target_pairs={{0,448},{64,0},{128,64},{192,128},{256,192},{320,256},{384,320},{4... | collective-permute-start | bytes 491528 | tf_op jit(solution)/shard_map/ppermute | solution.py:292
  118.9 9.6 %collective-permute-start.9 = (bf16[2,8,40,128]{3,2,1,0:T(8,128)(2,1)S(1)}, bf16[2,8,40,128]{3,2,1,0:T(8,128)(2,1)S(1)}, u32[]{:S(2)}, u32[]{:S(2)}) collective-permute-start(bf16[2,8,40,128]{3,2,1,0:T(8,128)(2,1)S(1)} %collective-permute-done.8.refs_2_), channel_id=1, source_target_pairs={{0,64},{64,128},{128,192},{192,256},{256,320},{320,384},{384,448},... | collective-permute-start | bytes 491528 | tf_op jit(solution)/shard_map/ppermute | solution.py:292
  120.8 9.8 %collective-permute-start.13 = (bf16[2,8,40,128]{3,2,1,0:T(8,128)(2,1)S(1)}, bf16[2,8,40,128]{3,2,1,0:T(8,128)(2,1)S(1)}, u32[]{:S(2)}, u32[]{:S(2)}) collective-permute-start(bf16[2,8,40,128]{3,2,1,0:T(8,128)(2,1)S(1)} %collective-permute-done.12.refs_6_), channel_id=1, source_target_pairs={{0,448},{64,0},{128,64},{192,128},{256,192},{320,256},{384,320},{4... | collective-permute-start | bytes 491528 | tf_op jit(solution)/shard_map/ppermute | solution.py:292
  128.4 8.4 %collective-permute-start.10 = (bf16[2,8,40,128]{3,2,1,0:T(8,128)(2,1)S(1)}, bf16[2,8,40,128]{3,2,1,0:T(8,128)(2,1)S(1)}, u32[]{:S(2)}, u32[]{:S(2)}) collective-permute-start(bf16[2,8,40,128]{3,2,1,0:T(8,128)(2,1)S(1)} %collective-permute-done.9.refs_3_), channel_id=1, source_target_pairs={{0,64},{64,128},{128,192},{192,256},{256,320},{320,384},{384,448},... | collective-permute-start | bytes 491528 | tf_op jit(solution)/shard_map/ppermute | solution.py:292
